TPU v7x, 32 devices: a whole 2x2x4 slice. The times are simulated.
32 devices in a mesh: rep: 2 (over x), frame: 4 (over z), tensor: 4 (over y, core).
Axes of the slice: x: 2, y: 2, z: 4, core: 2. Of those that a mesh axis runs over, the one named last changes fastest.
Arguments:
- tokens: bfloat16 [4, 16, 196, 768], P('rep', 'frame', 'tensor'), may hold values from -6 to 6
- query_space: bfloat16 [768, 768], P('frame', 'tensor'), may hold values from -0.3125 to 0.3125
- key_space: bfloat16 [768, 768], P('frame', 'tensor'), may hold values from -0.3125 to 0.3125
- value_space: bfloat16 [768, 768], P('frame', 'tensor'), may hold values from -0.21875 to 0.21875
- output_space: bfloat16 [768, 768], P('tensor', 'frame'), may hold values from -0.625 to 0.625
- query_time: bfloat16 [768, 768], P('frame', 'tensor'), may hold values from -0.3125 to 0.3125
- key_time: bfloat16 [768, 768], P('frame', 'tensor'), may hold values from -0.3125 to 0.3125
- value_time: bfloat16 [768, 768], P('frame', 'tensor'), may hold values from -0.21875 to 0.21875
- output_time: bfloat16 [768, 768], P('tensor', 'frame'), may hold values from -0.4375 to 0.4375
- mlp_in: bfloat16 [768, 3072], P('frame', 'tensor'), may hold values from -0.21875 to 0.21875
- bias_in: bfloat16 [3072], P('tensor'), may hold values from -3 to 3
- mlp_out: bfloat16 [3072, 768], P('tensor', 'frame'), may hold values from -0.109375 to 0.109375
- bias_out: bfloat16 [768], P('frame'), may hold values from -2 to 2
- gain_first: float32 [768], P(('frame', 'tensor')), may hold values from 0.5 to 1.5
- shift_first: float32 [768], P(('frame', 'tensor')), may hold values from -2 to 2
- gain_second: float32 [768], P(('frame', 'tensor')), may hold values from 0.5 to 1.5
- shift_second: float32 [768], P(('frame', 'tensor')), may hold values from -2 to 2
- gain_third: float32 [768], P(('frame', 'tensor')), may hold values from 0.5 to 1.5
- shift_third: float32 [768], P(('frame', 'tensor')), may hold values from -2 to 2
- place_slot: int32 [196], replicated, may hold values from -1 to 255, as said below
- cotangent: bfloat16 [4, 16, 196, 768], P('rep', 'frame', 'tensor'), may hold values from -6 to 6
Outputs:
- result: bfloat16 [4, 16, 196, 768], P('rep', 'frame', 'tensor')
- grad_tokens: float32 [4, 16, 196, 768], P('rep', 'frame', 'tensor')
- grad_query_space: float32 [768, 768], P('frame', 'tensor')
- grad_key_space: float32 [768, 768], P('frame', 'tensor')
- grad_value_space: float32 [768, 768], P('frame', 'tensor')
- grad_output_space: float32 [768, 768], P('tensor', 'frame')
- grad_query_time: float32 [768, 768], P('frame', 'tensor')
- grad_key_time: float32 [768, 768], P('frame', 'tensor')
- grad_value_time: float32 [768, 768], P('frame', 'tensor')
- grad_output_time: float32 [768, 768], P('tensor', 'frame')
- grad_mlp_in: float32 [768, 3072], P('frame', 'tensor')
- grad_bias_in: float32 [3072], P('tensor')
- grad_mlp_out: float32 [3072, 768], P('tensor', 'frame')
- grad_bias_out: float32 [768], P('frame')
- grad_gain_first: float32 [768], P(('frame', 'tensor'))
- grad_shift_first: float32 [768], P(('frame', 'tensor'))
- grad_gain_second: float32 [768], P(('frame', 'tensor'))
- grad_shift_second: float32 [768], P(('frame', 'tensor'))
- grad_gain_third: float32 [768], P(('frame', 'tensor'))
- grad_shift_third: float32 [768], P(('frame', 'tensor'))
Inputs may be any that keep to these rules, and one draw needn't show every extreme that they name: `place_slot`: each unmasked place has a slot of its own; a slot s is taken by frame index s // 64; exactly 64 places have slots of one frame index; at least 64 places are unmasked; slot 255 is always taken; a masked place is masked in every frame of every clip.
All inputs are finite; a program needn't handle non-finite values.
Results may differ from a plain program's by a relative error of at most 0.023.
Values may be sent and summed in bfloat16 or wider, within the bound.
A program may use at most 192 MiB of HBM per device.

v0:
```python
from functools import partial

import jax
import jax.numpy as jnp
from jax import lax
from jax.sharding import PartitionSpec as P

HEAD_DIM = 64
CAP = 64


SPACE_FORMS = ("blhe,bmhe->bhlm", "bhlm,bmhe->blhe", "bhlm,blhe->bmhe")
TIME_FORMS = ("clshe,cmshe->cshlm", "cshlm,cmshe->clshe", "cshlm,clshe->cmshe")


def norm_rows(values, gain_vec, shift_vec):
    centre = jnp.mean(values, axis=-1, keepdims=True)
    offset = values - centre
    spread = jnp.mean(offset * offset, axis=-1, keepdims=True)
    return offset * lax.rsqrt(spread + 1e-06) * gain_vec + shift_vec


def gather_rows(values):
    return lax.all_gather(values, "tensor", axis=2, tiled=True)


def reduce_rows(values):
    return lax.psum_scatter(values, "tensor", scatter_dimension=2, tiled=True)


def to_places(values):
    return lax.all_to_all(values, "frame", split_axis=2, concat_axis=1, tiled=True)


def to_frames(values):
    return lax.all_to_all(values, "frame", split_axis=1, concat_axis=2, tiled=True)


def fetch_attention(query_w, key_w, value_w, output_w):
    return (
        lax.all_gather(query_w, "frame", axis=0, tiled=True),
        lax.all_gather(key_w, "frame", axis=0, tiled=True),
        lax.all_gather(value_w, "frame", axis=0, tiled=True),
        lax.all_gather(output_w, "frame", axis=1, tiled=True),
    )


def fetch_mlp(weight_in, weight_out, bias_vec_out, bias_vec_in):
    fetched = (
        lax.all_gather(weight_in, "frame", axis=0, tiled=True),
        lax.all_gather(weight_out, "frame", axis=1, tiled=True),
        lax.all_gather(bias_vec_out, "frame", axis=0, tiled=True),
    )
    return (fetched[0], fetched[1], fetched[2], bias_vec_in)


def attend(queries, keys_in, values_in, key_bias, scaling, forms):
    score_form, mix_form, back_form = forms
    scores = (
        jnp.einsum(score_form, queries, keys_in, preferred_element_type=jnp.float32) * scaling
        + key_bias
    )
    attn_probs = jax.nn.softmax(scores, axis=-1)
    attended = jnp.einsum(
        mix_form, attn_probs.astype(jnp.bfloat16), values_in, preferred_element_type=jnp.float32
    )
    return (attended.astype(jnp.bfloat16), attn_probs)


def attend_back(grad_out, queries, keys_in, values_in, attn_probs, scaling, forms):
    score_form, mix_form, back_form = forms
    grad_probs = jnp.einsum(score_form, grad_out, values_in, preferred_element_type=jnp.float32)
    grad_values = jnp.einsum(
        back_form, attn_probs.astype(jnp.bfloat16), grad_out, preferred_element_type=jnp.float32
    )
    inner = jnp.sum(grad_probs * attn_probs, axis=-1, keepdims=True)
    grad_scores = (attn_probs * (grad_probs - inner)).astype(jnp.bfloat16)
    grad_queries = (
        jnp.einsum(mix_form, grad_scores, keys_in, preferred_element_type=jnp.float32) * scaling
    )
    grad_keys = (
        jnp.einsum(back_form, grad_scores, queries, preferred_element_type=jnp.float32) * scaling
    )
    return (
        grad_queries.astype(jnp.bfloat16),
        grad_keys.astype(jnp.bfloat16),
        grad_values.astype(jnp.bfloat16),
    )


def project_rows(residual, gain_vec, shift_vec, weights):
    query_w, key_w, value_w, output_w = weights
    normed = norm_rows(residual, gain_vec, shift_vec).astype(jnp.bfloat16)
    normed_all = gather_rows(normed)
    joined = jnp.concatenate((query_w, key_w, value_w), axis=1)
    projected = jnp.einsum("cfpd,dk->cfpk", normed_all, joined, preferred_element_type=jnp.float32)
    return (normed_all, projected.astype(jnp.bfloat16))


def space_forward(residual, gain_vec, shift_vec, weights, key_bias, scaling):
    output_w = weights[3]
    normed_all, projected = project_rows(residual, gain_vec, shift_vec, weights)
    clip_count, frames_dev, place_count = (
        projected.shape[0],
        projected.shape[1],
        projected.shape[2],
    )
    heads_dev = weights[0].shape[1] // HEAD_DIM
    heads_split = projected.reshape(clip_count * frames_dev, place_count, 3, heads_dev, HEAD_DIM)
    attended, attn_probs = attend(
        heads_split[:, :, 0],
        heads_split[:, :, 1],
        heads_split[:, :, 2],
        key_bias,
        scaling,
        SPACE_FORMS,
    )
    attended_rows = attended.reshape(clip_count, frames_dev, place_count, heads_dev * HEAD_DIM)
    branch = reduce_rows(
        jnp.einsum("cfpk,kd->cfpd", attended_rows, output_w, preferred_element_type=jnp.float32)
    )
    return (residual + branch, (normed_all, heads_split, attn_probs, attended_rows))


def time_forward(residual, gain_vec, shift_vec, weights, selector, scaling):
    output_w = weights[3]
    normed_all, projected = project_rows(residual, gain_vec, shift_vec, weights)
    packed = jnp.einsum(
        "sp,cfpk->cfsk", selector, projected, preferred_element_type=jnp.float32
    ).astype(jnp.bfloat16)
    by_place = to_places(packed)
    clip_count, frame_total, capacity = (by_place.shape[0], by_place.shape[1], by_place.shape[2])
    heads_dev = weights[0].shape[1] // HEAD_DIM
    heads_split = by_place.reshape(clip_count, frame_total, capacity, 3, heads_dev, HEAD_DIM)
    attended, attn_probs = attend(
        heads_split[:, :, :, 0],
        heads_split[:, :, :, 1],
        heads_split[:, :, :, 2],
        0.0,
        scaling,
        TIME_FORMS,
    )
    by_frame = to_frames(attended.reshape(clip_count, frame_total, capacity, heads_dev * HEAD_DIM))
    attended_rows = jnp.einsum(
        "sp,cfsk->cfpk", selector, by_frame, preferred_element_type=jnp.float32
    ).astype(jnp.bfloat16)
    branch = reduce_rows(
        jnp.einsum("cfpk,kd->cfpd", attended_rows, output_w, preferred_element_type=jnp.float32)
    )
    return (residual + branch, (normed_all, heads_split, attn_probs, attended_rows))


def mlp_forward(residual, gain_vec, shift_vec, weights):
    weight_in, weight_out, bias_vec_out, bias_vec_in = weights
    normed = norm_rows(residual, gain_vec, shift_vec).astype(jnp.bfloat16)
    normed_all = gather_rows(normed)
    before = jnp.einsum("cfpd,dk->cfpk", normed_all, weight_in, preferred_element_type=jnp.float32)
    before = before + bias_vec_in.astype(jnp.float32)
    hidden = jax.nn.gelu(before, approximate=True).astype(jnp.bfloat16)
    partial_out = jnp.einsum(
        "cfpk,kd->cfpd", hidden, weight_out, preferred_element_type=jnp.float32
    )
    branch = reduce_rows(partial_out) + bias_vec_out.astype(jnp.float32)
    return (residual + branch, (normed_all, before, hidden))


def attention_head(grad_resid, attended_rows, output_w):
    grad_all = gather_rows(grad_resid.astype(jnp.bfloat16))
    grad_mixed = jnp.einsum("cfpd,kd->cfpk", grad_all, output_w, preferred_element_type=jnp.float32)
    grad_output = jnp.einsum(
        "cfpk,cfpd->kd", attended_rows, grad_all, preferred_element_type=jnp.float32
    )
    return (grad_mixed.astype(jnp.bfloat16), grad_output)


def attention_tail(
    grad_resid, grad_proj, normed_all, residual, gain_vec, shift_vec, weights, grad_output
):
    query_w, key_w, value_w, output_w = weights
    joined = jnp.concatenate((query_w, key_w, value_w), axis=1)
    grad_joined = jnp.einsum(
        "cfpd,cfpk->dk", normed_all, grad_proj, preferred_element_type=jnp.float32
    )
    grad_normed = reduce_rows(
        jnp.einsum("cfpk,dk->cfpd", grad_proj, joined, preferred_element_type=jnp.float32)
    )
    _, pullback = jax.vjp(norm_rows, residual, gain_vec, shift_vec)
    grad_input, grad_gain, grad_shift = pullback(grad_normed)
    width_dev = query_w.shape[1]
    grads = (
        grad_joined[:, :width_dev],
        grad_joined[:, width_dev : 2 * width_dev],
        grad_joined[:, 2 * width_dev :],
        grad_output,
    )
    return (grad_resid + grad_input, grad_gain, grad_shift, grads)


def space_back(grad_resid, residual, saved, gain_vec, shift_vec, weights, scaling):
    normed_all, heads_split, attn_probs, attended_rows = saved
    grad_mixed, grad_output = attention_head(grad_resid, attended_rows, weights[3])
    batch_rows, place_count, heads_dev = (
        heads_split.shape[0],
        heads_split.shape[1],
        heads_split.shape[3],
    )
    grad_heads = grad_mixed.reshape(batch_rows, place_count, heads_dev, HEAD_DIM)
    grad_query, grad_key, grad_value = attend_back(
        grad_heads,
        heads_split[:, :, 0],
        heads_split[:, :, 1],
        heads_split[:, :, 2],
        attn_probs,
        scaling,
        SPACE_FORMS,
    )
    grad_proj = jnp.stack((grad_query, grad_key, grad_value), axis=2).reshape(
        grad_mixed.shape[0], grad_mixed.shape[1], place_count, 3 * heads_dev * HEAD_DIM
    )
    return attention_tail(
        grad_resid, grad_proj, normed_all, residual, gain_vec, shift_vec, weights, grad_output
    )


def time_back(grad_resid, residual, saved, gain_vec, shift_vec, weights, selector, scaling):
    normed_all, heads_split, attn_probs, attended_rows = saved
    grad_mixed, grad_output = attention_head(grad_resid, attended_rows, weights[3])
    packed = jnp.einsum(
        "sp,cfpk->cfsk", selector, grad_mixed, preferred_element_type=jnp.float32
    ).astype(jnp.bfloat16)
    by_place = to_places(packed)
    clip_count, frame_total, capacity = (
        heads_split.shape[0],
        heads_split.shape[1],
        heads_split.shape[2],
    )
    heads_dev = heads_split.shape[4]
    grad_heads = by_place.reshape(clip_count, frame_total, capacity, heads_dev, HEAD_DIM)
    grad_query, grad_key, grad_value = attend_back(
        grad_heads,
        heads_split[:, :, :, 0],
        heads_split[:, :, :, 1],
        heads_split[:, :, :, 2],
        attn_probs,
        scaling,
        TIME_FORMS,
    )
    stacked = jnp.stack((grad_query, grad_key, grad_value), axis=3).reshape(
        clip_count, frame_total, capacity, 3 * heads_dev * HEAD_DIM
    )
    by_frame = to_frames(stacked)
    grad_proj = jnp.einsum(
        "sp,cfsk->cfpk", selector, by_frame, preferred_element_type=jnp.float32
    ).astype(jnp.bfloat16)
    return attention_tail(
        grad_resid, grad_proj, normed_all, residual, gain_vec, shift_vec, weights, grad_output
    )


def mlp_back(grad_resid, residual, saved, gain_vec, shift_vec, weights):
    normed_all, before, hidden = saved
    weight_in, weight_out, bias_vec_out, bias_vec_in = weights
    grad_all = gather_rows(grad_resid.astype(jnp.bfloat16))
    grad_bias_out = jnp.sum(grad_all.astype(jnp.float32), axis=(0, 1, 2))
    grad_hidden = jnp.einsum(
        "cfpd,kd->cfpk", grad_all, weight_out, preferred_element_type=jnp.float32
    )
    grad_weight_out = jnp.einsum(
        "cfpk,cfpd->kd", hidden, grad_all, preferred_element_type=jnp.float32
    )
    _, gelu_back = jax.vjp(partial(jax.nn.gelu, approximate=True), before)
    grad_before = gelu_back(grad_hidden)[0].astype(jnp.bfloat16)
    grad_bias_in = jnp.sum(grad_before.astype(jnp.float32), axis=(0, 1, 2))
    grad_weight_in = jnp.einsum(
        "cfpd,cfpk->dk", normed_all, grad_before, preferred_element_type=jnp.float32
    )
    grad_local = jnp.einsum(
        "cfpk,dk->cfpd", grad_before, weight_in, preferred_element_type=jnp.float32
    )
    grad_normed = reduce_rows(grad_local)
    _, pullback = jax.vjp(norm_rows, residual, gain_vec, shift_vec)
    grad_input, grad_gain, grad_shift = pullback(grad_normed)
    return (
        grad_resid + grad_input,
        grad_gain,
        grad_shift,
        (grad_weight_in, grad_weight_out, grad_bias_out, grad_bias_in),
    )


def share_attention(grads):
    grad_query, grad_key, grad_value, grad_output = grads
    return (
        lax.psum_scatter(grad_query, "frame", scatter_dimension=0, tiled=True),
        lax.psum_scatter(grad_key, "frame", scatter_dimension=0, tiled=True),
        lax.psum_scatter(grad_value, "frame", scatter_dimension=0, tiled=True),
        lax.psum_scatter(grad_output, "frame", scatter_dimension=1, tiled=True),
    )


def shards(
    tokens,
    query_space,
    key_space,
    value_space,
    output_space,
    query_time,
    key_time,
    value_time,
    output_time,
    mlp_in,
    bias_in,
    mlp_out,
    bias_out,
    gain_first,
    shift_first,
    gain_second,
    shift_second,
    gain_third,
    shift_third,
    place_slot,
    cotangent,
):
    norm_params = (
        lax.all_gather(gain_first, ("frame", "tensor"), axis=0, tiled=True),
        lax.all_gather(shift_first, ("frame", "tensor"), axis=0, tiled=True),
        lax.all_gather(gain_second, ("frame", "tensor"), axis=0, tiled=True),
        lax.all_gather(shift_second, ("frame", "tensor"), axis=0, tiled=True),
        lax.all_gather(gain_third, ("frame", "tensor"), axis=0, tiled=True),
        lax.all_gather(shift_third, ("frame", "tensor"), axis=0, tiled=True),
    )
    scaling = HEAD_DIM ** (-0.5)
    frame_devices = lax.axis_size("frame")
    slot_total = CAP * frame_devices
    selector = (
        lax.broadcasted_iota(jnp.int32, (slot_total, place_slot.shape[0]), 0) == place_slot[None, :]
    ).astype(jnp.bfloat16)
    key_bias = jnp.where(place_slot >= 0, 0.0, -1e30).astype(jnp.float32)[None, None, None, :]
    space_w = fetch_attention(query_space, key_space, value_space, output_space)
    time_w = fetch_attention(query_time, key_time, value_time, output_time)
    mlp_w = fetch_mlp(mlp_in, mlp_out, bias_out, bias_in)
    residual = tokens.astype(jnp.float32)
    after_space, _ = space_forward(
        residual, norm_params[0], norm_params[1], space_w, key_bias, scaling
    )
    after_time, _ = time_forward(
        after_space, norm_params[2], norm_params[3], time_w, selector, scaling
    )
    after_mlp, _ = mlp_forward(after_time, norm_params[4], norm_params[5], mlp_w)
    result = after_mlp.astype(jnp.bfloat16)
    space_w = fetch_attention(query_space, key_space, value_space, output_space)
    time_w = fetch_attention(query_time, key_time, value_time, output_time)
    mlp_w = fetch_mlp(mlp_in, mlp_out, bias_out, bias_in)
    again_space, space_saved = space_forward(
        residual, norm_params[0], norm_params[1], space_w, key_bias, scaling
    )
    again_time, time_saved = time_forward(
        again_space, norm_params[2], norm_params[3], time_w, selector, scaling
    )
    _, mlp_saved = mlp_forward(again_time, norm_params[4], norm_params[5], mlp_w)
    grad_mlp = cotangent.astype(jnp.float32)
    grad_time, grad_gain_third, grad_shift_third, mlp_grads = mlp_back(
        grad_mlp, again_time, mlp_saved, norm_params[4], norm_params[5], mlp_w
    )
    grad_weight_in, grad_weight_out, grad_bias_vec_out, grad_bias_vec_in = mlp_grads
    tiled_bias = jnp.broadcast_to(
        grad_bias_vec_in[None, :], (frame_devices, grad_bias_vec_in.shape[0])
    )
    mlp_shares = (
        lax.psum_scatter(grad_weight_in, "frame", scatter_dimension=0, tiled=True),
        lax.psum_scatter(grad_weight_out, "frame", scatter_dimension=1, tiled=True),
        lax.psum_scatter(grad_bias_vec_out, "frame", scatter_dimension=0, tiled=True),
        lax.psum_scatter(tiled_bias, "frame", scatter_dimension=0, tiled=True),
    )
    grad_space, grad_gain_second, grad_shift_second, time_grads = time_back(
        grad_time,
        again_space,
        time_saved,
        norm_params[2],
        norm_params[3],
        time_w,
        selector,
        scaling,
    )
    time_shares = share_attention(time_grads)
    grad_tokens, grad_gain_first, grad_shift_first, space_grads = space_back(
        grad_space, residual, space_saved, norm_params[0], norm_params[1], space_w, scaling
    )
    space_shares = share_attention(space_grads)
    norm_shares = (
        lax.psum_scatter(grad_gain_first, ("frame", "tensor"), scatter_dimension=0, tiled=True),
        lax.psum_scatter(grad_shift_first, ("frame", "tensor"), scatter_dimension=0, tiled=True),
        lax.psum_scatter(grad_gain_second, ("frame", "tensor"), scatter_dimension=0, tiled=True),
        lax.psum_scatter(grad_shift_second, ("frame", "tensor"), scatter_dimension=0, tiled=True),
        lax.psum_scatter(grad_gain_third, ("frame", "tensor"), scatter_dimension=0, tiled=True),
        lax.psum_scatter(grad_shift_third, ("frame", "tensor"), scatter_dimension=0, tiled=True),
    )
    totals = lax.psum(
        (
            space_shares[0],
            space_shares[1],
            space_shares[2],
            space_shares[3],
            time_shares[0],
            time_shares[1],
            time_shares[2],
            time_shares[3],
            mlp_shares[0],
            mlp_shares[3],
            mlp_shares[1],
            mlp_shares[2],
            norm_shares[0],
            norm_shares[1],
            norm_shares[2],
            norm_shares[3],
            norm_shares[4],
            norm_shares[5],
        ),
        "rep",
    )
    return (
        result,
        grad_tokens,
        totals[0],
        totals[1],
        totals[2],
        totals[3],
        totals[4],
        totals[5],
        totals[6],
        totals[7],
        totals[8],
        totals[9].reshape(-1),
        totals[10],
        totals[11],
        totals[12],
        totals[13],
        totals[14],
        totals[15],
        totals[16],
        totals[17],
    )


def solution(mesh):
    placed = (
        P("rep", "frame", "tensor", None),
        P("frame", "tensor"),
        P("frame", "tensor"),
        P("frame", "tensor"),
        P("tensor", "frame"),
        P("frame", "tensor"),
        P("frame", "tensor"),
        P("frame", "tensor"),
        P("tensor", "frame"),
        P("frame", "tensor"),
        P("tensor"),
        P("tensor", "frame"),
        P("frame"),
        P(("frame", "tensor")),
        P(("frame", "tensor")),
        P(("frame", "tensor")),
        P(("frame", "tensor")),
        P(("frame", "tensor")),
        P(("frame", "tensor")),
        P(),
        P("rep", "frame", "tensor", None),
    )
    return jax.shard_map(
        shards,
        mesh=mesh,
        in_specs=placed,
        out_specs=(
            P("rep", "frame", "tensor", None),
            P("rep", "frame", "tensor", None),
            P("frame", "tensor"),
            P("frame", "tensor"),
            P("frame", "tensor"),
            P("tensor", "frame"),
            P("frame", "tensor"),
            P("frame", "tensor"),
            P("frame", "tensor"),
            P("tensor", "frame"),
            P("frame", "tensor"),
            P("tensor"),
            P("tensor", "frame"),
            P("frame"),
            P(("frame", "tensor")),
            P(("frame", "tensor")),
            P(("frame", "tensor")),
            P(("frame", "tensor")),
            P(("frame", "tensor")),
            P(("frame", "tensor")),
        ),
        check_vma=False,
    )
```

profile of v0, /device:TPU:0, one launch (start us, length us, event | category | flops | bytes accessed | tf_op | source)
XLA Modules:
  0.0 1709.6 jit_solution(6022377340424163276)
XLA Ops:
  18.8 63.0 %all-reduce.22 = (f32[768]{0:T(1024)S(1)}, f32[768]{0:T(1024)S(1)}, f32[768]{0:T(1024)S(1)}, f32[768]{0:T(1024)S(1)}, f32[768]{0:T(1024)}, /*index=5*/f32[768]{0:T(1024)}) all-reduce(f32[768]{0:T(1024)S(1)} %dynamic-update-slice.1, f32[768]{0:T(1024)S(1)} %dynamic-update-slice, ...), channel_id=1, replica_groups=mesh['rep'=2,'frame'=4,'tensor'=4] {'frame','tensor'}, use_global_device_ids=true, to_apply=%add.1 | all-reduce | flops 4608 | bytes 36864
  84.4 15.2 all_gather.85
  99.9 14.4 all_gather.86
  114.5 15.2 all_gather.87
  129.9 14.4 all_gather.88
  164.7 91.4 %all-reduce.34.cloned.1.call-done = f32[2,4,196,768]{3,1,0,2:T(4,128)} async-done(((f32[2,4,196,768]{3,1,0,2:T(4,128)}), f32[2,4,196,768]{3,1,0,2:T(4,128)}) %all-reduce.34.cloned.1.call-update) | async-done | bytes 4816912
  260.2 14.5 all_gather.92
  274.9 15.5 all_gather.93
  290.6 14.9 all_gather.94
  317.3 55.8 %all_to_all.76 = bf16[2,4,256,576]{3,1,0,2:T(4,128)(2,1)S(1)} all-to-all(bf16[2,4,256,576]{3,1,0,2:T(4,128)(2,1)} %copy.301), channel_id=1, replica_groups=mesh['rep'=2,'frame'=4,'tensor'=4] {'frame'}, dimensions={2} | all-to-all | bytes 4718592 | tf_op jit(solution)/shard_map/all_to_all | solution.py:32
  424.9 31.2 %all_gather.95 = bf16[192,768]{0,1:T(8,128)(2,1)S(1)} all-gather(bf16[192,192]{0,1:T(8,128)(2,1)S(1)} %copy.313), channel_id=1, replica_groups=mesh['rep'=2,'frame'=4,'tensor'=4] {'frame'}, dimensions={1}, use_global_device_ids=true | all-gather | bytes 368640 | tf_op jit(solution)/shard_map/all_gather | solution.py:44
  462.4 94.7 %all-reduce.36.cloned.1.call-done = f32[2,4,196,768]{3,1,0,2:T(4,128)} async-done(((f32[2,4,196,768]{3,1,0,2:T(4,128)}), f32[2,4,196,768]{3,1,0,2:T(4,128)}) %all-reduce.36.cloned.1.call-update) | async-done | bytes 4816912
  569.8 21.3 %all-gather.13.cloned.1.call-done = bf16[2,4,196,768]{3,1,0,2:T(4,128)(2,1)} async-done(((bf16[2,4,49,768]{3,1,0,2:T(4,128)(2,1)}), bf16[2,4,196,768]{3,1,0,2:T(4,128)(2,1)}) %all-gather.13.cloned.1.call-update) | async-done | bytes 2408464 | tf_op jit(solution)/shard_map/all_gather | solution.py:24
  597.6 25.0 %all-gather.17.cloned.1.call-done = bf16[768,768]{0,1:T(8,128)(2,1)} async-done(((bf16[768,192]{0,1:T(8,128)(2,1)}), bf16[768,768]{0,1:T(8,128)(2,1)}) %all-gather.17.cloned.1.call-update) | async-done | bytes 1179664 | tf_op jit(solution)/shard_map/all_gather | solution.py:51
  622.6 25.7 %all-gather.19.cloned.1.call-done = bf16[2,4,196,768]{3,1,0,2:T(4,128)(2,1)} async-done(((bf16[2,4,49,768]{3,1,0,2:T(4,128)(2,1)}), bf16[2,4,196,768]{3,1,0,2:T(4,128)(2,1)}) %all-gather.19.cloned.1.call-update) | async-done | bytes 2408464 | tf_op jit(solution)/shard_map/all_gather | solution.py:24
  664.2 95.5 %all-reduce.38.cloned.1.call-done = f32[2,4,196,768]{3,1,0,2:T(4,128)} async-done(((f32[2,4,196,768]{3,1,0,2:T(4,128)}), f32[2,4,196,768]{3,1,0,2:T(4,128)}) %all-reduce.38.cloned.1.call-update) | async-done | bytes 4816912
  775.9 24.4 %all-gather.21.cloned.1.call-done = bf16[2,4,196,768]{3,1,0,2:T(4,128)(2,1)} async-done(((bf16[2,4,49,768]{3,1,0,2:T(4,128)(2,1)}), bf16[2,4,196,768]{3,1,0,2:T(4,128)(2,1)}) %all-gather.21.cloned.1.call-update) | async-done | bytes 2408464 | tf_op jit(solution)/shard_map/all_gather | solution.py:24
  806.5 30.7 %all_to_all.77 = bf16[2,4,256,192]{3,1,0,2:T(4,128)(2,1)S(1)} all-to-all(bf16[2,4,256,192]{3,1,0,2:T(4,128)(2,1)} %copy.332), channel_id=1, replica_groups=mesh['rep'=2,'frame'=4,'tensor'=4] {'frame'}, dimensions={2} | all-to-all | bytes 1572864 | tf_op jit(solution)/shard_map/all_to_all | solution.py:32
  869.5 63.1 %all_to_all.78 = bf16[2,16,64,576]{3,2,0,1:T(8,128)(2,1)S(1)} all-to-all(bf16[2,16,64,576]{3,2,0,1:T(8,128)(2,1)} %copy.339), channel_id=1, replica_groups=mesh['rep'=2,'frame'=4,'tensor'=4] {'frame'}, dimensions={1} | all-to-all | bytes 4718592 | tf_op jit(solution)/shard_map/all_to_all | solution.py:36
  941.6 93.6 %all-reduce.40.cloned.1.call-done = f32[2,4,196,768]{3,1,0,2:T(4,128)} async-done(((f32[2,4,196,768]{3,1,0,2:T(4,128)}), f32[2,4,196,768]{3,1,0,2:T(4,128)}) %all-reduce.40.cloned.1.call-update) | async-done | bytes 4816912
  1121.0 23.3 %reduce-scatter.41.cloned.1.call-done = f32[192,192]{1,0:T(8,128)} async-done(((f32[768,192]{1,0:T(8,128)}), f32[192,192]{1,0:T(8,128)}) %reduce-scatter.41.cloned.1.call-update) | async-done | bytes 147472
  1146.0 23.1 %reduce-scatter.39.cloned.1.call-done = f32[192,192]{1,0:T(8,128)} async-done(((f32[768,192]{1,0:T(8,128)}), f32[192,192]{1,0:T(8,128)}) %reduce-scatter.39.cloned.1.call-update) | async-done | bytes 147472
  1170.8 23.3 %reduce-scatter.37.cloned.1.call-done = f32[192,192]{1,0:T(8,128)} async-done(((f32[768,192]{1,0:T(8,128)}), f32[192,192]{1,0:T(8,128)}) %reduce-scatter.37.cloned.1.call-update) | async-done | bytes 147472
  1195.9 23.1 %reduce-scatter.35.cloned.1.call-done = f32[192,192]{1,0:T(8,128)} async-done(((f32[768,192]{1,0:T(8,128)}), f32[192,192]{1,0:T(8,128)}) %reduce-scatter.35.cloned.1.call-update) | async-done | bytes 147472
  1220.7 23.3 %reduce-scatter.33.cloned.1.call-done = f32[192,192]{1,0:T(8,128)} async-done(((f32[768,192]{1,0:T(8,128)}), f32[192,192]{1,0:T(8,128)}) %reduce-scatter.33.cloned.1.call-update) | async-done | bytes 147472
  1245.7 23.3 %reduce-scatter.31.cloned.1.call-done = f32[192,192]{1,0:T(8,128)} async-done(((f32[768,192]{1,0:T(8,128)}), f32[192,192]{1,0:T(8,128)}) %reduce-scatter.31.cloned.1.call-update) | async-done | bytes 147472
  1270.8 47.7 %reduce-scatter.29.cloned.1.call-done = f32[768,192]{0,1:T(8,128)} async-done(((f32[768,768]{0,1:T(8,128)}), f32[768,192]{0,1:T(8,128)}) %reduce-scatter.29.cloned.1.call-update) | async-done | bytes 589840 | tf_op jit(solution)/shard_map/reduce_scatter | solution.py:371
  1318.5 49.4 %reduce-scatter.27.cloned.1.call-done = f32[192,768]{1,0:T(8,128)} async-done(((f32[768,768]{1,0:T(8,128)}), f32[192,768]{1,0:T(8,128)}) %reduce-scatter.27.cloned.1.call-update) | async-done | bytes 589840 | tf_op jit(solution)/shard_map/reduce_scatter | solution.py:370
  1399.3 15.8 all-reduce.24
  1415.9 28.8 %all-reduce.44.cloned.1.call-done = (f32[192,192]{0,1:T(8,128)}, f32[192,192]{0,1:T(8,128)}, f32[192,192]{0,1:T(8,128)}, f32[192,192]{1,0:T(8,128)}, f32[192,192...) async-done(((f32[192,192]{0,1:T(8,128)}, f32[192,192]{0,1:T(8,128)}, ...) | async-done | bytes 2359312 | tf_op jit(solution)/shard_map/psum | solution.py:398
  1455.1 165.3 %all-reduce.42.cloned.1.call-done = (f32[2,4,196,768]{3,1,0,2:T(4,128)}, f32[2,4,196,768]{3,1,0,2:T(4,128)}) async-done(((f32[2,4,196,768]{3,1,0,2:T(4,128)}, f32[2,4,196,768]{3,1,0,2:T(4,128)}), (f32[2,4,196,768]{3,1,0,2:T(4,128)}, f32[2,4,196,768]{3,1,0,2:T(4,128)})) %all-reduce.42.cloned.1.call-update) | async-done | bytes 9633808
  1628.2 60.4 %all-reduce.21 = (f32[768]{0:T(1024)S(1)}, f32[768]{0:T(1024)S(1)}, f32[768]{0:T(1024)S(1)}, f32[768]{0:T(1024)S(1)}, f32[768]{0:T(1024)S(1)}, /*index=5*/f32[768]{0:T(1024)S(1)}) all-reduce(f32[768]{0:T(1024)S(1)} %get-tuple-element.124, ...), channel_id=20, replica_groups=mesh['rep'=2,'frame'=4,'tensor'=4] {'frame','tensor'}, use_global_device_ids=true, to_apply=%region_51.52.clone | all-reduce | flops 4608 | bytes 36864
  (395 shorter events, 362.3 us)
Async XLA Ops:
  8.0 136.3 %all-gather.9.cloned.1.call-start = ((), (), s32[]{:S(2)}) async-start(), calls=%async_computation.14 | async-start | bytes 3010560 | tf_op jit(solution)/shard_map/all_gather | solution.py:24
  9.8 104.7 %copy-start.17 = (f32[2,4,49]{1,0,2:T(2,128)}, f32[2,4,49]{1,0,2:T(2,128)S(1)}, u32[]{:S(2)}) copy-start(f32[2,4,49]{1,0,2:T(2,128)S(1)} %copy.278) | copy-start | bytes 4708
  11.5 103.0 %copy-start.52 = (bf16[192,192]{1,0:T(8,128)(2,1)S(1)}, bf16[192,192]{1,0:T(8,128)(2,1)}, u32[]{:S(2)}) copy-start(bf16[192,192]{1,0:T(8,128)(2,1)} %param.24) | copy-start | bytes 221188
  84.2 171.9 %all-reduce.34.cloned.1.call-start = ((), (), s32[]{:S(2)}) async-start(), calls=%async_computation.32 | async-start | bytes 9633792
  162.8 142.8 %all-gather.11.cloned.1.call-start = ((), (), s32[]{:S(2)}) async-start(), calls=%async_computation.15 | async-start | bytes 3010560 | tf_op jit(solution)/shard_map/all_gather | solution.py:24
  421.2 34.9 %all-to-all-start.1 = ((bf16[2,16,64,192]{3,2,0,1:T(8,128)(2,1)}), bf16[2,16,64,192]{3,2,0,1:T(8,128)(2,1)S(1)}, u32[]{:S(2)}, u32[]{:S(2)}) async-start(bf16[2,16,64,192]{3,2,0,1:T(8,128)(2,1)} %copy.309), calls=%async_computation.1 | async-start | bytes 2097152 | tf_op jit(solution)/shard_map/all_to_all | solution.py:36
  424.7 132.4 %all-reduce.36.cloned.1.call-start = ((), (), s32[]{:S(2)}) async-start(), calls=%async_computation.33 | async-start | bytes 9633792
  461.8 108.0 %all-gather.15.cloned.1.call-start = ((), (), s32[]{:S(2)}) async-start(), calls=%async_computation.17 | async-start | bytes 1474560 | tf_op jit(solution)/shard_map/all_gather | solution.py:50
  462.4 128.7 %all-gather.13.cloned.1.call-start = ((), (), s32[]{:S(2)}) async-start(), calls=%async_computation.16 | async-start | bytes 3010560 | tf_op jit(solution)/shard_map/all_gather | solution.py:24
  566.6 56.0 %all-gather.17.cloned.1.call-start = ((), (), s32[]{:S(2)}) async-start(), calls=%async_computation.18 | async-start | bytes 1474560 | tf_op jit(solution)/shard_map/all_gather | solution.py:51
  567.2 81.1 %all-gather.19.cloned.1.call-start = ((), (), s32[]{:S(2)}) async-start(), calls=%async_computation.19 | async-start | bytes 3010560 | tf_op jit(solution)/shard_map/all_gather | solution.py:24
  568.3 191.4 %all-reduce.38.cloned.1.call-start = ((), (), s32[]{:S(2)}) async-start(), calls=%async_computation.34 | async-start | bytes 9633792
  664.2 136.1 %all-gather.21.cloned.1.call-start = ((), (), s32[]{:S(2)}) async-start(), calls=%async_computation.20 | async-start | bytes 3010560 | tf_op jit(solution)/shard_map/all_gather | solution.py:24
  775.6 259.6 %all-reduce.40.cloned.1.call-start = ((), (), s32[]{:S(2)}) async-start(), calls=%async_computation.35 | async-start | bytes 9633792
  941.5 93.7 %copy-start.29 = (f32[2,4,49]{1,0,2:T(2,128)S(1)}, f32[2,4,49]{1,0,2:T(2,128)}, u32[]{:S(2)}) copy-start(f32[2,4,49]{1,0,2:T(2,128)} %copy-done.28) | copy-start | bytes 4708
  941.6 127.4 %all-gather.23.cloned.1.call-start = ((), (), s32[]{:S(2)}) async-start(), calls=%async_computation.21 | async-start | bytes 3010560 | tf_op jit(solution)/shard_map/all_gather | solution.py:24
  1044.5 67.9 %reduce-scatter.45.cloned.1.call-start = ((), (), s32[]{:S(2)}) async-start(), calls=%async_computation.31 | async-start | bytes 983040
  1048.6 70.6 %reduce-scatter.43.cloned.1.call-start = ((), (), s32[]{:S(2)}) async-start(), calls=%async_computation.30 | async-start | bytes 983040
  1054.3 90.0 %reduce-scatter.41.cloned.1.call-start = ((), (), s32[]{:S(2)}) async-start(), calls=%async_computation.29 | async-start | bytes 983040
  1055.5 113.6 %reduce-scatter.39.cloned.1.call-start = ((), (), s32[]{:S(2)}) async-start(), calls=%async_computation.28 | async-start | bytes 983040
  1056.8 137.4 %reduce-scatter.37.cloned.1.call-start = ((), (), s32[]{:S(2)}) async-start(), calls=%async_computation.27 | async-start | bytes 983040
  1086.0 133.0 %reduce-scatter.35.cloned.1.call-start = ((), (), s32[]{:S(2)}) async-start(), calls=%async_computation.26 | async-start | bytes 983040
  1095.6 148.4 %reduce-scatter.33.cloned.1.call-start = ((), (), s32[]{:S(2)}) async-start(), calls=%async_computation.25 | async-start | bytes 983040
  1096.8 172.2 %reduce-scatter.31.cloned.1.call-start = ((), (), s32[]{:S(2)}) async-start(), calls=%async_computation.24 | async-start | bytes 983040
  1098.1 220.4 %reduce-scatter.29.cloned.1.call-start = ((), (), s32[]{:S(2)}) async-start(), calls=%async_computation.23 | async-start | bytes 2949120 | tf_op jit(solution)/shard_map/reduce_scatter | solution.py:371
  1105.9 262.0 %reduce-scatter.27.cloned.1.call-start = ((), (), s32[]{:S(2)}) async-start(), calls=%async_computation.22 | async-start | bytes 2949120 | tf_op jit(solution)/shard_map/reduce_scatter | solution.py:370
  1112.3 332.4 %all-reduce.44.cloned.1.call-start = ((), (), s32[]{:S(2)}) async-start(), calls=%async_computation.37 | async-start | bytes 5505024 | tf_op jit(solution)/shard_map/psum | solution.py:398
  1146.0 222.1 %copy-start.68 = (bf16[768,768]{0,1:T(8,128)(2,1)S(1)}, bf16[768,768]{0,1:T(8,128)(2,1)}, u32[]{:S(2)}) copy-start(bf16[768,768]{0,1:T(8,128)(2,1)} %all-gather.17.cloned.1.call-done) | copy-start | bytes 3538948
  1367.9 252.5 %all-reduce.42.cloned.1.call-start = ((), (), s32[]{:S(2)}) async-start(), calls=%async_computation.36 | async-start | bytes 19267584
  1453.3 169.7 %copy-start.1 = (bf16[2,4,49,768]{3,1,2,0:T(4,128)(2,1)S(1)}, bf16[2,4,49,768]{3,1,2,0:T(4,128)(2,1)}, u32[]{:S(2)}) copy-start(bf16[2,4,49,768]{3,1,2,0:T(4,128)(2,1)} %param.21) | copy-start | bytes 1806340
  1453.3 169.7 %copy-start.18 = (f32[2,4,49]{1,0,2:T(2,128)S(1)}, f32[2,4,49]{1,0,2:T(2,128)}, u32[]{:S(2)}) copy-start(f32[2,4,49]{1,0,2:T(2,128)} %copy-done.17) | copy-start | bytes 4708
  1453.3 169.7 %copy-start.57 = (f32[768]{0:T(1024)S(1)}, f32[768]{0:T(1024)}, u32[]{:S(2)}) copy-start(f32[768]{0:T(1024)} %copy-done.56) | copy-start | bytes 9220
  (69 other events, 1085.0 us)
Sparse Core Ops, SparseCore 0:
  84.4 21.5 all-gather.8
  162.9 93.1 all-reduce.33
  260.4 24.4 all-gather.10
  461.9 95.1 all-reduce.35
  775.8 24.4 all-gather.20
  1368.0 76.6 all-reduce.43
  1447.3 173.0 all-reduce.41
Sparse Core Ops, SparseCore 1:
  463.8 29.6 all-gather.14
  566.7 24.3 all-gather.12
  592.5 30.0 all-gather.16
  624.8 23.5 all-gather.18
  664.3 95.4 all-reduce.37
  941.6 93.5 all-reduce.39
  1044.6 24.3 all-gather.22
  1071.1 23.2 reduce-scatter.44
  1096.6 22.6 reduce-scatter.42
  1121.6 22.7 reduce-scatter.40
  1146.5 22.6 reduce-scatter.38
  1171.4 22.7 reduce-scatter.36
  1196.3 22.6 reduce-scatter.34
  1221.3 22.6 reduce-scatter.32
  1246.3 22.7 reduce-scatter.30
  1271.4 47.1 reduce-scatter.28
  1320.8 47.0 reduce-scatter.26
where the time goes:
time: 1720 us; the launch traced here: 1710 us
  waiting for transfers between devices  921 us (54%)
  blocking collectives  440 us (26%)
  local copies, waits for them, and re-layouts  154 us (9%)
  matrix products  100 us (6%)
  other arithmetic  68.8 us (4%)
  between operations  20.9 us (1%)
    unnamed x37, waiting for transfers between devices  687 us
    unnamed x4, blocking collectives  150 us
    all_to_all x2, blocking collectives, to_places(): lax.all_to_all(values, 'frame', split_axis=2, concat_axis=1, tiled=True)  86.5 us
    all_gather x6, waiting for transfers between devices, gather_rows(): return lax.all_gather(values, 'tensor', axis=2, tiled=True)  83.3 us
    unnamed x207, local copies, waits for them, and re-layouts  67.5 us
    all_to_all x1, blocking collectives, to_frames(): lax.all_to_all(values, 'frame', split_axis=1, concat_axis=2, tiled=True)  63.1 us
    reduce_scatter x1, waiting for transfers between devices, shards(): lax.psum_scatter(grad_weight_in, 'frame', scatter_dimension=0, tiled=True)  49.4 us
    reduce_scatter x1, waiting for transfers between devices, shards(): lax.psum_scatter(grad_weight_out, 'frame', scatter_dimension=1, tiled=True)  47.7 us
  transfers between devices with their start and end apart: 25, of which 20 were waited for; matrix products, arithmetic and copies ran while one was open for 7% of the time, Pallas kernels for 0%

commit v1 on v0

v1 whole, which is shorter than its diff:
```python
from functools import partial

import jax
import jax.numpy as jnp
from jax import lax
from jax.experimental import pallas as pl
from jax.experimental.pallas import tpu as pltpu
from jax.sharding import PartitionSpec as P

HEAD = 64
PAD = 56
BF = jnp.bfloat16
F32 = jnp.float32
NT = (((1,), (1,)), ((), ()))
TN = (((0,), (0,)), ((), ()))
GELU_C = 0.7978845608028654
SCALE = HEAD ** (-0.5)


def dot(a, b, dims=(((1,), (0,)), ((), ()))):
    return lax.dot_general(a, b, dims, preferred_element_type=F32)


def norm_stats(v):
    m = jnp.mean(v, axis=-1, keepdims=True)
    off = v - m
    s = jnp.mean(off * off, axis=-1, keepdims=True)
    r = lax.rsqrt(s + 1e-06)
    return off * r, r


def norm(v, g, b):
    xhat, _ = norm_stats(v)
    return xhat * g + b


def norm_back(v, g, dy):
    xhat, r = norm_stats(v)
    dyg = dy * g
    mean1 = jnp.mean(dyg, axis=-1, keepdims=True)
    mean2 = jnp.mean(dyg * xhat, axis=-1, keepdims=True)
    dx = r * (dyg - mean1 - xhat * mean2)
    dgain = jnp.sum(dy * xhat, axis=0, keepdims=True)
    dshift = jnp.sum(dy, axis=0, keepdims=True)
    return dx, dgain, dshift


def softmax(s):
    m = jnp.max(s, axis=-1, keepdims=True)
    e = jnp.exp(s - m)
    return e / jnp.sum(e, axis=-1, keepdims=True)


def attend_head(q, k, v, bias):
    s = dot(q, k, NT) * SCALE + bias
    p = softmax(s)
    return dot(p.astype(BF), v).astype(BF)


def attend_head_back(do, q, k, v, bias):
    s = dot(q, k, NT) * SCALE + bias
    p = softmax(s)
    dp = dot(do, v, NT)
    dv = dot(p.astype(BF), do, TN)
    inner = jnp.sum(dp * p, axis=-1, keepdims=True)
    ds = (p * (dp - inner)).astype(BF)
    dq = dot(ds, k) * SCALE
    dk = dot(ds, q, TN) * SCALE
    return dq.astype(BF), dk.astype(BF), dv.astype(BF)


def space_forward(width, heads, frames, rows, x_ref, vec_ref, bias_ref, w_ref, qkv_ref, os_ref, xs_ref, ht_ref, h_scr):
    t = pl.program_id(0)

    @pl.when(t == 0)
    def _():
        x = x_ref[...].astype(F32)
        h_scr[...] = norm(x, vec_ref[0:1, :], vec_ref[1:2, :]).astype(BF)
        xs_ref[...] = x

    qkv_ref[0] = dot(h_scr[...], w_ref[0, 0, :, : 3 * width]).astype(BF)
    bias = bias_ref[...]
    for i in range(frames):
        r = pl.ds(i * rows, rows)
        for h in range(heads):
            q = qkv_ref[0, r, h * HEAD : (h + 1) * HEAD]
            k = qkv_ref[0, r, width + h * HEAD : width + (h + 1) * HEAD]
            v = qkv_ref[0, r, 2 * width + h * HEAD : 2 * width + (h + 1) * HEAD]
            os_ref[0, r, h * HEAD : (h + 1) * HEAD] = attend_head(q, k, v, bias)
    xs_ref[...] += dot(os_ref[0], w_ref[0, 0, :, 3 * width :], NT)

    @pl.when(t == pl.num_programs(0) - 1)
    def _():
        ht_ref[...] = norm(xs_ref[...], vec_ref[2:3, :], vec_ref[3:4, :]).astype(BF)


def space_backward(
    width, heads, frames, rows,
    x_ref, xs_ref, gt_ref, dht_ref, vec_ref, bias_ref, w_ref, qkv_ref, os_ref,
    gx_ref, gw_ref, sv_ref, h_scr, gs_scr, dat_scr, dh_scr, dqkv_scr,
):
    t = pl.program_id(0)

    @pl.when(t == 0)
    def _():
        x = x_ref[...].astype(F32)
        h_scr[...] = norm(x, vec_ref[0:1, :], vec_ref[1:2, :]).astype(BF)
        dx, dg, db = norm_back(xs_ref[...], vec_ref[2:3, :], dht_ref[...].astype(F32))
        gs = gt_ref[...] + dx
        gs_scr[...] = gs
        dat_scr[...] = gs.astype(BF)
        sv_ref[2:3, :] = dg
        sv_ref[3:4, :] = db
        sv_ref[4:8, :] = jnp.zeros((4, sv_ref.shape[1]), F32)
        dh_scr[...] = jnp.zeros_like(dh_scr)

    dat = dat_scr[...]
    dos = dot(dat, w_ref[0, 0, :, 3 * width :]).astype(BF)
    bias = bias_ref[...]
    for i in range(frames):
        r = pl.ds(i * rows, rows)
        for h in range(heads):
            a, b, c = (slice(j * width + h * HEAD, j * width + (h + 1) * HEAD) for j in range(3))
            dq, dk, dv = attend_head_back(
                dos[i * rows : (i + 1) * rows, a], qkv_ref[0, r, a], qkv_ref[0, r, b], qkv_ref[0, r, c], bias
            )
            dqkv_scr[r, a] = dq
            dqkv_scr[r, b] = dk
            dqkv_scr[r, c] = dv
    dqkv = dqkv_scr[...]
    gw_ref[0, :, : 3 * width] = dot(h_scr[...], dqkv, TN).astype(BF)
    gw_ref[0, :, 3 * width :] = dot(dat, os_ref[0], TN).astype(BF)
    dh_scr[...] += dot(dqkv, w_ref[0, 0, :, : 3 * width], NT)

    @pl.when(t == pl.num_programs(0) - 1)
    def _():
        dx, dg, db = norm_back(x_ref[...].astype(F32), vec_ref[0:1, :], dh_scr[...])
        gx_ref[...] = (gs_scr[...] + dx).astype(gx_ref.dtype)
        sv_ref[0:1, :] = dg
        sv_ref[1:2, :] = db


def group_bias(size, places):
    i = lax.broadcasted_iota(jnp.int32, (size, size), 0)
    j = lax.broadcasted_iota(jnp.int32, (size, size), 1)
    return jnp.where(i % places == j % places, 0.0, -1e30).astype(F32)


def time_forward(width, heads, groups, size, places, core_ref, h_ref, w_ref, mask_ref, qkv_ref, ot_ref):
    qkv_ref[0] = dot(h_ref[...], w_ref[0, 0, :, : 3 * width]).astype(BF)
    bias = group_bias(size, places)

    def one(g, carry):
        r = pl.ds(pl.multiple_of(g * size, size), size)
        keep = mask_ref[r, :]
        for h in range(heads):
            a, b, c = (slice(j * width + h * HEAD, j * width + (h + 1) * HEAD) for j in range(3))
            s = dot(qkv_ref[0, r, a], qkv_ref[0, r, b], NT) * SCALE + bias
            o = dot(softmax(s).astype(BF), qkv_ref[0, r, c])
            ot_ref[0, r, a] = jnp.where(keep > 0, o, 0.0).astype(BF)
        return carry

    lax.fori_loop(0, groups, one, 0)


def time_backward(
    width, heads, groups, size, places, core_ref, h_ref, w_ref, mask_ref, qkv_ref, do_ref, gw_ref, dh_ref, dqkv_scr
):
    bias = group_bias(size, places)

    def one(g, carry):
        r = pl.ds(pl.multiple_of(g * size, size), size)
        keep = mask_ref[r, :]
        for h in range(heads):
            a, b, c = (slice(j * width + h * HEAD, j * width + (h + 1) * HEAD) for j in range(3))
            do = jnp.where(keep > 0, do_ref[0, r, a].astype(F32), 0.0).astype(BF)
            dq, dk, dv = attend_head_back(do, qkv_ref[0, r, a], qkv_ref[0, r, b], qkv_ref[0, r, c], bias)
            dqkv_scr[r, a] = dq
            dqkv_scr[r, b] = dk
            dqkv_scr[r, c] = dv
        return carry

    lax.fori_loop(0, groups, one, 0)
    dqkv = dqkv_scr[...]
    gw_ref[0] = dot(h_ref[...], dqkv, TN).astype(BF)
    dh = dot(dqkv, w_ref[0, 0, :, : 3 * width], NT)

    @pl.when(pl.program_id(0) == 0)
    def _():
        dh_ref[...] = dh

    @pl.when(pl.program_id(0) > 0)
    def _():
        dh_ref[...] += dh


def mlp_both(
    width, tensors,
    xs_ref, cot_ref, ot_ref, vec_ref, bin_ref, wt_ref, win_ref, wout_ref,
    res_ref, gt_ref, do_ref, gin_ref, gout_ref, gwt_ref, sv_ref, gb_ref,
    xt_scr, hm_scr, xm_scr, dhm_scr,
):
    t = pl.program_id(0)

    @pl.when(t == 0)
    def _():
        xt = xs_ref[...]
        for j in range(tensors):
            xt = xt + dot(ot_ref[j], wt_ref[0, j, :, 3 * width :], NT)
        xt_scr[...] = xt
        hm_scr[...] = norm(xt, vec_ref[4:5, :], vec_ref[5:6, :]).astype(BF)
        xm_scr[...] = xt + vec_ref[6:7, :]
        dhm_scr[...] = jnp.zeros_like(dhm_scr)

    hm = hm_scr[...]
    dz = cot_ref[...]
    win = win_ref[0, 0]
    wout = wout_ref[0, 0]
    pre = dot(hm, win) + bin_ref[pl.ds(t, 1), :]
    sq = pre * pre
    th = jnp.tanh(GELU_C * (pre + 0.044715 * (pre * sq)))
    hidden = (0.5 * pre * (1.0 + th)).astype(BF)
    xm_scr[...] += dot(hidden, wout, NT)
    slope = 0.5 * (1.0 + th) + 0.5 * pre * (1.0 - th * th) * (GELU_C * (1.0 + 0.134145 * sq))
    dpre = dot(dz, wout) * slope
    dpre_b = dpre.astype(BF)
    gb_ref[pl.ds(t, 1), :] = jnp.sum(dpre_b.astype(F32), axis=0, keepdims=True)
    gout_ref[0] = dot(dz, hidden, TN).astype(BF)
    gin_ref[0] = dot(hm, dpre_b, TN).astype(BF)
    dhm_scr[...] += dot(dpre_b, win, NT)

    @pl.when(t == pl.num_programs(0) - 1)
    def _():
        res_ref[...] = xm_scr[...].astype(BF)
        gm = dz.astype(F32)
        dx, dg, db = norm_back(xt_scr[...], vec_ref[4:5, :], dhm_scr[...])
        gt = gm + dx
        gt_ref[...] = gt
        dat = gt.astype(BF)
        for j in range(tensors):
            do_ref[j] = dot(dat, wt_ref[0, j, :, 3 * width :]).astype(BF)
            gwt_ref[j] = dot(dat, ot_ref[j], TN).astype(BF)
        sv_ref[...] = jnp.zeros_like(sv_ref)
        sv_ref[0:1, :] = dg
        sv_ref[1:2, :] = db
        sv_ref[2:3, :] = jnp.sum(gm, axis=0, keepdims=True)


def whole(shape):
    zero = (0,) * len(shape)
    return pl.BlockSpec(shape, lambda *_: zero)


def call(body, grid, ins, in_specs, outs, out_specs, scratch, prefetch=0, name=None):
    return pl.pallas_call(
        body,
        out_shape=tuple(jax.ShapeDtypeStruct(s, d) for s, d in outs),
        grid_spec=pltpu.PrefetchScalarGridSpec(
            num_scalar_prefetch=prefetch,
            grid=(grid,),
            in_specs=in_specs,
            out_specs=tuple(out_specs),
            scratch_shapes=scratch,
        ),
        compiler_params=pltpu.CompilerParams(
            dimension_semantics=("arbitrary",), vmem_limit_bytes=60 * 1024 * 1024
        ),
        name=name,
    )(*ins)


def swap_core(v):
    size = lax.axis_size("tensor")
    return lax.ppermute(v, "tensor", [(i, i ^ 1) for i in range(size)])


def shards(
    tokens, query_space, key_space, value_space, output_space, query_time, key_time, value_time,
    output_time, mlp_in, bias_in, mlp_out, bias_out, gain_first, shift_first, gain_second,
    shift_second, gain_third, shift_third, place_slot, cotangent,
):
    F = lax.axis_size("frame")
    T = lax.axis_size("tensor")
    clips, frames_dev, places_dev, D = tokens.shape
    width = query_space.shape[1]
    heads = width // HEAD
    hid = mlp_in.shape[1]
    rows_w = query_space.shape[0]
    fr = clips * frames_dev // T
    fp = frames_dev // fr
    R = fr * T * PAD
    f_id = lax.axis_index("frame")
    t_id = lax.axis_index("tensor")
    core = t_id % 2

    def pack(q, k, v, o):
        return jnp.concatenate((q, k, v, o.T), axis=1)

    wl = jnp.stack(
        (
            pack(query_space, key_space, value_space, output_space),
            pack(query_time, key_time, value_time, output_time),
            mlp_in,
            mlp_out.T,
        )
    )
    part_bin = lax.dynamic_slice(bias_in, (f_id * (hid // F),), (hid // F,)).astype(F32)
    part_bout = lax.dynamic_slice(
        bias_out, (t_id * (bias_out.shape[0] // T),), (bias_out.shape[0] // T,)
    ).astype(F32)
    small = jnp.concatenate(
        (gain_first, shift_first, gain_second, shift_second, gain_third, shift_third, part_bout, part_bin)
    )
    FT = ("frame", "tensor")
    small_all = lax.all_gather(small, FT, axis=0, tiled=False)
    nv = 7 * gain_first.shape[0]
    vec = small_all[:, :nv].reshape(F * T, 7, -1).transpose(1, 0, 2).reshape(7, D)
    vec = jnp.concatenate((vec, jnp.zeros((1, D), F32)), axis=0)
    bin_all = small_all[:, nv:].reshape(F, T, -1).transpose(1, 0, 2).reshape(T, hid)
    W = lax.all_gather(wl, FT, axis=0, tiled=False).reshape(F, T, 4, rows_w, D)
    W = W.transpose(2, 1, 0, 3, 4).reshape(4, T, F * rows_w, D)

    def to_owner(v):
        v = jnp.pad(v, ((0, 0), (0, 0), (0, PAD - places_dev), (0, 0)))
        v = v.reshape(T, fr, PAD, D)
        v = lax.all_to_all(v, "tensor", split_axis=0, concat_axis=0, tiled=True)
        return v.transpose(1, 0, 2, 3).reshape(R, D)

    def from_owner(v):
        v = v.reshape(fr, T, PAD, D).transpose(1, 0, 2, 3)
        v = lax.all_to_all(v, "tensor", split_axis=0, concat_axis=0, tiled=True)
        return v.reshape(clips, frames_dev, PAD, D)[:, :, :places_dev]

    x = to_owner(tokens)
    cot = to_owner(cotangent)
    keep = place_slot >= 0
    bias = jnp.where(keep, 0.0, -1e30).astype(F32).reshape(T, places_dev)
    bias = jnp.pad(bias, ((0, 0), (0, PAD - places_dev)), constant_values=-1e30).reshape(1, T * PAD)
    rows = T * PAD

    qkv_s, os_s, xs, ht = call(
        partial(space_forward, width, heads, fr, rows),
        T,
        (x, vec, bias, W),
        [whole((R, D)), whole((8, D)), whole((1, rows)), pl.BlockSpec((1, 1, D, D), lambda t: (0, t, 0, 0))],
        [((T, R, 3 * width), BF), ((T, R, width), BF), ((R, D), F32), ((R, D), BF)],
        [
            pl.BlockSpec((1, R, 3 * width), lambda t: (t, 0, 0)),
            pl.BlockSpec((1, R, width), lambda t: (t, 0, 0)),
            whole((R, D)),
            whole((R, D)),
        ],
        [pltpu.VMEM((R, D), BF)],
        name="space_forward",
    )

    groups = PAD // 8
    nf = 2 * F * fr
    size = nf * 8
    RT = groups * size

    def to_time(own):
        v = own.transpose(1, 0, 2, 3)
        return lax.all_to_all(v, "frame", split_axis=0, concat_axis=0, tiled=True)

    def group_rows(a, b):
        v = jnp.stack((a, b)).reshape(nf, groups, 8, a.shape[-1])
        return v.transpose(1, 0, 2, 3).reshape(RT, a.shape[-1])

    def ungroup_rows(v):
        n = v.shape[-1]
        return v.reshape(groups, nf, 8, n).transpose(1, 0, 2, 3).reshape(2, F, fr, PAD, n)

    def to_frames(v):
        v = lax.all_to_all(v, "frame", split_axis=0, concat_axis=0, tiled=True)
        return v.transpose(1, 0, 2, 3).reshape(R, v.shape[-1])

    h_own = to_time(ht.reshape(fr, T, PAD, D))
    h_t = group_rows(h_own, swap_core(h_own))
    keep_q = lax.dynamic_slice(
        jnp.pad(keep.astype(F32).reshape(T, places_dev), ((0, 0), (0, PAD - places_dev))), (f_id, 0), (1, PAD)
    )
    mask = jnp.broadcast_to(keep_q.reshape(groups, 1, 8), (groups, nf, 8)).reshape(RT, 1)
    core_arr = core.reshape(1).astype(jnp.int32)
    halves = T // 2
    time_w = pl.BlockSpec((1, 1, D, D), lambda i, c: (1, c[0] + 2 * i, 0, 0))
    per_half = lambda n: pl.BlockSpec((1, RT, n), lambda i, c: (i, 0, 0))
    qkv_t, ot = call(
        partial(time_forward, width, heads, groups, size, 8),
        halves,
        (core_arr, h_t, W, mask),
        [whole((RT, D)), time_w, whole((RT, 1))],
        [((halves, RT, 3 * width), BF), ((halves, RT, width), BF)],
        [per_half(3 * width), per_half(width)],
        [],
        prefetch=1,
        name="time_forward",
    )
    ot_u = jnp.stack([ungroup_rows(ot[i]) for i in range(halves)], axis=-2)
    ot_u = ot_u.reshape(2, F, fr, PAD, halves * width)
    ot_mine, ot_other = to_frames(ot_u[0]), to_frames(swap_core(ot_u[1]))

    def by_tensor(mine, other):
        m = mine.reshape(R, halves, width)
        o = other.reshape(R, halves, width)
        first = jnp.where(core == 0, m, o)
        second = jnp.where(core == 0, o, m)
        return jnp.stack((first, second), axis=2).reshape(R, T, width).transpose(1, 0, 2)

    ot_all = by_tensor(ot_mine, ot_other)
    win_spec = lambda kind: pl.BlockSpec((1, 1, D, D), lambda t: (kind, t, 0, 0))
    res, gt, dot_all, g_in, g_out, g_wt, sv_m, gb = call(
        partial(mlp_both, width, T),
        T,
        (xs, cot, ot_all, vec, bin_all, W, W, W),
        [
            whole((R, D)), whole((R, D)), whole((T, R, width)), whole((8, D)), whole((T, hid)),
            pl.BlockSpec((1, T, D, D), lambda t: (1, 0, 0, 0)), win_spec(2), win_spec(3),
        ],
        [
            ((R, D), BF), ((R, D), F32), ((T, R, width), BF), ((T, D, hid), BF), ((T, D, hid), BF),
            ((T, D, width), BF), ((8, D), F32), ((T, hid), F32),
        ],
        [
            whole((R, D)), whole((R, D)), whole((T, R, width)),
            pl.BlockSpec((1, D, hid), lambda t: (t, 0, 0)), pl.BlockSpec((1, D, hid), lambda t: (t, 0, 0)),
            whole((T, D, width)), whole((8, D)), whole((T, hid)),
        ],
        [pltpu.VMEM((R, D), F32), pltpu.VMEM((R, D), BF), pltpu.VMEM((R, D), F32), pltpu.VMEM((R, D), F32)],
        name="mlp_both",
    )
    d = dot_all.reshape(halves, 2, R, width)
    d_mine = jnp.where(core == 0, d[:, 0], d[:, 1])
    d_other = jnp.where(core == 0, d[:, 1], d[:, 0])
    as_frames = lambda v: v.transpose(1, 0, 2).reshape(fr, T, PAD, halves * width)
    d_own = to_time(as_frames(d_mine))
    d_par = to_time(swap_core(as_frames(d_other)))
    d_t = group_rows(d_own, d_par).reshape(RT, halves, width).transpose(1, 0, 2)
    g_time, dh_part = call(
        partial(time_backward, width, heads, groups, size, 8),
        halves,
        (core_arr, h_t, W, mask, qkv_t, d_t),
        [whole((RT, D)), time_w, whole((RT, 1)), per_half(3 * width), per_half(width)],
        [((halves, D, 3 * width), BF), ((RT, D), F32)],
        [pl.BlockSpec((1, D, 3 * width), lambda i, c: (i, 0, 0)), whole((RT, D))],
        [pltpu.VMEM((RT, 3 * width), BF)],
        prefetch=1,
        name="time_backward",
    )
    dh_u = ungroup_rows(dh_part)
    dh_sum = (dh_u[0] + swap_core(dh_u[1].astype(BF)).astype(F32)).astype(BF)
    dht = to_frames(dh_sum)

    gx, g_space, sv_s = call(
        partial(space_backward, width, heads, fr, rows),
        T,
        (x, xs, gt, dht, vec, bias, W, qkv_s, os_s),
        [
            whole((R, D)), whole((R, D)), whole((R, D)), whole((R, D)), whole((8, D)), whole((1, rows)),
            pl.BlockSpec((1, 1, D, D), lambda t: (0, t, 0, 0)),
            pl.BlockSpec((1, R, 3 * width), lambda t: (t, 0, 0)),
            pl.BlockSpec((1, R, width), lambda t: (t, 0, 0)),
        ],
        [((R, D), BF), ((T, D, D), BF), ((8, D), F32)],
        [whole((R, D)), pl.BlockSpec((1, D, D), lambda t: (t, 0, 0)), whole((8, D))],
        [
            pltpu.VMEM((R, D), BF), pltpu.VMEM((R, D), F32), pltpu.VMEM((R, D), BF), pltpu.VMEM((R, D), F32),
            pltpu.VMEM((R, 3 * width), BF),
        ],
        name="space_backward",
    )
    zero = jnp.zeros_like(g_time)
    g_first = jnp.where(core == 0, g_time, zero)
    g_second = jnp.where(core == 0, zero, g_time)
    g_qkv = jnp.stack((g_first, g_second), axis=1).reshape(T, D, 3 * width)
    part = jnp.stack((g_space, jnp.concatenate((g_qkv, g_wt), axis=2), g_in, g_out))
    part = part.reshape(4, T, F, rows_w, D).transpose(2, 1, 0, 3, 4).reshape(F * T, 4, rows_w, D)
    share = lax.psum_scatter(part, FT, scatter_dimension=0, tiled=False)
    share = lax.psum(share.astype(F32), "rep")
    smalls = jnp.concatenate((sv_s[0:4], sv_m[0:3], gb), axis=0)
    smalls = lax.psum(smalls, ("rep", "frame", "tensor"))

    def unpack(g):
        return g[:, :width], g[:, width : 2 * width], g[:, 2 * width : 3 * width], g[:, 3 * width :].T

    gs_q, gs_k, gs_v, gs_o = unpack(share[0])
    gt_q, gt_k, gt_v, gt_o = unpack(share[1])
    n = gain_first.shape[0]
    at = (f_id * T + t_id) * n
    own = lambda row: lax.dynamic_slice(smalls[row], (at,), (n,))
    nb = bias_out.shape[0]
    return (
        from_owner(res),
        from_owner(gx).astype(F32),
        gs_q, gs_k, gs_v, gs_o,
        gt_q, gt_k, gt_v, gt_o,
        share[2],
        lax.dynamic_slice(smalls, (7 + t_id, 0), (1, hid))[0],
        share[3].T,
        lax.dynamic_slice(smalls[6], (f_id * nb,), (nb,)),
        own(0), own(1), own(2), own(3), own(4), own(5),
    )


def solution(mesh):
    rows = P("rep", "frame", "tensor", None)
    ft, tf, vec = P("frame", "tensor"), P("tensor", "frame"), P(("frame", "tensor"))
    placed = (
        rows, ft, ft, ft, tf, ft, ft, ft, tf, ft, P("tensor"), tf, P("frame"),
        vec, vec, vec, vec, vec, vec, P(), rows,
    )
    return jax.shard_map(
        shards,
        mesh=mesh,
        in_specs=placed,
        out_specs=(
            rows, rows, ft, ft, ft, tf, ft, ft, ft, tf, ft, P("tensor"), tf, P("frame"),
            vec, vec, vec, vec, vec, vec,
        ),
        check_vma=False,
    )
```

time: 1720 us -> 698 us (0.41)
  waiting for transfers between devices: 921 us -> 269 us
  blocking collectives: 440 us -> 147 us
  Pallas kernels: 0 us -> 123 us
  matrix products: 100 us -> 0 us
  local copies, waits for them, and re-layouts: 154 us -> 66.6 us
  other arithmetic: 68.8 us -> 25.3 us
  starting transfers between devices: 5.32 us -> 39 us
    unnamed x37 -> x3, waiting for transfers between devices: 687 us -> 0.05 us
    all_gather x8 -> x0, blocking collectives: 135 us -> none  [the longest x2 45.6 us: fetch_attention(): lax.all_gather(output_w, 'frame', axis=1, tiled=True)]
    pallas_call x0 -> x5, Pallas kernels: none -> 123 us  [call(): pl.pallas_call(body, out_shape=tuple((jax.ShapeDtypeStruct(s, d) for s, d...]
    all_to_all x3 -> x2, blocking collectives: 150 us -> 35.9 us  [to_time(): return lax.all_to_all(v, 'frame', split_axis=0, concat_axis=0, tiled=True)]
    dot_general x32 -> x0, matrix products: 100 us -> none  [the longest x1 8.12 us: mlp_back(): jnp.einsum('cfpd,kd->cfpk', grad_all, weight_out, preferred_element_type=...]
    reduce_scatter x2 -> x1, waiting for transfers between devices: 97.1 us -> 193 us  [shards(): share = lax.psum_scatter(part, FT, scatter_dimension=0, tiled=False)]
    unnamed x4 -> x1, blocking collectives: 150 us -> 67.5 us
    all_gather x8 -> x1, waiting for transfers between devices: 108 us -> 29.4 us  [shards(): W = lax.all_gather(wl, FT, axis=0, tiled=False).reshape(F, T, 4, rows_w, D)]
  transfers between devices with their start and end apart: 25 -> 15, of which waited for: 20 -> 10; matrix products, arithmetic and copies ran while one was open for 7% -> 4% of each run, Pallas kernels for 0% -> 3%
where the time goes in v1:
time: 698 us; the launch traced here: 684 us
  waiting for transfers between devices  269 us (39%)
  blocking collectives  147 us (21%)
  Pallas kernels  123 us (18%)
  local copies, waits for them, and re-layouts  66.6 us (10%)
  starting transfers between devices  39 us (6%)
  other arithmetic  25.3 us (4%)
  between operations  15.2 us (2%)
    reduce_scatter x1, waiting for transfers between devices, shards(): share = lax.psum_scatter(part, FT, scatter_dimension=0, tiled=False)  193 us
    pallas_call x5, Pallas kernels, call(): pl.pallas_call(body, out_shape=tuple((jax.ShapeDtypeStruct(s, d) for s, d...  123 us
    unnamed x1, blocking collectives  67.5 us
    psum x1, blocking collectives, shards(): smalls = lax.psum(smalls, ('rep', 'frame', 'tensor'))  43.4 us
    all_to_all x2, blocking collectives, to_time(): return lax.all_to_all(v, 'frame', split_axis=0, concat_axis=0, tiled=True)  35.9 us
    all_gather x1, waiting for transfers between devices, shards(): W = lax.all_gather(wl, FT, axis=0, tiled=False).reshape(F, T, 4, rows_w, D)  29.4 us
    all_to_all x3, waiting for transfers between devices, to_frames(): v = lax.all_to_all(v, 'frame', split_axis=0, concat_axis=0, tiled=True)  23.8 us
    reshape x1, local copies, waits for them, and re-layouts, shards(): W = lax.all_gather(wl, FT, axis=0, tiled=False).reshape(F, T, 4, rows_w, D)  17.3 us
  transfers between devices with their start and end apart: 15, of which 10 were waited for; matrix products, arithmetic and copies ran while one was open for 4% of the time, Pallas kernels for 3%

profile of v1, /device:TPU:0, one launch (start us, length us, event | category | flops | bytes accessed | tf_op | source)
XLA Modules:
  0.0 684.3 jit_solution(15832008607931760225)
XLA Ops:
  10.7 2.2 pad_maximum_fusion.2
  14.0 4.3 all-to-all-start
  21.5 67.5 %all-reduce.5 = f32[8448]{0:T(1024)S(1)} all-reduce(f32[8448]{0:T(1024)S(1)} %dynamic-update-slice), channel_id=2, replica_groups=mesh['rep'=2,'frame'=4,'tensor'=4] {'frame','tensor'}, use_global_device_ids=true, to_apply=%add.5 | all-reduce | flops 8448 | bytes 67584
  90.9 29.4 %all-gather.4.cloned.1.call-done = bf16[64,192,768]{2,1,0:T(8,128)(2,1)} async-done(((bf16[4,192,768]{2,1,0:T(8,128)(2,1)}), bf16[64,192,768]{2,1,0:T(8,128)(2,1)}) %all-gather.4.cloned.1.call-update) | async-done | bytes 18874384 | tf_op jit(solution)/shard_map/all_gather | solution.py:320
  120.3 17.3 %copy.117 = bf16[4,4,4,192,768]{4,3,0,1,2:T(8,128)(2,1)} copy(bf16[4,4,4,192,768]{4,3,2,1,0:T(8,128)(2,1)} %bitcast.143) | data formatting | bytes 37748736 | tf_op jit(solution)/shard_map/reshape | solution.py:320
  137.6 13.6 %space_forward.1 = (bf16[4,448,576]{2,1,0:T(8,128)(2,1)}, bf16[4,448,192]{2,1,0:T(8,128)(2,1)}, f32[448,768]{1,0:T(8,128)}, bf16[448,768]{1,0:T(8,128)(2,1)}) custom-call(bf16[448,768]{1,0:T(8,128)(2,1)} %bitcast.149, f32[8,768]{1,0:T(8,128)} %concatenate.25.vec_ref, f32[1,224]{1,0:T(1,128)} %reshape.213.bias_ref, bf16[4,4,768,768]{3,2,1,0:T(8,128)(2,1)} %bitcast.135), custom_call_target="tpu_custom_call" | custom-call | tf_op jit(solution)/shard_map/space_forward/pallas_call | solution.py:255
  152.5 23.9 %all_to_all.50 = bf16[4,2,56,768]{3,2,1,0:T(8,128)(2,1)S(1)} all-to-all(bf16[4,2,56,768]{3,2,1,0:T(8,128)(2,1)S(1)} %bitcast.167), channel_id=1, replica_groups=mesh['rep'=2,'frame'=4,'tensor'=4] {'frame'}, dimensions={0} | all-to-all | bytes 1376256 | tf_op jit(solution)/shard_map/all_to_all | solution.py:364
  177.4 3.5 all-to-all-start.1
  183.4 22.3 %time_forward.1 = (bf16[2,896,576]{2,1,0:T(8,128)(2,1)}, bf16[2,896,192]{2,1,0:T(8,128)(2,1)}) custom-call(s32[1]{0:T(128)} %bitcast.18.core_ref, bf16[896,768]{1,0:T(8,128)(2,1)} %bitcast.145, bf16[4,4,768,768]{3,2,1,0:T(8,128)(2,1)} %bitcast.136, f32[896,1]{1,0:T(8,128)} %reshape.247.mask_ref), custom_call_target="tpu_custom_call" | custom-call | tf_op jit(solution)/shard_map/time_forward/pallas_call | solution.py:255
  208.6 3.5 all-to-all-start.3
  214.8 8.8 %all-to-all-done.3 = bf16[4,2,56,384]{3,2,1,0:T(8,128)(2,1)S(1)} async-done(((bf16[4,2,56,384]{3,2,1,0:T(8,128)(2,1)}), bf16[4,2,56,384]{3,2,1,0:T(8,128)(2,1)S(1)}, u32[]{:S(2)}, u32[]{:S(2)}) %all-to-all-start.3) | async-done | bytes 344096 | tf_op jit(solution)/shard_map/all_to_all | solution.py:375
  223.6 3.7 all-to-all-start.4
  229.0 9.0 %all-to-all-done.4 = bf16[4,2,56,384]{3,2,1,0:T(8,128)(2,1)S(1)} async-done(((bf16[4,2,56,384]{3,2,1,0:T(8,128)(2,1)}), bf16[4,2,56,384]{3,2,1,0:T(8,128)(2,1)S(1)}, u32[]{:S(2)}, u32[]{:S(2)}) %all-to-all-start.4) | async-done | bytes 344096 | tf_op jit(solution)/shard_map/all_to_all | solution.py:375
  241.3 26.8 %mlp_both.1 = (bf16[448,768]{1,0:T(8,128)(2,1)}, f32[448,768]{1,0:T(8,128)}, bf16[4,448,192]{2,1,0:T(8,128)(2,1)}, bf16[4,768,768]{2,1,0:T(8,128)(2,1)}, bf16[4,...) custom-call(f32[448,768]{1,0:T(8,128)} %get-tuple-element.39.xs_ref, ...), custom_call_target="tpu_custom_call" | custom-call | tf_op jit(solution)/shard_map/mlp_both/pallas_call | solution.py:255
  271.4 3.5 all-to-all-start.6
  276.9 6.9 %all-to-all-done.6 = bf16[4,2,56,384]{3,2,1,0:T(8,128)(2,1)S(1)} async-done(((bf16[4,2,56,384]{3,2,1,0:T(8,128)(2,1)}), bf16[4,2,56,384]{3,2,1,0:T(8,128)(2,1)S(1)}, u32[]{:S(2)}, u32[]{:S(2)}) %all-to-all-start.6) | async-done | bytes 344096 | tf_op jit(solution)/shard_map/all_to_all | solution.py:364
  283.8 11.9 %all_to_all.51 = bf16[4,2,56,384]{3,2,1,0:T(8,128)(2,1)S(1)} all-to-all(bf16[4,2,56,384]{3,2,1,0:T(8,128)(2,1)S(1)} %copy.135), channel_id=1, replica_groups=mesh['rep'=2,'frame'=4,'tensor'=4] {'frame'}, dimensions={0} | all-to-all | bytes 688128 | tf_op jit(solution)/shard_map/all_to_all | solution.py:364
  297.4 31.4 %time_backward.1 = (bf16[2,768,576]{2,1,0:T(8,128)(2,1)}, f32[896,768]{1,0:T(8,128)}) custom-call(s32[1]{0:T(128)} %bitcast.18.core_ref, bf16[896,768]{1,0:T(8,128)(2,1)} %bitcast.146, bf16[4,4,768,768]{3,2,1,0:T(8,128)(2,1)} %bitcast.140, f32[896,1]{1,0:T(8,128)} %reshape.247.mask_ref, bf16[2,896,576]{2,1,0:T(8,128)(2,1)} %get-tuple-element.44.qkv_ref, ...), custom_call_target="tpu_custom_call" | custom-call | tf_op jit(solution)/shard_map/time_backward/pallas_call | solution.py:255
  334.1 3.5 all-to-all-start.8
  337.6 9.4 %reduce-scatter.2.cloned.1.call-start = ((), (), s32[]{:S(2)}) async-start(), calls=%async_computation.11 | async-start | bytes 20054016 | tf_op jit(solution)/shard_map/reduce_scatter | solution.py:478
  348.0 2.2 copy.142
  350.2 5.9 all-to-all-done.8
  357.0 28.4 %space_backward.1 = (bf16[448,768]{1,0:T(8,128)(2,1)}, bf16[4,768,768]{2,1,0:T(8,128)(2,1)}, f32[8,768]{1,0:T(8,128)}) custom-call(bf16[448,768]{1,0:T(8,128)(2,1)} %bitcast.150, f32[448,768]{1,0:T(8,128)} %get-tuple-element.39.xs_ref, f32[448,768]{1,0:T(8,128)} %get-tuple-element.43.gt_ref, bf16[448,768]{1,0:T(8,128)(2,1)} %bitcast.158, ...), custom_call_target="tpu_custom_call" | custom-call | tf_op jit(solution)/shard_map/space_backward/pallas_call | solution.py:255
  385.5 12.8 %maximum_bitcast_fusion = bf16[4,4,4,192,768]{4,3,0,1,2:T(8,128)(2,1)S(1)} fusion(bf16[1,4,4,192,768]{4,3,2,1,0:T(8,128)(2,1)} %bitcast.154, bf16[1,4,4,192,768]{4,3,2,1,0:T(8,128)(2,1)} %bitcast.153, bf16[1,4,4,192,192]{4,3,2,1,0:T(8,128)(2,1)} %bitcast.173, bf16[1,4,4,192,576]{4,3,2,1,0:T(8,128)(2,1)S(1)} %bitcast.144, bf16[1,4,4,192,768]{4,3,2,1,0:T(8,128)(2,1)} %bitcast.155), kind=kLoop, calls=%fused_computation | loop fusion | flops 94371840 | bytes 37748736 | tf_op jit(solution)/shard_map/transpose | solution.py:477
  398.2 6.9 %copy.143 = bf16[4,4,4,192,768]{4,3,2,1,0:T(8,128)(2,1)} copy(bf16[4,4,4,192,768]{4,3,0,1,2:T(8,128)(2,1)S(1)} %maximum_bitcast_fusion) | data formatting | bytes 37748736 | tf_op jit(solution)/shard_map/transpose | solution.py:477
  405.2 193.0 %reduce-scatter.2.cloned.1.call-done = bf16[1,4,192,768]{3,2,1,0:T(8,128)(2,1)} async-done(((bf16[16,4,192,768]{3,2,1,0:T(8,128)(2,1)}), bf16[1,4,192,768]{3,2,1,0:T(8,128)(2,1)}) %reduce-scatter.2.cloned.1.call-update) | async-done | bytes 1179664 | tf_op jit(solution)/shard_map/reduce_scatter | solution.py:478
  598.2 2.9 bitcast_convert_fusion
  602.1 3.5 all-to-all-start.5
  605.6 10.5 %all-to-all-done.5 = bf16[4,2,56,768]{3,2,1,0:T(8,128)(2,1)S(1)} async-done(((bf16[4,2,56,768]{3,2,1,0:T(8,128)(2,1)}), bf16[4,2,56,768]{3,2,1,0:T(8,128)(2,1)S(1)}, u32[]{:S(2)}, u32[]{:S(2)}) %all-to-all-start.5) | async-done | bytes 688160 | tf_op jit(solution)/shard_map/all_to_all | solution.py:331
  618.1 3.5 all-to-all-start.9
  621.6 43.4 %psum.15 = f32[11,768]{1,0:T(8,128)S(1)} all-reduce(f32[11,768]{1,0:T(8,128)S(1)} %pad_maximum_fusion.6), channel_id=1, replica_groups=mesh['rep'=2,'frame'=4,'tensor'=4] {'rep','frame','tensor'}, use_global_device_ids=true, to_apply=%region_2.3 | all-reduce | flops 8448 | bytes 67584 | tf_op jit(solution)/shard_map/psum | solution.py:481
  671.4 2.8 slice_bitcast_fusion
  (143 shorter events, 50.7 us)
Async XLA Ops:
  7.2 113.1 %all-gather.4.cloned.1.call-start = ((), (), s32[]{:S(2)}) async-start(), calls=%async_computation.13 | async-start | bytes 20054016 | tf_op jit(solution)/shard_map/all_gather | solution.py:320
  12.9 5.4 copy-start.9
  12.9 6.1 copy-start.17
  12.9 7.3 %copy-start.16 = (bf16[192]{0:T(256)(128)(2,1)S(1)}, bf16[192]{0:T(256)(128)(2,1)}, u32[]{:S(2)}) copy-start(bf16[192]{0:T(256)(128)(2,1)} %param.33) | copy-start | bytes 1156
  12.9 8.2 %copy-start.10 = (f32[48]{0:T(128)S(1)}, f32[48]{0:T(128)}, u32[]{:S(2)}) copy-start(f32[48]{0:T(128)} %param.34) | copy-start | bytes 580
  12.9 8.2 %copy-start.11 = (f32[48]{0:T(128)S(1)}, f32[48]{0:T(128)}, u32[]{:S(2)}) copy-start(f32[48]{0:T(128)} %param.35) | copy-start | bytes 580
  12.9 8.2 %copy-start.12 = (f32[48]{0:T(128)S(1)}, f32[48]{0:T(128)}, u32[]{:S(2)}) copy-start(f32[48]{0:T(128)} %param.36) | copy-start | bytes 580
  12.9 8.2 %copy-start.13 = (f32[48]{0:T(128)S(1)}, f32[48]{0:T(128)}, u32[]{:S(2)}) copy-start(f32[48]{0:T(128)} %param.37) | copy-start | bytes 580
  13.0 8.2 %copy-start.14 = (f32[48]{0:T(128)S(1)}, f32[48]{0:T(128)}, u32[]{:S(2)}) copy-start(f32[48]{0:T(128)} %param.38) | copy-start | bytes 580
  13.0 8.2 %copy-start.15 = (f32[48]{0:T(128)S(1)}, f32[48]{0:T(128)}, u32[]{:S(2)}) copy-start(f32[48]{0:T(128)} %param.39) | copy-start | bytes 580
  14.0 76.0 %all-to-all-start = ((bf16[4,2,56,768]{3,2,1,0:T(8,128)(2,1)}), bf16[4,2,56,768]{3,2,1,0:T(8,128)(2,1)S(1)}, u32[]{:S(2)}, u32[]{:S(2)}) async-start(bf16[4,2,56,768]{3,2,1,0:T(8,128)(2,1)} %bitcast), calls=%async_computation | async-start | bytes 1376256 | tf_op jit(solution)/shard_map/all_to_all | solution.py:326
  151.2 25.2 %copy-start.5 = (bf16[2,4,49,768]{3,1,2,0:T(4,128)(2,1)S(1)}, bf16[2,4,49,768]{3,1,2,0:T(4,128)(2,1)}, u32[]{:S(2)}) copy-start(bf16[2,4,49,768]{3,1,2,0:T(4,128)(2,1)} %param.41) | copy-start | bytes 1806340
  176.4 5.6 collective-permute-start
  177.4 31.3 %all-to-all-start.1 = ((bf16[4,2,56,768]{3,2,1,0:T(8,128)(2,1)}), bf16[4,2,56,768]{3,2,1,0:T(8,128)(2,1)S(1)}, u32[]{:S(2)}, u32[]{:S(2)}) async-start(bf16[4,2,56,768]{3,2,1,0:T(8,128)(2,1)} %bitcast.15), calls=%async_computation.1 | async-start | bytes 1376256 | tf_op jit(solution)/shard_map/all_to_all | solution.py:326
  208.6 15.0 %all-to-all-start.3 = ((bf16[4,2,56,384]{3,2,1,0:T(8,128)(2,1)}), bf16[4,2,56,384]{3,2,1,0:T(8,128)(2,1)S(1)}, u32[]{:S(2)}, u32[]{:S(2)}) async-start(bf16[4,2,56,384]{3,2,1,0:T(8,128)(2,1)} %squeeze.16), calls=%async_computation.3 | async-start | bytes 688128 | tf_op jit(solution)/shard_map/all_to_all | solution.py:375
  212.8 2.0 collective-permute-start.1
  223.6 14.4 %all-to-all-start.4 = ((bf16[4,2,56,384]{3,2,1,0:T(8,128)(2,1)}), bf16[4,2,56,384]{3,2,1,0:T(8,128)(2,1)S(1)}, u32[]{:S(2)}, u32[]{:S(2)}) async-start(bf16[4,2,56,384]{3,2,1,0:T(8,128)(2,1)} %collective-permute-done.1), calls=%async_computation.4 | async-start | bytes 688128 | tf_op jit(solution)/shard_map/all_to_all | solution.py:375
  271.4 12.4 %all-to-all-start.6 = ((bf16[4,2,56,384]{3,2,1,0:T(8,128)(2,1)}), bf16[4,2,56,384]{3,2,1,0:T(8,128)(2,1)S(1)}, u32[]{:S(2)}, u32[]{:S(2)}) async-start(bf16[4,2,56,384]{3,2,1,0:T(8,128)(2,1)} %copy.134), calls=%async_computation.6 | async-start | bytes 688128 | tf_op jit(solution)/shard_map/all_to_all | solution.py:364
  275.1 1.7 collective-permute-start.2
  330.9 2.2 collective-permute-start.3
  331.0 16.0 %copy-start.1 = (bf16[2,768,576]{2,1,0:T(8,128)(2,1)S(1)}, bf16[2,768,576]{2,1,0:T(8,128)(2,1)}, u32[]{:S(2)}) copy-start(bf16[2,768,576]{2,1,0:T(8,128)(2,1)} %get-tuple-element.51) | copy-start | bytes 5308420
  334.1 22.0 %all-to-all-start.8 = ((bf16[4,2,56,768]{3,2,1,0:T(8,128)(2,1)}), bf16[4,2,56,768]{3,2,1,0:T(8,128)(2,1)S(1)}, u32[]{:S(2)}, u32[]{:S(2)}) async-start(bf16[4,2,56,768]{3,2,1,0:T(8,128)(2,1)} %add_convert_fusion), calls=%async_computation.8 | async-start | bytes 1376256 | tf_op jit(solution)/shard_map/all_to_all | solution.py:375
  337.6 260.6 %reduce-scatter.2.cloned.1.call-start = ((), (), s32[]{:S(2)}) async-start(), calls=%async_computation.11 | async-start | bytes 20054016 | tf_op jit(solution)/shard_map/reduce_scatter | solution.py:478
  357.0 28.4 %copy-start = (bf16[2,2,768,576]{3,2,1,0:T(8,128)(2,1)S(1)}, bf16[2,2,768,576]{3,2,1,0:T(8,128)(2,1)}, u32[]{:S(2)}) copy-start(bf16[2,2,768,576]{3,2,1,0:T(8,128)(2,1)} %copy.142) | copy-start | bytes 10616836
  405.2 196.0 %copy-start.2 = (bf16[448,768]{1,0:T(8,128)(2,1)S(1)}, bf16[448,768]{1,0:T(8,128)(2,1)}, u32[]{:S(2)}) copy-start(bf16[448,768]{1,0:T(8,128)(2,1)} %get-tuple-element.42) | copy-start | bytes 2064388
  405.2 266.3 %all-reduce.8.cloned.1.call-start = ((), (), s32[]{:S(2)}) async-start(), calls=%async_computation.12 | async-start | bytes 4718592 | tf_op jit(solution)/shard_map/psum | solution.py:479
  601.2 4.5 copy-start.7
  601.2 16.0 %copy-start.3 = (bf16[448,768]{1,0:T(8,128)(2,1)S(1)}, bf16[448,768]{1,0:T(8,128)(2,1)}, u32[]{:S(2)}) copy-start(bf16[448,768]{1,0:T(8,128)(2,1)} %get-tuple-element.49) | copy-start | bytes 2064388
  602.1 14.0 %all-to-all-start.5 = ((bf16[4,2,56,768]{3,2,1,0:T(8,128)(2,1)}), bf16[4,2,56,768]{3,2,1,0:T(8,128)(2,1)S(1)}, u32[]{:S(2)}, u32[]{:S(2)}) async-start(bf16[4,2,56,768]{3,2,1,0:T(8,128)(2,1)} %bitcast.132), calls=%async_computation.5 | async-start | bytes 1376256 | tf_op jit(solution)/shard_map/all_to_all | solution.py:331
  605.6 16.0 %copy-start.8 = (f32[8,768]{1,0:T(8,128)S(1)}, f32[8,768]{1,0:T(8,128)}, u32[]{:S(2)}) copy-start(f32[8,768]{1,0:T(8,128)} %get-tuple-element.55) | copy-start | bytes 73732
  605.6 16.0 %copy-start.6 = (f32[4,768]{1,0:T(4,128)S(1)}, f32[4,768]{1,0:T(4,128)}, u32[]{:S(2)}) copy-start(f32[4,768]{1,0:T(4,128)} %get-tuple-element.57) | copy-start | bytes 36868
  618.1 51.8 %all-to-all-start.9 = ((bf16[4,2,56,768]{3,2,1,0:T(8,128)(2,1)}), bf16[4,2,56,768]{3,2,1,0:T(8,128)(2,1)S(1)}, u32[]{:S(2)}, u32[]{:S(2)}) async-start(bf16[4,2,56,768]{3,2,1,0:T(8,128)(2,1)} %bitcast.131), calls=%async_computation.9 | async-start | bytes 1376256 | tf_op jit(solution)/shard_map/all_to_all | solution.py:331
  (1 other events, 3.8 us)
Sparse Core Ops, SparseCore 0:
  13.1 107.1 all-gather.3
  405.3 192.8 reduce-scatter.1
  601.3 68.9 all-reduce.7

commit v2 on v1

--- a/solution.py
+++ b/solution.py
@@ -15,6 +15,9 @@
 TN = (((0,), (0,)), ((), ()))
 GELU_C = 0.7978845608028654
 SCALE = HEAD ** (-0.5)
+MESH = pl.DeviceIdType.MESH
+KS = 2
+SPLIT = 2
 
 
 def dot(a, b, dims=(((1,), (0,)), ((), ()))):
@@ -267,6 +270,450 @@
         ),
         name=name,
     )(*ins)
+
+
+def row_views(refs, outs, to_owner, n, mine, theirs):
+    if to_owner:
+        return refs[n].at[theirs], outs[n].at[:, mine]
+    return refs[n].at[:, theirs], outs[n].at[mine]
+
+
+def rows_start(T, t, rc, refs, outs, to_owner, rs, rr, rl):
+    for n in range(len(refs)):
+        for p in range(1, T):
+            src, dst = row_views(refs, outs, to_owner, n, t, t ^ p)
+            rc(src, dst, rs.at[n, p], rr.at[n, p], tensor=t ^ p).start()
+        src, dst = row_views(refs, outs, to_owner, n, t, t)
+        pltpu.make_async_copy(src, dst, rl.at[n]).start()
+
+
+def rows_wait(T, t, rc, refs, outs, to_owner, rs, rr, rl):
+    for n in range(len(refs)):
+        for p in range(1, T):
+            src, _ = row_views(refs, outs, to_owner, n, t, t ^ p)
+            _, dst = row_views(refs, outs, to_owner, n, t ^ p, t)
+            c = rc(src, dst, rs.at[n, p], rr.at[n, p], tensor=t ^ p)
+            c.wait_send()
+            c.wait_recv()
+        src, dst = row_views(refs, outs, to_owner, n, t, t)
+        pltpu.make_async_copy(src, dst, rl.at[n]).wait()
+
+
+def gather_kernel(F, T, K, KS, w_ref, s_ref, a_ref, b_ref, W_ref, S_ref, ao_ref, bo_ref, loc_sem, zs, zr, ys, yr, xs, xr, cs, cr, ss, sr, rs, rr, rl):
+    r, f, t = lax.axis_index("rep"), lax.axis_index("frame"), lax.axis_index("tensor")
+    rows = w_ref.shape[1]
+    half = rows // 2
+    core, ypart, xpart = t ^ 1, t ^ 2, r ^ 1
+    mine = pl.ds(pl.multiple_of((r % 2) * half, half), half)
+    other = pl.ds(pl.multiple_of((1 - r % 2) * half, half), half)
+
+    def rc(src, dst, ssem, rsem, **dev):
+        return pltpu.make_async_remote_copy(src, dst, ssem, rsem, device_id=dev, device_id_type=MESH)
+
+    bar = pltpu.get_barrier_semaphore()
+    for d in range(1, F):
+        for peer in (f - d, f + d):
+            @pl.when((peer >= 0) & (peer < F))
+            def _():
+                pl.semaphore_signal(bar, inc=1, device_id={"frame": peer}, device_id_type=MESH)
+    pl.semaphore_signal(bar, inc=1, device_id={"tensor": core}, device_id_type=MESH)
+    pl.semaphore_signal(bar, inc=1, device_id={"tensor": ypart}, device_id_type=MESH)
+    pl.semaphore_signal(bar, inc=1, device_id={"tensor": t ^ 3}, device_id_type=MESH)
+    pl.semaphore_signal(bar, inc=1, device_id={"rep": xpart}, device_id_type=MESH)
+    pl.semaphore_wait(bar, F + 3)
+
+    def blk(k, tt, src, part=None):
+        return W_ref.at[k, tt, src] if part is None else W_ref.at[k, tt, src, part]
+
+    def zpart(k):
+        return None if k < KS else mine
+
+    def z_copy(k, src, to):
+        ref = blk(k, t, src, zpart(k))
+        return rc(ref, ref, zs.at[k, src, jnp.where(to > f, 1, 0)], zr.at[k, src], frame=to)
+
+    def z_own(k, to):
+        s = w_ref.at[k] if k < KS else w_ref.at[k, mine]
+        return rc(s, blk(k, t, f, zpart(k)), zs.at[k, f, jnp.where(to > f, 1, 0)], zr.at[k, f], frame=to)
+
+    def y_copy(k, src, own):
+        s = w_ref.at[k, mine] if own else W_ref.at[k, t, src, mine]
+        return rc(s, W_ref.at[k, t, src, mine], ys.at[k, src], yr.at[k, src], tensor=ypart)
+
+    def y_in(k, src):
+        ref = W_ref.at[k, ypart, src, mine]
+        return rc(ref, ref, ys.at[k, src], yr.at[k, src], tensor=ypart)
+
+    def x_copy(k, src, part):
+        ref = W_ref.at[k, ypart, src, part]
+        return rc(ref, ref, xs.at[k, src], xr.at[k, src], rep=xpart)
+
+    def xo_copy(k, src, part):
+        ref = W_ref.at[k, t, src, part]
+        return rc(ref, ref, xs.at[K + k, src], xr.at[K + k, src], rep=xpart)
+
+    def c_copy(j, k, src, tt, own=False):
+        if j >= 3:
+            dst = W_ref.at[k, tt, src, mine if j == 3 else other]
+            return rc(dst, dst, cs.at[j, k, src], cr.at[j, k, src], tensor=core)
+        if j == 0:
+            dst = W_ref.at[k, tt, src]
+            return rc(w_ref.at[k] if own else dst, dst, cs.at[0, k, src], cr.at[0, k, src], tensor=core)
+        part = mine if j == 1 else other
+        dst = W_ref.at[k, tt, src, part]
+        return rc(dst, dst, cs.at[j, k, src], cr.at[j, k, src], tensor=core)
+
+    def small(i, dst, src, **dev):
+        return rc(src, dst, ss.at[i], sr.at[i], **dev)
+
+    def each(d, fn):
+        if d == 0:
+            fn(f, 0)
+        else:
+            for sign in (-1, 1):
+                src = f + sign * d
+                @pl.when((src >= 0) & (src < F))
+                def _():
+                    fn(src, sign)
+
+    for k in range(K):
+        for to in (f - 1, f + 1):
+            @pl.when((to >= 0) & (to < F))
+            def _():
+                z_own(k, to).start()
+        y_copy(k, f, True).start()
+    for k in range(K):
+        c_copy(0, k, f, t, own=True).start()
+        pltpu.make_async_copy(w_ref.at[k], W_ref.at[k, t, f], loc_sem.at[k]).start()
+    for d in range(1, F):
+        for sign in (-1, 1):
+            to = f + sign * d
+            @pl.when((to >= 0) & (to < F))
+            def _():
+                rc(s_ref, S_ref.at[t, f], ss.at[to], sr.at[f], frame=to).start()
+    pltpu.make_async_copy(s_ref, S_ref.at[t, f], loc_sem.at[K]).start()
+    pltpu.make_async_copy(s_ref, S_ref.at[t, f], loc_sem.at[K]).wait()
+
+    def z_step(k, d):
+        def fn(src, sign):
+            z_copy(k, src, f).wait_recv()
+            to = f - sign
+            @pl.when((to >= 0) & (to < F))
+            def _():
+                z_copy(k, src, to).start()
+            y_copy(k, src, False).start()
+            if k < KS:
+                c_copy(0, k, src, t).start()
+            else:
+                xo_copy(k, src, mine).start()
+                c_copy(3, k, src, t).start()
+        each(d, fn)
+
+    def y_step(k, d):
+        def fn(src, sign):
+            y_in(k, src).wait_recv()
+            x_copy(k, src, mine).start()
+            c_copy(1, k, src, ypart).start()
+        each(d, fn)
+
+    def x_step(k, d):
+        def fn(src, sign):
+            x_copy(k, src, other).wait_recv()
+            c_copy(2, k, src, ypart).start()
+            if k >= KS and sign != 0:
+                xo_copy(k, src, other).wait_recv()
+                c_copy(4, k, src, t).start()
+        each(d, fn)
+
+    for d in range(F):
+        for k in range(K):
+            if d > 0:
+                z_step(k, d)
+            y_step(k, d)
+            if d > 0:
+                x_step(k, d - 1)
+        if d == 1:
+            rows_start(T, t, rc, (a_ref, b_ref), (ao_ref, bo_ref), True, rs, rr, rl)
+            for dd in range(1, F):
+                def fn(src, sign):
+                    rc(s_ref, S_ref.at[t, src], ss.at[src], sr.at[src], frame=f).wait_recv()
+                each(dd, fn)
+            rc(S_ref.at[t], S_ref.at[t], ss.at[F], sr.at[F], tensor=ypart).start()
+        if d == 2:
+            rc(S_ref.at[ypart], S_ref.at[ypart], ss.at[F], sr.at[F], tensor=ypart).wait_recv()
+            rc(S_ref.at[t], S_ref.at[t], ss.at[F + 1], sr.at[F + 1], tensor=core).start()
+            rc(S_ref.at[ypart], S_ref.at[ypart], ss.at[F + 2], sr.at[F + 2], tensor=core).start()
+    for k in range(K):
+        x_step(k, F - 1)
+    rows_wait(T, t, rc, (a_ref, b_ref), (ao_ref, bo_ref), True, rs, rr, rl)
+    ct, cy = core, core ^ 2
+    for k in range(K):
+        pltpu.make_async_copy(w_ref.at[k], W_ref.at[k, t, f], loc_sem.at[k]).wait()
+        for d in range(F):
+            def fn(src, sign):
+                if k < KS or sign == 0:
+                    c_copy(0, k, src, ct).wait_recv()
+                    c_copy(0, k, src, t).wait_send()
+                else:
+                    for j in (3, 4):
+                        c_copy(j, k, src, ct).wait_recv()
+                        c_copy(j, k, src, t).wait_send()
+                    xo_copy(k, src, mine).wait_send()
+                c_copy(1, k, src, cy).wait_recv()
+                c_copy(2, k, src, cy).wait_recv()
+                c_copy(1, k, src, ypart).wait_send()
+                c_copy(2, k, src, ypart).wait_send()
+                y_copy(k, src, False).wait_send()
+                x_copy(k, src, mine).wait_send()
+                if sign == 0:
+                    for to in (f - 1, f + 1):
+                        @pl.when((to >= 0) & (to < F))
+                        def _():
+                            z_own(k, to).wait_send()
+                else:
+                    to = f - sign
+                    @pl.when((to >= 0) & (to < F))
+                    def _():
+                        z_copy(k, src, to).wait_send()
+            each(d, fn)
+    for dd in range(1, F):
+        def fn(src, sign):
+            rc(s_ref, S_ref.at[t, f], ss.at[src], sr.at[f], frame=src).wait_send()
+        each(dd, fn)
+    rc(S_ref.at[t], S_ref.at[t], ss.at[F], sr.at[F], tensor=ypart).wait_send()
+    rc(S_ref.at[t], S_ref.at[t], ss.at[F + 1], sr.at[F + 1], tensor=core).wait_send()
+    rc(S_ref.at[ypart], S_ref.at[ypart], ss.at[F + 2], sr.at[F + 2], tensor=core).wait_send()
+    rc(S_ref.at[ct], S_ref.at[ct], ss.at[F + 1], sr.at[F + 1], tensor=core).wait_recv()
+    rc(S_ref.at[cy], S_ref.at[cy], ss.at[F + 2], sr.at[F + 2], tensor=core).wait_recv()
+
+
+def gather_all(wl, small, a, b):
+    F, T = lax.axis_size("frame"), lax.axis_size("tensor")
+    K, rows, D = wl.shape
+    dma = pltpu.SemaphoreType.DMA
+    any_spec = pl.BlockSpec(memory_space=pl.ANY)
+    owned = (a.shape[1], a.shape[0]) + a.shape[2:]
+    sds = jax.ShapeDtypeStruct
+    return pl.pallas_call(
+        partial(gather_kernel, F, T, K, KS),
+        out_shape=(
+            sds((K, T, F, rows, D), wl.dtype), sds((T, F) + small.shape, small.dtype),
+            sds(owned, a.dtype), sds(owned, b.dtype),
+        ),
+        in_specs=[pl.BlockSpec(memory_space=pltpu.VMEM)] * 4,
+        out_specs=(any_spec,) * 4,
+        scratch_shapes=[
+            dma((K + 1,)), dma((K, F, 2)), dma((K, F)), dma((K, F)), dma((K, F)), dma((2 * K, F)), dma((2 * K, F)),
+            dma((5, K, F)), dma((5, K, F)), dma((F + 3,)), dma((F + 3,)), dma((2, T)), dma((2, T)), dma((2,)),
+        ],
+        compiler_params=pltpu.CompilerParams(collective_id=0, has_side_effects=True, vmem_limit_bytes=16 * 1024 * 1024),
+        name="gather_all",
+    )(wl, small, a, b)
+
+
+def reduce_kernel(F, T, G, split, *refs):
+    g_refs, s_ref, a_ref, b_ref = refs[:G], *refs[G : G + 3]
+    out_ref, sout_ref, ao_ref, bo_ref = refs[G + 3 : G + 7]
+    (acc, cin, xin, yin, zdn, zup, fin, sacc, scin, sxin, syin, szin,
+     lsem, cs, cr, xs, xr, ys, yr, zs, zr, fs, fr_, ss, sr, rs, rr, rl) = refs[G + 7 :]
+    K = G * split
+    r, f, t = lax.axis_index("rep"), lax.axis_index("frame"), lax.axis_index("tensor")
+    rows = acc.shape[3]
+    half = rows // 2
+    core, ypart, xpart = t ^ 1, t ^ 2, r ^ 1
+    mine = pl.ds(pl.multiple_of((r % 2) * half, half), half)
+    other = pl.ds(pl.multiple_of((1 - r % 2) * half, half), half)
+
+    def rc(src, dst, ssem, rsem, **dev):
+        return pltpu.make_async_remote_copy(src, dst, ssem, rsem, device_id=dev, device_id_type=MESH)
+
+    bar = pltpu.get_barrier_semaphore()
+    for d in range(1, F):
+        for peer in (f - d, f + d):
+            @pl.when((peer >= 0) & (peer < F))
+            def _():
+                pl.semaphore_signal(bar, inc=1, device_id={"frame": peer}, device_id_type=MESH)
+    pl.semaphore_signal(bar, inc=1, device_id={"tensor": core}, device_id_type=MESH)
+    pl.semaphore_signal(bar, inc=1, device_id={"tensor": ypart}, device_id_type=MESH)
+    pl.semaphore_signal(bar, inc=1, device_id={"tensor": t ^ 3}, device_id_type=MESH)
+    pl.semaphore_signal(bar, inc=1, device_id={"rep": xpart}, device_id_type=MESH)
+    pl.semaphore_wait(bar, F + 3)
+
+    def source(k, tt):
+        return g_refs[k // split].at[tt, :, pl.ds((k % split) * rows, rows)]
+
+    def load(k, j):
+        return pltpu.make_async_copy(source(k, t if j == 0 else ypart), acc.at[k, j], lsem.at[k, j])
+
+    def c_copy(k, j):
+        return rc(source(k, core if j == 0 else core ^ 2), cin.at[k, j], cs.at[k, j], cr.at[k, j], tensor=core)
+
+    def x_copy(k):
+        return rc(acc.at[k, 1, :, other], xin.at[k], xs.at[k], xr.at[k], rep=xpart)
+
+    def y_copy(k):
+        return rc(acc.at[k, 1, :, mine], yin.at[k], ys.at[k], yr.at[k], tensor=ypart)
+
+    def z_copy(k, dst, down):
+        buf = zdn if down else zup
+        return rc(acc.at[k, 0, dst], buf.at[k, dst], zs.at[k, dst], zr.at[k, dst, 0 if down else 1],
+                  frame=f - 1 if down else f + 1)
+
+    def fin_copy(k):
+        return rc(acc.at[k, 0, f], fin.at[k], fs.at[k], fr_.at[k], rep=xpart)
+
+    def small_copy(i):
+        if i == 0:
+            return rc(s_ref.at[pl.ds(0, 2), 1 - t % 2], scin, ss.at[0], sr.at[0], tensor=core)
+        if i == 1:
+            return rc(sacc, sxin, ss.at[1], sr.at[1], rep=xpart)
+        return rc(sacc.at[1 - t // 2], syin, ss.at[2], sr.at[2], tensor=ypart)
+
+    def small_frames(fn):
+        for d in range(1, F):
+            for to in (f - d, f + d):
+                @pl.when((to >= 0) & (to < F))
+                def _():
+                    fn(to)
+
+    def small_step(i):
+        if 0 < i < 4:
+            small_copy(i - 1).wait()
+        if i == 1:
+            for yy in range(2):
+                sacc[yy] = s_ref[yy, t % 2] + scin[yy]
+        elif i == 2:
+            sacc[...] += sxin[...]
+        elif i == 3:
+            syin[...] += sacc[t // 2]
+            small_frames(lambda to: rc(syin.at[to], szin.at[f], ss.at[3 + to], sr.at[3 + f], frame=to).start())
+        elif i == 4:
+            small_frames(lambda to: rc(syin.at[to], szin.at[to], ss.at[3 + to], sr.at[3 + to], frame=to).wait())
+            szin[f] = syin[f]
+            out = szin[0]
+            for n in range(1, F):
+                out = out + szin[n]
+            sout_ref[...] = out
+        if i < 3:
+            small_copy(i).start()
+
+    for k in range(K):
+        for j in (1, 0):
+            c_copy(k, j).start()
+            load(k, j).start()
+    rows_start(T, t, rc, (a_ref, b_ref), (ao_ref, bo_ref), False, rs, rr, rl)
+
+    def add(k, j):
+        c_copy(k, j).wait_recv()
+        load(k, j).wait()
+        @pl.loop(0, F)
+        def _(i):
+            acc[k, j, i] = acc[k, j, i] + cin[k, j, i]
+
+    def step_a(k):
+        add(k, 1)
+        x_copy(k).start()
+        add(k, 0)
+
+    def step_b(k):
+        x_copy(k).wait()
+        @pl.loop(0, F)
+        def _(i):
+            acc[k, 1, i, mine] = acc[k, 1, i, mine] + xin[k, i]
+        y_copy(k).start()
+
+    def step_c(k):
+        y_copy(k).wait()
+        @pl.loop(0, F)
+        def _(i):
+            acc[k, 0, i, mine] = acc[k, 0, i, mine] + yin[k, i]
+        for dst in range(F):
+            @pl.when((f == F - 1) & (dst < f))
+            def _():
+                z_copy(k, dst, True).start()
+            up = F - 1 - dst
+            @pl.when((f == 0) & (up > f))
+            def _():
+                z_copy(k, up, False).start()
+
+    def take(k, dst, down):
+        buf = zdn if down else zup
+        rc(buf.at[k, dst], buf.at[k, dst], zs.at[k, dst], zr.at[k, dst, 0 if down else 1], frame=f).wait_recv()
+        acc[k, 0, dst] = acc[k, 0, dst] + buf[k, dst]
+        @pl.when(dst != f)
+        def _():
+            z_copy(k, dst, down).start()
+
+    def step_d(k):
+        for hop in range(1, F):
+            @pl.when(f == F - 1 - hop)
+            def _():
+                for dst in range(F):
+                    @pl.when(dst <= f)
+                    def _():
+                        take(k, dst, True)
+            @pl.when(f == hop)
+            def _():
+                for up in range(F):
+                    dst = F - 1 - up
+                    @pl.when(dst >= f)
+                    def _():
+                        take(k, dst, False)
+        fin_copy(k).start()
+
+    def step_e(k):
+        fin_copy(k).wait()
+        part = pl.ds((k % split) * rows, rows)
+        out_ref[k // split, part, :] = acc[k, 0, f].astype(F32) + fin[k].astype(F32)
+
+    steps = (step_a, step_b, step_c, step_d, step_e)
+    for s in range(K + len(steps) - 1):
+        for i, fn in enumerate(steps):
+            if 0 <= s - i < K:
+                fn(s - i)
+        if s < 5:
+            small_step(s)
+    rows_wait(T, t, rc, (a_ref, b_ref), (ao_ref, bo_ref), False, rs, rr, rl)
+    for k in range(K):
+        for j in (1, 0):
+            c_copy(k, j).wait_send()
+        for dst in range(F):
+            @pl.when(dst < f)
+            def _():
+                z_copy(k, dst, True).wait_send()
+            @pl.when(dst > f)
+            def _():
+                z_copy(k, dst, False).wait_send()
+
+
+def reduce_all(grads, small, a, b):
+    F, T = lax.axis_size("frame"), lax.axis_size("tensor")
+    G = len(grads)
+    K = G * SPLIT
+    _, _, full, D = grads[0].shape
+    rows = full // SPLIT
+    dma = pltpu.SemaphoreType.DMA
+    V = pltpu.VMEM
+    sm = small.shape[2:]
+    sds = jax.ShapeDtypeStruct
+    any_spec, vmem = pl.BlockSpec(memory_space=pl.ANY), pl.BlockSpec(memory_space=pltpu.VMEM)
+    split_rows = (a.shape[1], a.shape[0]) + a.shape[2:]
+    return pl.pallas_call(
+        partial(reduce_kernel, F, T, G, SPLIT),
+        out_shape=(sds((G, full, D), F32), sds(sm, F32), sds(split_rows, a.dtype), sds(split_rows, b.dtype)),
+        in_specs=[any_spec] * G + [vmem] * 3,
+        out_specs=(vmem, vmem, any_spec, any_spec),
+        scratch_shapes=[
+            V((K, 2, F, rows, D), BF), V((K, 2, F, rows, D), BF), V((K, F, rows // 2, D), BF), V((K, F, rows // 2, D), BF),
+            V((K, F, rows, D), BF), V((K, F, rows, D), BF), V((K, rows, D), BF),
+            V((2, F) + sm, F32), V((2, F) + sm, F32), V((2, F) + sm, F32), V((F,) + sm, F32), V((F,) + sm, F32),
+            dma((K, 2)), dma((K, 2)), dma((K, 2)), dma((K,)), dma((K,)), dma((K,)), dma((K,)),
+            dma((K, F)), dma((K, F, 2)), dma((K,)), dma((K,)), dma((3 + F,)), dma((3 + F,)),
+            dma((2, T)), dma((2, T)), dma((2,)),
+        ],
+        compiler_params=pltpu.CompilerParams(collective_id=1, has_side_effects=True, vmem_limit_bytes=62 * 1024 * 1024),
+        name="reduce_all",
+    )(*grads, small.reshape((2, T // 2, F) + sm).astype(F32), a, b)
 
 
 def swap_core(v):
@@ -311,28 +758,25 @@
     small = jnp.concatenate(
         (gain_first, shift_first, gain_second, shift_second, gain_third, shift_third, part_bout, part_bin)
     )
-    FT = ("frame", "tensor")
-    small_all = lax.all_gather(small, FT, axis=0, tiled=False)
+
+    def lanes(flat):
+        pad = -flat.shape[-1] % 1024
+        flat = jnp.pad(flat, [(0, 0)] * (flat.ndim - 1) + [(0, pad)])
+        return flat.reshape(flat.shape[:-1] + (-1, 128))
+
+    def split_places(v):
+        v = jnp.pad(v, ((0, 0), (0, 0), (0, PAD - places_dev), (0, 0)))
+        return v.reshape(T, fr, PAD, D)
+
+    W, small_all, x, cot = gather_all(wl, lanes(small), split_places(tokens), split_places(cotangent))
+    W = W.reshape(4, T, F * rows_w, D)
+    x, cot = x.reshape(R, D), cot.reshape(R, D)
+    small_all = small_all.reshape(T, F, -1)
     nv = 7 * gain_first.shape[0]
-    vec = small_all[:, :nv].reshape(F * T, 7, -1).transpose(1, 0, 2).reshape(7, D)
+    vec = small_all[:, :, :nv].reshape(T, F, 7, -1).transpose(2, 1, 0, 3).reshape(7, D)
     vec = jnp.concatenate((vec, jnp.zeros((1, D), F32)), axis=0)
-    bin_all = small_all[:, nv:].reshape(F, T, -1).transpose(1, 0, 2).reshape(T, hid)
-    W = lax.all_gather(wl, FT, axis=0, tiled=False).reshape(F, T, 4, rows_w, D)
-    W = W.transpose(2, 1, 0, 3, 4).reshape(4, T, F * rows_w, D)
-
-    def to_owner(v):
-        v = jnp.pad(v, ((0, 0), (0, 0), (0, PAD - places_dev), (0, 0)))
-        v = v.reshape(T, fr, PAD, D)
-        v = lax.all_to_all(v, "tensor", split_axis=0, concat_axis=0, tiled=True)
-        return v.transpose(1, 0, 2, 3).reshape(R, D)
-
-    def from_owner(v):
-        v = v.reshape(fr, T, PAD, D).transpose(1, 0, 2, 3)
-        v = lax.all_to_all(v, "tensor", split_axis=0, concat_axis=0, tiled=True)
-        return v.reshape(clips, frames_dev, PAD, D)[:, :, :places_dev]
-
-    x = to_owner(tokens)
-    cot = to_owner(cotangent)
+    bin_all = small_all[:, :, nv : nv + hid // F].reshape(T, hid)
+
     keep = place_slot >= 0
     bias = jnp.where(keep, 0.0, -1e30).astype(F32).reshape(T, places_dev)
     bias = jnp.pad(bias, ((0, 0), (0, PAD - places_dev)), constant_values=-1e30).reshape(1, T * PAD)
@@ -473,31 +917,45 @@
     g_first = jnp.where(core == 0, g_time, zero)
     g_second = jnp.where(core == 0, zero, g_time)
     g_qkv = jnp.stack((g_first, g_second), axis=1).reshape(T, D, 3 * width)
-    part = jnp.stack((g_space, jnp.concatenate((g_qkv, g_wt), axis=2), g_in, g_out))
-    part = part.reshape(4, T, F, rows_w, D).transpose(2, 1, 0, 3, 4).reshape(F * T, 4, rows_w, D)
-    share = lax.psum_scatter(part, FT, scatter_dimension=0, tiled=False)
-    share = lax.psum(share.astype(F32), "rep")
-    smalls = jnp.concatenate((sv_s[0:4], sv_m[0:3], gb), axis=0)
-    smalls = lax.psum(smalls, ("rep", "frame", "tensor"))
+    kinds = (g_space, jnp.concatenate((g_qkv, g_wt), axis=2), g_in, g_out)
+    kinds = tuple(g.reshape(T, F, rows_w, D) for g in kinds)
+    n = gain_first.shape[0]
+    nb = bias_out.shape[0]
+    norms = jnp.concatenate((sv_s[0:4], sv_m[0:2]), axis=0).reshape(6, F, T, n).transpose(2, 1, 0, 3)
+    small_g = jnp.concatenate(
+        (
+            norms.reshape(T, F, 6 * n),
+            jnp.broadcast_to(sv_m[2].reshape(1, F, nb), (T, F, nb)),
+            jnp.broadcast_to(gb[:, None, :], (T, F, hid)),
+        ),
+        axis=2,
+    )
+    share, smalls, res_rows, gx_rows = reduce_all(
+        kinds, lanes(small_g), res.reshape(fr, T, PAD, D), gx.reshape(fr, T, PAD, D)
+    )
+    reps = lax.axis_size("rep")
+    if reps > 2:
+        share, smalls = (lax.psum(0.5 * v, "rep") for v in (share, smalls))
+    smalls = smalls.reshape(-1)
+
+    def join_places(v):
+        return v.reshape(clips, frames_dev, PAD, D)[:, :, :places_dev]
 
     def unpack(g):
         return g[:, :width], g[:, width : 2 * width], g[:, 2 * width : 3 * width], g[:, 3 * width :].T
 
     gs_q, gs_k, gs_v, gs_o = unpack(share[0])
     gt_q, gt_k, gt_v, gt_o = unpack(share[1])
-    n = gain_first.shape[0]
-    at = (f_id * T + t_id) * n
-    own = lambda row: lax.dynamic_slice(smalls[row], (at,), (n,))
-    nb = bias_out.shape[0]
+    own = lambda i: smalls[i * n : (i + 1) * n]
     return (
-        from_owner(res),
-        from_owner(gx).astype(F32),
+        join_places(res_rows),
+        join_places(gx_rows).astype(F32),
         gs_q, gs_k, gs_v, gs_o,
         gt_q, gt_k, gt_v, gt_o,
         share[2],
-        lax.dynamic_slice(smalls, (7 + t_id, 0), (1, hid))[0],
+        smalls[6 * n + nb : 6 * n + nb + hid],
         share[3].T,
-        lax.dynamic_slice(smalls[6], (f_id * nb,), (nb,)),
+        smalls[6 * n : 6 * n + nb],
         own(0), own(1), own(2), own(3), own(4), own(5),
     )
 

time: 698 us -> 503 us (0.72); the launches traced: 684 us -> 498 us
  waiting for transfers between devices: 269 us -> 42.6 us
  Pallas kernels: 123 us -> 338 us
  blocking collectives: 147 us -> 33.1 us
  local copies, waits for them, and re-layouts: 66.6 us -> 47.5 us
  starting transfers between devices: 39 us -> 23.2 us
  other arithmetic: 25.3 us -> 11.4 us
  between operations: 15.2 us -> 1.46 us
    pallas_call x0 -> x2, Pallas kernels: none -> 216 us  [the longest x1 115 us: reduce_all(): pl.pallas_call(partial(reduce_kernel, F, T, G, SPLIT), out_shape=(sds((G,...]
    reduce_scatter x1 -> x0, waiting for transfers between devices: 193 us -> none  [shards(): share = lax.psum_scatter(part, FT, scatter_dimension=0, tiled=False)]
    unnamed x1 -> x0, blocking collectives: 67.5 us -> none
    psum x1 -> x0, blocking collectives: 43.4 us -> none  [shards(): smalls = lax.psum(smalls, ('rep', 'frame', 'tensor'))]
    all_gather x1 -> x0, waiting for transfers between devices: 29.4 us -> none  [shards(): W = lax.all_gather(wl, FT, axis=0, tiled=False).reshape(F, T, 4, rows_w, D)]
    reshape x7 -> x8, local copies, waits for them, and re-layouts: 19.9 us -> 1.12 us  [the longest x1 0.69 us: shards(): bin_all = small_all[:, :, nv:nv + hid // F].reshape(T, hid)]
    all_to_all x4 -> x0, starting transfers between devices: 14.7 us -> none  [the longest x2 7.75 us: to_owner(): v = lax.all_to_all(v, 'tensor', split_axis=0, concat_axis=0, tiled=True)]
    transpose x1 -> x0, other arithmetic: 12.8 us -> none  [shards(): part.reshape(4, T, F, rows_w, D).transpose(2, 1, 0, 3, 4)]
  transfers between devices with their start and end apart: 15 -> 8, of which waited for: 10 -> 8; matrix products, arithmetic and copies ran while one was open for 4% -> 2% of each run, Pallas kernels for 3% -> 0%
where the time goes in v2:
time: 503 us; the launch traced here: 498 us
  Pallas kernels  338 us (67%)
  local copies, waits for them, and re-layouts  47.5 us (9%)
  waiting for transfers between devices  42.6 us (8%)
  blocking collectives  33.1 us (7%)
  starting transfers between devices  23.2 us (5%)
  other arithmetic  11.4 us (2%)
    pallas_call x5, Pallas kernels, call(): pl.pallas_call(body, out_shape=tuple((jax.ShapeDtypeStruct(s, d) for s, d...  122 us
    pallas_call x1, Pallas kernels, reduce_all(): pl.pallas_call(partial(reduce_kernel, F, T, G, SPLIT), out_shape=(sds((G,...  115 us
    pallas_call x1, Pallas kernels, gather_all(): pl.pallas_call(partial(gather_kernel, F, T, K, KS), out_shape=(sds((K, T,...  101 us
    all_to_all x2, blocking collectives, to_time(): return lax.all_to_all(v, 'frame', split_axis=0, concat_axis=0, tiled=True)  33.1 us
    all_to_all x3, waiting for transfers between devices, to_frames(): v = lax.all_to_all(v, 'frame', split_axis=0, concat_axis=0, tiled=True)  29.3 us
    all_to_all x3, starting transfers between devices, to_frames(): v = lax.all_to_all(v, 'frame', split_axis=0, concat_axis=0, tiled=True)  19.4 us
    unnamed x43, local copies, waits for them, and re-layouts  15.9 us
  transfers between devices with their start and end apart: 8, of which 8 were waited for; matrix products, arithmetic and copies ran while one was open for 2% of the time, Pallas kernels for 0%

profile of v2, /device:TPU:0, one launch (start us, length us, event | category | flops | bytes accessed | tf_op | source)
XLA Modules:
  0.0 497.6 jit_solution(16353779395729027432)
XLA Ops:
  7.8 101.2 %gather_all.1 = (bf16[4,4,4,192,768]{4,3,2,1,0:T(8,128)(2,1)S(1)}, f32[4,4,8,128]{3,2,1,0:T(8,128)S(1)}, bf16[2,4,56,768]{3,2,1,0:T(8,128)(2,1)S(1)}, bf16[2,4,56,768]{3,2,1,0:T(8,128)(2,1)S(1)}) custom-call(bf16[4,192,768]{2,1,0:T(8,128)(2,1)S(1)} %pad_maximum_fusion.3.w_ref, f32[8,128]{1,0:T(8,128)S(1)} %pad_bitcast_fusion.s_ref, ...), custom_call_target="tpu_custom_call" | custom-call | tf_op jit(solution)/shard_map/gather_all/pallas_call | solution.py:497
  109.0 6.4 %copy-done = bf16[4,4,4,192,768]{4,3,2,1,0:T(8,128)(2,1)} copy-done((bf16[4,4,4,192,768]{4,3,2,1,0:T(8,128)(2,1)}, bf16[4,4,4,192,768]{4,3,2,1,0:T(8,128)(2,1)S(1)}, u32[]{:S(2)}) %copy-start) | copy-done | bytes 18874392
  118.8 13.6 %space_forward.1 = (bf16[4,448,576]{2,1,0:T(8,128)(2,1)}, bf16[4,448,192]{2,1,0:T(8,128)(2,1)}, f32[448,768]{1,0:T(8,128)}, bf16[448,768]{1,0:T(8,128)(2,1)}) custom-call(bf16[448,768]{1,0:T(8,128)(2,1)} %bitcast.121, f32[8,768]{1,0:T(8,128)} %concatenate.29.vec_ref, f32[1,224]{1,0:T(1,128)} %reshape.216.bias_ref, bf16[4,4,768,768]{3,2,1,0:T(8,128)(2,1)} %bitcast.112), custom_call_target="tpu_custom_call" | custom-call | tf_op jit(solution)/shard_map/space_forward/pallas_call | solution.py:258
  133.6 21.2 %all_to_all.30 = bf16[4,2,56,768]{3,2,1,0:T(8,128)(2,1)S(1)} all-to-all(bf16[4,2,56,768]{3,2,1,0:T(8,128)(2,1)S(1)} %bitcast.141), channel_id=1, replica_groups=mesh['rep'=2,'frame'=4,'tensor'=4] {'frame'}, dimensions={0} | all-to-all | bytes 1376256 | tf_op jit(solution)/shard_map/all_to_all | solution.py:808
  157.1 1.2 copy.111
  158.2 22.3 %time_forward.1 = (bf16[2,896,576]{2,1,0:T(8,128)(2,1)}, bf16[2,896,192]{2,1,0:T(8,128)(2,1)}) custom-call(s32[1]{0:T(128)} %bitcast.14.core_ref, bf16[896,768]{1,0:T(8,128)(2,1)} %bitcast.125, bf16[4,4,768,768]{3,2,1,0:T(8,128)(2,1)} %bitcast.113, f32[896,1]{1,0:T(8,128)} %reshape.243.mask_ref), custom_call_target="tpu_custom_call" | custom-call | tf_op jit(solution)/shard_map/time_forward/pallas_call | solution.py:258
  180.6 1.2 fusion.4
  183.5 3.5 all-to-all-start.1
  187.9 1.6 collective-permute-done.1
  189.5 8.6 %all-to-all-done.1 = bf16[4,2,56,384]{3,2,1,0:T(8,128)(2,1)S(1)} async-done(((bf16[4,2,56,384]{3,2,1,0:T(8,128)(2,1)}), bf16[4,2,56,384]{3,2,1,0:T(8,128)(2,1)S(1)}, u32[]{:S(2)}, u32[]{:S(2)}) %all-to-all-start.1) | async-done | bytes 344096 | tf_op jit(solution)/shard_map/all_to_all | solution.py:819
  198.1 3.7 all-to-all-start.2
  202.6 9.5 %all-to-all-done.2 = bf16[4,2,56,384]{3,2,1,0:T(8,128)(2,1)S(1)} async-done(((bf16[4,2,56,384]{3,2,1,0:T(8,128)(2,1)}), bf16[4,2,56,384]{3,2,1,0:T(8,128)(2,1)S(1)}, u32[]{:S(2)}, u32[]{:S(2)}) %all-to-all-start.2) | async-done | bytes 344096 | tf_op jit(solution)/shard_map/all_to_all | solution.py:819
  212.8 1.5 pad_maximum_fusion.4
  215.4 26.8 %mlp_both.1 = (bf16[448,768]{1,0:T(8,128)(2,1)}, f32[448,768]{1,0:T(8,128)}, bf16[4,448,192]{2,1,0:T(8,128)(2,1)}, bf16[4,768,768]{2,1,0:T(8,128)(2,1)}, bf16[4,...) custom-call(f32[448,768]{1,0:T(8,128)} %get-tuple-element.50.xs_ref, ...), custom_call_target="tpu_custom_call" | custom-call | tf_op jit(solution)/shard_map/mlp_both/pallas_call | solution.py:258
  242.2 1.2 fusion.3
  245.6 3.5 all-to-all-start.3
  249.4 1.6 collective-permute-done.2
  251.0 6.9 %all-to-all-done.3 = bf16[4,2,56,384]{3,2,1,0:T(8,128)(2,1)S(1)} async-done(((bf16[4,2,56,384]{3,2,1,0:T(8,128)(2,1)}), bf16[4,2,56,384]{3,2,1,0:T(8,128)(2,1)S(1)}, u32[]{:S(2)}, u32[]{:S(2)}) %all-to-all-start.3) | async-done | bytes 344096 | tf_op jit(solution)/shard_map/all_to_all | solution.py:808
  258.0 11.9 %all_to_all.31 = bf16[4,2,56,384]{3,2,1,0:T(8,128)(2,1)S(1)} all-to-all(bf16[4,2,56,384]{3,2,1,0:T(8,128)(2,1)S(1)} %copy.123), channel_id=1, replica_groups=mesh['rep'=2,'frame'=4,'tensor'=4] {'frame'}, dimensions={0} | all-to-all | bytes 688128 | tf_op jit(solution)/shard_map/all_to_all | solution.py:808
  271.6 31.3 %time_backward.1 = (bf16[2,768,576]{2,1,0:T(8,128)(2,1)}, f32[896,768]{1,0:T(8,128)}) custom-call(s32[1]{0:T(128)} %bitcast.14.core_ref, bf16[896,768]{1,0:T(8,128)(2,1)} %bitcast.126, bf16[4,4,768,768]{3,2,1,0:T(8,128)(2,1)} %bitcast.117, f32[896,1]{1,0:T(8,128)} %reshape.243.mask_ref, bf16[2,896,576]{2,1,0:T(8,128)(2,1)} %get-tuple-element.55.qkv_ref, ...), custom_call_target="tpu_custom_call" | custom-call | tf_op jit(solution)/shard_map/time_backward/pallas_call | solution.py:258
  302.9 2.0 copy.150
  305.1 2.0 collective-permute-done.3
  308.2 12.3 %all-to-all-start.5 = ((bf16[4,2,56,768]{3,2,1,0:T(8,128)(2,1)}), bf16[4,2,56,768]{3,2,1,0:T(8,128)(2,1)S(1)}, u32[]{:S(2)}, u32[]{:S(2)}) async-start(bf16[4,2,56,768]{3,2,1,0:T(8,128)(2,1)} %add_convert_fusion), calls=%async_computation.5 | async-start | bytes 1376256 | tf_op jit(solution)/shard_map/all_to_all | solution.py:819
  324.4 3.2 pad_maximum_fusion.refs_1_
  327.6 11.2 %all-to-all-done.5 = bf16[4,2,56,768]{3,2,1,0:T(8,128)(2,1)S(1)} async-done(((bf16[4,2,56,768]{3,2,1,0:T(8,128)(2,1)}), bf16[4,2,56,768]{3,2,1,0:T(8,128)(2,1)S(1)}, u32[]{:S(2)}, u32[]{:S(2)}) %all-to-all-start.5) | async-done | bytes 688160 | tf_op jit(solution)/shard_map/all_to_all | solution.py:819
  339.7 28.2 %space_backward.1 = (bf16[448,768]{1,0:T(8,128)(2,1)}, bf16[4,768,768]{2,1,0:T(8,128)(2,1)}, f32[8,768]{1,0:T(8,128)}) custom-call(bf16[448,768]{1,0:T(8,128)(2,1)} %bitcast.122, f32[448,768]{1,0:T(8,128)} %get-tuple-element.50.xs_ref, f32[448,768]{1,0:T(8,128)} %get-tuple-element.54.gt_ref, bf16[448,768]{1,0:T(8,128)(2,1)} %bitcast.136, ...), custom_call_target="tpu_custom_call" | custom-call | tf_op jit(solution)/shard_map/space_backward/pallas_call | solution.py:258
  369.8 114.8 %reduce_all.1 = (f32[4,192,768]{2,1,0:T(8,128)}, f32[16,128]{1,0:T(8,128)}, bf16[4,2,56,768]{3,2,1,0:T(8,128)(2,1)}, bf16[4,2,56,768]{3,2,1,0:T(8,128)(2,1)}) custom-call(bf16[4,4,192,768]{3,2,1,0:T(8,128)(2,1)} %bitcast.133, bf16[4,4,192,768]{3,2,1,0:T(8,128)(2,1)} %pad_maximum_fusion.refs_1_, bf16[4,4,192,768]{3,2,1,0:T(8,128)(2,1)} %bitcast.131, ...), custom_call_target="tpu_custom_call" | custom-call | tf_op jit(solution)/shard_map/reduce_all/pallas_call | solution.py:701
  484.7 1.4 slice.165
  486.1 1.5 fusion.5
  487.6 1.3 slice.166
  488.9 2.8 slice_bitcast_fusion
  495.0 1.3 copy_convert_fusion
  (119 shorter events, 35.3 us)
Async XLA Ops:
  0.7 5.5 %copy-start.7 = (bf16[2,4,49,768]{3,1,2,0:T(4,128)(2,1)S(1)}, bf16[2,4,49,768]{3,1,2,0:T(4,128)(2,1)}, u32[]{:S(2)}) copy-start(bf16[2,4,49,768]{3,1,2,0:T(4,128)(2,1)} %param.41) | copy-start | bytes 1806340
  6.2 0.9 copy-start.10
  6.2 0.9 copy-start.11
  6.2 1.0 copy-start.12
  6.2 1.0 copy-start.13
  6.2 1.0 copy-start.14
  6.3 1.1 copy-start.15
  6.3 1.3 copy-start.8
  6.4 1.2 copy-start.9
  7.8 109.7 %copy-start.17 = (s32[196]{0:T(256)S(1)}, s32[196]{0:T(256)}, u32[]{:S(2)}) copy-start(s32[196]{0:T(256)} %param.40) | copy-start | bytes 2356
  109.0 6.5 %copy-start = (bf16[4,4,4,192,768]{4,3,2,1,0:T(8,128)(2,1)}, bf16[4,4,4,192,768]{4,3,2,1,0:T(8,128)(2,1)S(1)}, u32[]{:S(2)}) copy-start(bf16[4,4,4,192,768]{4,3,2,1,0:T(8,128)(2,1)S(1)} %get-tuple-element.49) | copy-start | bytes 56623108
  115.5 0.9 copy-start.1
  116.3 0.8 copy-start.2
  154.8 2.1 collective-permute-start
  183.5 14.6 %all-to-all-start.1 = ((bf16[4,2,56,384]{3,2,1,0:T(8,128)(2,1)}), bf16[4,2,56,384]{3,2,1,0:T(8,128)(2,1)S(1)}, u32[]{:S(2)}, u32[]{:S(2)}) async-start(bf16[4,2,56,384]{3,2,1,0:T(8,128)(2,1)} %squeeze.26), calls=%async_computation.1 | async-start | bytes 688128 | tf_op jit(solution)/shard_map/all_to_all | solution.py:819
  187.7 1.8 collective-permute-start.1
  198.1 14.0 %all-to-all-start.2 = ((bf16[4,2,56,384]{3,2,1,0:T(8,128)(2,1)}), bf16[4,2,56,384]{3,2,1,0:T(8,128)(2,1)S(1)}, u32[]{:S(2)}, u32[]{:S(2)}) async-start(bf16[4,2,56,384]{3,2,1,0:T(8,128)(2,1)} %collective-permute-done.1), calls=%async_computation.2 | async-start | bytes 688128 | tf_op jit(solution)/shard_map/all_to_all | solution.py:819
  245.6 12.4 %all-to-all-start.3 = ((bf16[4,2,56,384]{3,2,1,0:T(8,128)(2,1)}), bf16[4,2,56,384]{3,2,1,0:T(8,128)(2,1)S(1)}, u32[]{:S(2)}, u32[]{:S(2)}) async-start(bf16[4,2,56,384]{3,2,1,0:T(8,128)(2,1)} %copy.122), calls=%async_computation.3 | async-start | bytes 688128 | tf_op jit(solution)/shard_map/all_to_all | solution.py:808
  249.3 1.7 collective-permute-start.2
  305.0 2.2 collective-permute-start.3
  307.2 14.9 %copy-start.3 = (bf16[2,768,576]{2,1,0:T(8,128)(2,1)S(1)}, bf16[2,768,576]{2,1,0:T(8,128)(2,1)}, u32[]{:S(2)}) copy-start(bf16[2,768,576]{2,1,0:T(8,128)(2,1)} %get-tuple-element.61) | copy-start | bytes 5308420
  308.2 30.6 %all-to-all-start.5 = ((bf16[4,2,56,768]{3,2,1,0:T(8,128)(2,1)}), bf16[4,2,56,768]{3,2,1,0:T(8,128)(2,1)S(1)}, u32[]{:S(2)}, u32[]{:S(2)}) async-start(bf16[4,2,56,768]{3,2,1,0:T(8,128)(2,1)} %add_convert_fusion), calls=%async_computation.5 | async-start | bytes 1376256 | tf_op jit(solution)/shard_map/all_to_all | solution.py:819
  323.0 1.4 copy-start.4
  339.7 29.2 %copy-start.16 = (f32[4,768]{1,0:T(4,128)S(1)}, f32[4,768]{1,0:T(4,128)}, u32[]{:S(2)}) copy-start(f32[4,768]{1,0:T(4,128)} %get-tuple-element.67) | copy-start | bytes 36868
  491.6 3.4 copy-start.6
  493.3 3.0 copy-start.5

commit v3 on v2

--- a/solution.py
+++ b/solution.py
@@ -16,7 +16,7 @@
 GELU_C = 0.7978845608028654
 SCALE = HEAD ** (-0.5)
 MESH = pl.DeviceIdType.MESH
-KS = 2
+KS = 1
 SPLIT = 2
 
 
@@ -200,7 +200,7 @@
 def mlp_both(
     width, tensors,
     xs_ref, cot_ref, ot_ref, vec_ref, bin_ref, wt_ref, win_ref, wout_ref,
-    res_ref, gt_ref, do_ref, gin_ref, gout_ref, gwt_ref, sv_ref, gb_ref,
+    res_ref, gt_ref, do_ref, gg_ref, gwt_ref, sv_ref, gb_ref,
     xt_scr, hm_scr, xm_scr, dhm_scr,
 ):
     t = pl.program_id(0)
@@ -217,8 +217,9 @@
 
     hm = hm_scr[...]
     dz = cot_ref[...]
-    win = win_ref[0, 0]
-    wout = wout_ref[0, 0]
+    lines, _, _, rows, cols = win_ref.shape
+    win = win_ref[:, 0, 0].reshape(lines * rows, cols)
+    wout = wout_ref[:, 0, 0].reshape(lines * rows, cols)
     pre = dot(hm, win) + bin_ref[pl.ds(t, 1), :]
     sq = pre * pre
     th = jnp.tanh(GELU_C * (pre + 0.044715 * (pre * sq)))
@@ -228,8 +229,8 @@
     dpre = dot(dz, wout) * slope
     dpre_b = dpre.astype(BF)
     gb_ref[pl.ds(t, 1), :] = jnp.sum(dpre_b.astype(F32), axis=0, keepdims=True)
-    gout_ref[0] = dot(dz, hidden, TN).astype(BF)
-    gin_ref[0] = dot(hm, dpre_b, TN).astype(BF)
+    gg_ref[:, 0, 0] = dot(hm, dpre_b, TN).astype(BF).reshape(lines, rows, cols)
+    gg_ref[:, 0, 1] = dot(dz, hidden, TN).astype(BF).reshape(lines, rows, cols)
     dhm_scr[...] += dot(dpre_b, win, NT)
 
     @pl.when(t == pl.num_programs(0) - 1)
@@ -512,10 +513,10 @@
 
 
 def reduce_kernel(F, T, G, split, *refs):
-    g_refs, s_ref, a_ref, b_ref = refs[:G], *refs[G : G + 3]
-    out_ref, sout_ref, ao_ref, bo_ref = refs[G + 3 : G + 7]
+    g_refs, h_ref, s_ref, a_ref, b_ref = refs[:G], *refs[G : G + 4]
+    out_ref, sout_ref, ao_ref, bo_ref = refs[G + 4 : G + 8]
     (acc, cin, xin, yin, zdn, zup, fin, sacc, scin, sxin, syin, szin,
-     lsem, cs, cr, xs, xr, ys, yr, zs, zr, fs, fr_, ss, sr, rs, rr, rl) = refs[G + 7 :]
+     lsem, cs, cr, xs, xr, ys, yr, zs, zr, fs, fr_, ss, sr, rs, rr, rl, hin, hs, hr) = refs[G + 8 :]
     K = G * split
     r, f, t = lax.axis_index("rep"), lax.axis_index("frame"), lax.axis_index("tensor")
     rows = acc.shape[3]
@@ -558,6 +559,9 @@
         buf = zdn if down else zup
         return rc(acc.at[k, 0, dst], buf.at[k, dst], zs.at[k, dst], zr.at[k, dst, 0 if down else 1],
                   frame=f - 1 if down else f + 1)
+
+    def pair_copy():
+        return rc(h_ref, hin, hs, hr, rep=xpart)
 
     def fin_copy(k):
         return rc(acc.at[k, 0, f], fin.at[k], fs.at[k], fr_.at[k], rep=xpart)
@@ -673,6 +677,11 @@
                 fn(s - i)
         if s < 5:
             small_step(s)
+        if s == K - 1:
+            pair_copy().start()
+    pair_copy().wait()
+    for i in range(h_ref.shape[0]):
+        out_ref[G + i] = h_ref[i].astype(F32) + hin[i].astype(F32)
     rows_wait(T, t, rc, (a_ref, b_ref), (ao_ref, bo_ref), False, rs, rr, rl)
     for k in range(K):
         for j in (1, 0):
@@ -686,7 +695,7 @@
                 z_copy(k, dst, False).wait_send()
 
 
-def reduce_all(grads, small, a, b):
+def reduce_all(grads, half, small, a, b):
     F, T = lax.axis_size("frame"), lax.axis_size("tensor")
     G = len(grads)
     K = G * SPLIT
@@ -700,8 +709,8 @@
     split_rows = (a.shape[1], a.shape[0]) + a.shape[2:]
     return pl.pallas_call(
         partial(reduce_kernel, F, T, G, SPLIT),
-        out_shape=(sds((G, full, D), F32), sds(sm, F32), sds(split_rows, a.dtype), sds(split_rows, b.dtype)),
-        in_specs=[any_spec] * G + [vmem] * 3,
+        out_shape=(sds((G + half.shape[0], full, D), F32), sds(sm, F32), sds(split_rows, a.dtype), sds(split_rows, b.dtype)),
+        in_specs=[any_spec] * G + [vmem] * 4,
         out_specs=(vmem, vmem, any_spec, any_spec),
         scratch_shapes=[
             V((K, 2, F, rows, D), BF), V((K, 2, F, rows, D), BF), V((K, F, rows // 2, D), BF), V((K, F, rows // 2, D), BF),
@@ -709,11 +718,11 @@
             V((2, F) + sm, F32), V((2, F) + sm, F32), V((2, F) + sm, F32), V((F,) + sm, F32), V((F,) + sm, F32),
             dma((K, 2)), dma((K, 2)), dma((K, 2)), dma((K,)), dma((K,)), dma((K,)), dma((K,)),
             dma((K, F)), dma((K, F, 2)), dma((K,)), dma((K,)), dma((3 + F,)), dma((3 + F,)),
-            dma((2, T)), dma((2, T)), dma((2,)),
+            dma((2, T)), dma((2, T)), dma((2,)), V(half.shape, BF), dma(()), dma(()),
         ],
         compiler_params=pltpu.CompilerParams(collective_id=1, has_side_effects=True, vmem_limit_bytes=62 * 1024 * 1024),
         name="reduce_all",
-    )(*grads, small.reshape((2, T // 2, F) + sm).astype(F32), a, b)
+    )(*grads, half, small.reshape((2, T // 2, F) + sm).astype(F32), a, b)
 
 
 def swap_core(v):
@@ -747,8 +756,6 @@
         (
             pack(query_space, key_space, value_space, output_space),
             pack(query_time, key_time, value_time, output_time),
-            mlp_in,
-            mlp_out.T,
         )
     )
     part_bin = lax.dynamic_slice(bias_in, (f_id * (hid // F),), (hid // F,)).astype(F32)
@@ -769,7 +776,10 @@
         return v.reshape(T, fr, PAD, D)
 
     W, small_all, x, cot = gather_all(wl, lanes(small), split_places(tokens), split_places(cotangent))
-    W = W.reshape(4, T, F * rows_w, D)
+    FT = ("frame", "tensor")
+    W, wl_mlp = lax.optimization_barrier((W, jnp.stack((mlp_in, mlp_out.T))))
+    W_mlp = lax.all_gather(wl_mlp, FT, axis=0, tiled=False).reshape(F, T, 2, rows_w, D)
+    W = W.reshape(2, T, F * rows_w, D)
     x, cot = x.reshape(R, D), cot.reshape(R, D)
     small_all = small_all.reshape(T, F, -1)
     nv = 7 * gain_first.shape[0]
@@ -852,26 +862,29 @@
         return jnp.stack((first, second), axis=2).reshape(R, T, width).transpose(1, 0, 2)
 
     ot_all = by_tensor(ot_mine, ot_other)
-    win_spec = lambda kind: pl.BlockSpec((1, 1, D, D), lambda t: (kind, t, 0, 0))
-    res, gt, dot_all, g_in, g_out, g_wt, sv_m, gb = call(
+    win_spec = lambda kind: pl.BlockSpec((F, 1, 1, rows_w, D), lambda t: (0, t, kind, 0, 0))
+    res, gt, dot_all, g_mlp, g_wt, sv_m, gb = call(
         partial(mlp_both, width, T),
         T,
-        (xs, cot, ot_all, vec, bin_all, W, W, W),
+        (xs, cot, ot_all, vec, bin_all, W, W_mlp, W_mlp),
         [
             whole((R, D)), whole((R, D)), whole((T, R, width)), whole((8, D)), whole((T, hid)),
-            pl.BlockSpec((1, T, D, D), lambda t: (1, 0, 0, 0)), win_spec(2), win_spec(3),
+            pl.BlockSpec((1, T, D, D), lambda t: (1, 0, 0, 0)), win_spec(0), win_spec(1),
         ],
         [
-            ((R, D), BF), ((R, D), F32), ((T, R, width), BF), ((T, D, hid), BF), ((T, D, hid), BF),
+            ((R, D), BF), ((R, D), F32), ((T, R, width), BF), ((F, T, 2, rows_w, D), BF),
             ((T, D, width), BF), ((8, D), F32), ((T, hid), F32),
         ],
         [
             whole((R, D)), whole((R, D)), whole((T, R, width)),
-            pl.BlockSpec((1, D, hid), lambda t: (t, 0, 0)), pl.BlockSpec((1, D, hid), lambda t: (t, 0, 0)),
+            pl.BlockSpec((F, 1, 2, rows_w, D), lambda t: (0, t, 0, 0, 0)),
             whole((T, D, width)), whole((8, D)), whole((T, hid)),
         ],
         [pltpu.VMEM((R, D), F32), pltpu.VMEM((R, D), BF), pltpu.VMEM((R, D), F32), pltpu.VMEM((R, D), F32)],
         name="mlp_both",
+    )
+    share_mlp = lax.psum_scatter(
+        g_mlp.reshape(F * T, 2, rows_w, D), FT, scatter_dimension=0, tiled=False
     )
     d = dot_all.reshape(halves, 2, R, width)
     d_mine = jnp.where(core == 0, d[:, 0], d[:, 1])
@@ -917,7 +930,7 @@
     g_first = jnp.where(core == 0, g_time, zero)
     g_second = jnp.where(core == 0, zero, g_time)
     g_qkv = jnp.stack((g_first, g_second), axis=1).reshape(T, D, 3 * width)
-    kinds = (g_space, jnp.concatenate((g_qkv, g_wt), axis=2), g_in, g_out)
+    kinds = (g_space, jnp.concatenate((g_qkv, g_wt), axis=2))
     kinds = tuple(g.reshape(T, F, rows_w, D) for g in kinds)
     n = gain_first.shape[0]
     nb = bias_out.shape[0]
@@ -931,7 +944,7 @@
         axis=2,
     )
     share, smalls, res_rows, gx_rows = reduce_all(
-        kinds, lanes(small_g), res.reshape(fr, T, PAD, D), gx.reshape(fr, T, PAD, D)
+        kinds, share_mlp, lanes(small_g), res.reshape(fr, T, PAD, D), gx.reshape(fr, T, PAD, D)
     )
     reps = lax.axis_size("rep")
     if reps > 2:

time: 503 us -> 460 us (0.915)
  Pallas kernels: 338 us -> 263 us
  waiting for transfers between devices: 42.6 us -> 60.9 us
  between operations: 1.46 us -> 14.9 us
  blocking collectives: 33.1 us -> 39.8 us
    pallas_call x1, Pallas kernels: 101 us -> 63.1 us  [gather_all(): pl.pallas_call(partial(gather_kernel, F, T, K, KS), out_shape=(sds((K, T,...]
    pallas_call x1, Pallas kernels: 115 us -> 76.7 us  [reduce_all(): pl.pallas_call(partial(reduce_kernel, F, T, G, SPLIT), out_shape=(sds((G...]
    all_to_all x3, waiting for transfers between devices: 29.3 us -> 45.9 us  [to_frames(): v = lax.all_to_all(v, 'frame', split_axis=0, concat_axis=0, tiled=True)]
    all_to_all x2, blocking collectives: 33.1 us -> 39.8 us  [to_time(): return lax.all_to_all(v, 'frame', split_axis=0, concat_axis=0, tiled=True)]
  transfers between devices with their start and end apart: 8 -> 10, of which waited for: 8 -> 8; matrix products, arithmetic and copies ran while one was open for 2% -> 6% of each run, Pallas kernels for 0% -> 21%
where the time goes in v3:
time: 460 us; the launch traced here: 459 us
  Pallas kernels  263 us (57%)
  waiting for transfers between devices  60.9 us (13%)
  local copies, waits for them, and re-layouts  44.4 us (10%)
  blocking collectives  39.8 us (9%)
  starting transfers between devices  23.6 us (5%)
  between operations  14.9 us (3%)
  other arithmetic  13.3 us (3%)
    pallas_call x5, Pallas kernels, call(): pl.pallas_call(body, out_shape=tuple((jax.ShapeDtypeStruct(s, d) for s, d...  123 us
    pallas_call x1, Pallas kernels, reduce_all(): pl.pallas_call(partial(reduce_kernel, F, T, G, SPLIT), out_shape=(sds((G...  76.7 us
    pallas_call x1, Pallas kernels, gather_all(): pl.pallas_call(partial(gather_kernel, F, T, K, KS), out_shape=(sds((K, T,...  63.1 us
    all_to_all x3, waiting for transfers between devices, to_frames(): v = lax.all_to_all(v, 'frame', split_axis=0, concat_axis=0, tiled=True)  45.9 us
    all_to_all x2, blocking collectives, to_time(): return lax.all_to_all(v, 'frame', split_axis=0, concat_axis=0, tiled=True)  39.8 us
    all_to_all x3, starting transfers between devices, to_frames(): v = lax.all_to_all(v, 'frame', split_axis=0, concat_axis=0, tiled=True)  19.2 us
    unnamed x43, local copies, waits for them, and re-layouts  15.4 us
  transfers between devices with their start and end apart: 10, of which 8 were waited for; matrix products, arithmetic and copies ran while one was open for 6% of the time, Pallas kernels for 21%

profile of v3, /device:TPU:0, one launch (start us, length us, event | category | flops | bytes accessed | tf_op | source)
XLA Modules:
  0.0 459.4 jit_solution(10370715113402462080)
XLA Ops:
  15.1 63.1 %gather_all.1 = (bf16[2,4,4,192,768]{4,3,2,1,0:T(8,128)(2,1)S(1)}, f32[4,4,8,128]{3,2,1,0:T(8,128)S(1)}, bf16[2,4,56,768]{3,2,1,0:T(8,128)(2,1)S(1)}, bf16[2,4,56,768]{3,2,1,0:T(8,128)(2,1)S(1)}) custom-call(bf16[2,192,768]{2,1,0:T(8,128)(2,1)S(1)} %pad_maximum_fusion.5.w_ref, f32[8,128]{1,0:T(8,128)S(1)} %pad_bitcast_fusion.s_ref, ...), custom_call_target="tpu_custom_call" | custom-call | tf_op jit(solution)/shard_map/gather_all/pallas_call | solution.py:498
  78.2 3.6 copy-done
  85.2 13.7 %space_forward.1 = (bf16[4,448,576]{2,1,0:T(8,128)(2,1)}, bf16[4,448,192]{2,1,0:T(8,128)(2,1)}, f32[448,768]{1,0:T(8,128)}, bf16[448,768]{1,0:T(8,128)(2,1)}) custom-call(bf16[448,768]{1,0:T(8,128)(2,1)} %bitcast.118, f32[8,768]{1,0:T(8,128)} %concatenate.29.vec_ref, f32[1,224]{1,0:T(1,128)} %reshape.216.bias_ref, bf16[2,4,768,768]{3,2,1,0:T(8,128)(2,1)} %bitcast.113), custom_call_target="tpu_custom_call" | custom-call | tf_op jit(solution)/shard_map/space_forward/pallas_call | solution.py:259
  100.1 27.7 %all_to_all.30 = bf16[4,2,56,768]{3,2,1,0:T(8,128)(2,1)S(1)} all-to-all(bf16[4,2,56,768]{3,2,1,0:T(8,128)(2,1)S(1)} %bitcast.141), channel_id=1, replica_groups=mesh['rep'=2,'frame'=4,'tensor'=4] {'frame'}, dimensions={0} | all-to-all | bytes 1376256 | tf_op jit(solution)/shard_map/all_to_all | solution.py:818
  128.9 1.6 collective-permute-done
  130.6 1.2 copy.111
  131.8 22.4 %time_forward.1 = (bf16[2,896,576]{2,1,0:T(8,128)(2,1)}, bf16[2,896,192]{2,1,0:T(8,128)(2,1)}) custom-call(s32[1]{0:T(128)} %bitcast.14.core_ref, bf16[896,768]{1,0:T(8,128)(2,1)} %bitcast.126, bf16[2,4,768,768]{3,2,1,0:T(8,128)(2,1)} %bitcast.114, f32[896,1]{1,0:T(8,128)} %reshape.245.mask_ref), custom_call_target="tpu_custom_call" | custom-call | tf_op jit(solution)/shard_map/time_forward/pallas_call | solution.py:259
  154.2 1.2 fusion.4
  157.1 3.5 all-to-all-start.1
  161.8 1.4 collective-permute-done.1
  163.2 14.4 %all-to-all-done.1 = bf16[4,2,56,384]{3,2,1,0:T(8,128)(2,1)S(1)} async-done(((bf16[4,2,56,384]{3,2,1,0:T(8,128)(2,1)}), bf16[4,2,56,384]{3,2,1,0:T(8,128)(2,1)S(1)}, u32[]{:S(2)}, u32[]{:S(2)}) %all-to-all-start.1) | async-done | bytes 344096 | tf_op jit(solution)/shard_map/all_to_all | solution.py:829
  177.5 3.5 all-to-all-start.2
  182.1 10.1 %all-to-all-done.2 = bf16[4,2,56,384]{3,2,1,0:T(8,128)(2,1)S(1)} async-done(((bf16[4,2,56,384]{3,2,1,0:T(8,128)(2,1)}), bf16[4,2,56,384]{3,2,1,0:T(8,128)(2,1)S(1)}, u32[]{:S(2)}, u32[]{:S(2)}) %all-to-all-start.2) | async-done | bytes 344096 | tf_op jit(solution)/shard_map/all_to_all | solution.py:829
  192.8 1.5 pad_maximum_fusion.3
  195.3 26.9 %mlp_both.1 = (bf16[448,768]{1,0:T(8,128)(2,1)}, f32[448,768]{1,0:T(8,128)}, bf16[4,448,192]{2,1,0:T(8,128)(2,1)}, bf16[4,4,2,192,768]{4,3,2,1,0:T(8,128)(2,1)},...) custom-call(f32[448,768]{1,0:T(8,128)} %get-tuple-element.52.xs_ref, ...), custom_call_target="tpu_custom_call" | custom-call | tf_op jit(solution)/shard_map/mlp_both/pallas_call | solution.py:259
  225.6 3.5 all-to-all-start.3
  229.4 1.8 collective-permute-done.2
  231.3 8.1 %all-to-all-done.3 = bf16[4,2,56,384]{3,2,1,0:T(8,128)(2,1)S(1)} async-done(((bf16[4,2,56,384]{3,2,1,0:T(8,128)(2,1)}), bf16[4,2,56,384]{3,2,1,0:T(8,128)(2,1)S(1)}, u32[]{:S(2)}, u32[]{:S(2)}) %all-to-all-start.3) | async-done | bytes 344096 | tf_op jit(solution)/shard_map/all_to_all | solution.py:818
  239.4 12.2 %all_to_all.31 = bf16[4,2,56,384]{3,2,1,0:T(8,128)(2,1)S(1)} all-to-all(bf16[4,2,56,384]{3,2,1,0:T(8,128)(2,1)S(1)} %copy.123), channel_id=1, replica_groups=mesh['rep'=2,'frame'=4,'tensor'=4] {'frame'}, dimensions={0} | all-to-all | bytes 688128 | tf_op jit(solution)/shard_map/all_to_all | solution.py:818
  253.3 31.5 %time_backward.1 = (bf16[2,768,576]{2,1,0:T(8,128)(2,1)}, f32[896,768]{1,0:T(8,128)}) custom-call(s32[1]{0:T(128)} %bitcast.14.core_ref, bf16[896,768]{1,0:T(8,128)(2,1)} %bitcast.127, bf16[2,4,768,768]{3,2,1,0:T(8,128)(2,1)} %bitcast.116, f32[896,1]{1,0:T(8,128)} %reshape.245.mask_ref, bf16[2,896,576]{2,1,0:T(8,128)(2,1)} %get-tuple-element.58.qkv_ref, ...), custom_call_target="tpu_custom_call" | custom-call | tf_op jit(solution)/shard_map/time_backward/pallas_call | solution.py:259
  284.8 2.1 copy.150
  287.1 2.0 collective-permute-done.3
  290.1 12.3 %all-to-all-start.5 = ((bf16[4,2,56,768]{3,2,1,0:T(8,128)(2,1)}), bf16[4,2,56,768]{3,2,1,0:T(8,128)(2,1)S(1)}, u32[]{:S(2)}, u32[]{:S(2)}) async-start(bf16[4,2,56,768]{3,2,1,0:T(8,128)(2,1)} %add_convert_fusion), calls=%async_computation.5 | async-start | bytes 1376256 | tf_op jit(solution)/shard_map/all_to_all | solution.py:829
  306.3 3.2 pad_maximum_fusion.refs_1_
  309.6 21.5 %all-to-all-done.5 = bf16[4,2,56,768]{3,2,1,0:T(8,128)(2,1)S(1)} async-done(((bf16[4,2,56,768]{3,2,1,0:T(8,128)(2,1)}), bf16[4,2,56,768]{3,2,1,0:T(8,128)(2,1)S(1)}, u32[]{:S(2)}, u32[]{:S(2)}) %all-to-all-start.5) | async-done | bytes 688160 | tf_op jit(solution)/shard_map/all_to_all | solution.py:829
  331.9 28.3 %space_backward.1 = (bf16[448,768]{1,0:T(8,128)(2,1)}, bf16[4,768,768]{2,1,0:T(8,128)(2,1)}, f32[8,768]{1,0:T(8,128)}) custom-call(bf16[448,768]{1,0:T(8,128)(2,1)} %bitcast.119, f32[448,768]{1,0:T(8,128)} %get-tuple-element.52.xs_ref, f32[448,768]{1,0:T(8,128)} %get-tuple-element.57.gt_ref, bf16[448,768]{1,0:T(8,128)(2,1)} %bitcast.136, ...), custom_call_target="tpu_custom_call" | custom-call | tf_op jit(solution)/shard_map/space_backward/pallas_call | solution.py:259
  362.2 76.7 %reduce_all.1 = (f32[4,192,768]{2,1,0:T(8,128)}, f32[16,128]{1,0:T(8,128)}, bf16[4,2,56,768]{3,2,1,0:T(8,128)(2,1)}, bf16[4,2,56,768]{3,2,1,0:T(8,128)(2,1)}) custom-call(bf16[4,4,192,768]{3,2,1,0:T(8,128)(2,1)} %bitcast.133, bf16[4,4,192,768]{3,2,1,0:T(8,128)(2,1)} %pad_maximum_fusion.refs_1_, bf16[2,192,768]{2,1,0:T(8,128)(2,1)} %bitcast.158, ...), custom_call_target="tpu_custom_call" | custom-call | tf_op jit(solution)/shard_map/reduce_all/pallas_call | solution.py:710
  438.9 1.5 slice.166
  440.4 1.5 fusion.5
  441.9 1.4 slice.165
  443.2 2.2 copy.137
  445.4 2.4 copy_convert_fusion
  (126 shorter events, 37.0 us)
Async XLA Ops:
  7.2 5.6 %copy-start.7 = (bf16[2,4,49,768]{3,1,2,0:T(4,128)(2,1)S(1)}, bf16[2,4,49,768]{3,1,2,0:T(4,128)(2,1)}, u32[]{:S(2)}) copy-start(bf16[2,4,49,768]{3,1,2,0:T(4,128)(2,1)} %param.41) | copy-start | bytes 1806340
  7.2 188.1 %all-gather.3.cloned.1.call-start = ((), (), s32[]{:S(2)}) async-start(), calls=%async_computation.8 | async-start | bytes 10027008 | tf_op jit(solution)/shard_map/all_gather | solution.py:781
  12.8 0.9 copy-start.10
  12.8 0.9 copy-start.11
  12.8 1.0 copy-start.12
  12.8 1.0 copy-start.13
  12.8 1.0 copy-start.14
  12.8 1.1 copy-start.15
  13.0 1.3 copy-start.8
  13.0 1.3 copy-start.9
  14.2 69.3 %copy-start.17 = (s32[196]{0:T(256)S(1)}, s32[196]{0:T(256)}, u32[]{:S(2)}) copy-start(s32[196]{0:T(256)} %param.40) | copy-start | bytes 2356
  78.2 3.6 copy-start
  81.8 0.9 copy-start.1
  82.7 0.9 copy-start.2
  127.7 2.7 collective-permute-start
  157.1 20.4 %all-to-all-start.1 = ((bf16[4,2,56,384]{3,2,1,0:T(8,128)(2,1)}), bf16[4,2,56,384]{3,2,1,0:T(8,128)(2,1)S(1)}, u32[]{:S(2)}, u32[]{:S(2)}) async-start(bf16[4,2,56,384]{3,2,1,0:T(8,128)(2,1)} %squeeze.26), calls=%async_computation.1 | async-start | bytes 688128 | tf_op jit(solution)/shard_map/all_to_all | solution.py:829
  161.3 1.9 collective-permute-start.1
  177.5 14.6 %all-to-all-start.2 = ((bf16[4,2,56,384]{3,2,1,0:T(8,128)(2,1)}), bf16[4,2,56,384]{3,2,1,0:T(8,128)(2,1)S(1)}, u32[]{:S(2)}, u32[]{:S(2)}) async-start(bf16[4,2,56,384]{3,2,1,0:T(8,128)(2,1)} %collective-permute-done.1), calls=%async_computation.2 | async-start | bytes 688128 | tf_op jit(solution)/shard_map/all_to_all | solution.py:829
  181.0 181.2 %reduce-scatter.2.cloned.1.call-start = ((), (), s32[]{:S(2)}) async-start(), calls=%async_computation.7 | async-start | bytes 10027008 | tf_op jit(solution)/shard_map/reduce_scatter | solution.py:886
  222.3 1.2 copy-start.6
  225.6 13.8 %all-to-all-start.3 = ((bf16[4,2,56,384]{3,2,1,0:T(8,128)(2,1)}), bf16[4,2,56,384]{3,2,1,0:T(8,128)(2,1)S(1)}, u32[]{:S(2)}, u32[]{:S(2)}) async-start(bf16[4,2,56,384]{3,2,1,0:T(8,128)(2,1)} %copy.122), calls=%async_computation.3 | async-start | bytes 688128 | tf_op jit(solution)/shard_map/all_to_all | solution.py:818
  229.3 1.9 collective-permute-start.2
  286.9 2.2 collective-permute-start.3
  289.1 14.9 %copy-start.4 = (bf16[2,768,576]{2,1,0:T(8,128)(2,1)S(1)}, bf16[2,768,576]{2,1,0:T(8,128)(2,1)}, u32[]{:S(2)}) copy-start(bf16[2,768,576]{2,1,0:T(8,128)(2,1)} %get-tuple-element.64) | copy-start | bytes 5308420
  290.1 40.9 %all-to-all-start.5 = ((bf16[4,2,56,768]{3,2,1,0:T(8,128)(2,1)}), bf16[4,2,56,768]{3,2,1,0:T(8,128)(2,1)S(1)}, u32[]{:S(2)}, u32[]{:S(2)}) async-start(bf16[4,2,56,768]{3,2,1,0:T(8,128)(2,1)} %add_convert_fusion), calls=%async_computation.5 | async-start | bytes 1376256 | tf_op jit(solution)/shard_map/all_to_all | solution.py:829
  304.9 1.4 copy-start.5
  331.9 29.3 %copy-start.16 = (f32[4,768]{1,0:T(4,128)S(1)}, f32[4,768]{1,0:T(4,128)}, u32[]{:S(2)}) copy-start(f32[4,768]{1,0:T(4,128)} %get-tuple-element.69) | copy-start | bytes 36868
  438.9 8.8 %copy-start.3 = (f32[4,192,768]{2,1,0:T(8,128)S(1)}, f32[4,192,768]{2,1,0:T(8,128)}, u32[]{:S(2)}) copy-start(f32[4,192,768]{2,1,0:T(8,128)} %get-tuple-element.74) | copy-start | bytes 7077892
Sparse Core Ops, SparseCore 0:
  83.7 95.5 all-gather.2
  222.4 118.3 reduce-scatter.1

commit v4 on v3

--- a/solution.py
+++ b/solution.py
@@ -100,7 +100,7 @@
 def space_backward(
     width, heads, frames, rows,
     x_ref, xs_ref, gt_ref, dht_ref, vec_ref, bias_ref, w_ref, qkv_ref, os_ref,
-    gx_ref, gw_ref, sv_ref, h_scr, gs_scr, dat_scr, dh_scr, dqkv_scr,
+    gx_ref, gw_ref, sv_ref, h_scr, gs_scr, dat_scr, dh_scr, dqkv_scr, dos_scr,
 ):
     t = pl.program_id(0)
 
@@ -118,18 +118,22 @@
         dh_scr[...] = jnp.zeros_like(dh_scr)
 
     dat = dat_scr[...]
-    dos = dot(dat, w_ref[0, 0, :, 3 * width :]).astype(BF)
+    dos_scr[...] = dot(dat, w_ref[0, 0, :, 3 * width :]).astype(BF)
     bias = bias_ref[...]
-    for i in range(frames):
-        r = pl.ds(i * rows, rows)
+
+    def frame(i, carry):
+        r = pl.ds(pl.multiple_of(i * rows, 32), rows)
         for h in range(heads):
             a, b, c = (slice(j * width + h * HEAD, j * width + (h + 1) * HEAD) for j in range(3))
             dq, dk, dv = attend_head_back(
-                dos[i * rows : (i + 1) * rows, a], qkv_ref[0, r, a], qkv_ref[0, r, b], qkv_ref[0, r, c], bias
+                dos_scr[r, a], qkv_ref[0, r, a], qkv_ref[0, r, b], qkv_ref[0, r, c], bias
             )
             dqkv_scr[r, a] = dq
             dqkv_scr[r, b] = dk
             dqkv_scr[r, c] = dv
+        return carry
+
+    lax.fori_loop(0, frames, frame, 0)
     dqkv = dqkv_scr[...]
     gw_ref[0, :, : 3 * width] = dot(h_scr[...], dqkv, TN).astype(BF)
     gw_ref[0, :, 3 * width :] = dot(dat, os_ref[0], TN).astype(BF)
@@ -167,50 +171,74 @@
 
 
 def time_backward(
-    width, heads, groups, size, places, core_ref, h_ref, w_ref, mask_ref, qkv_ref, do_ref, gw_ref, dh_ref, dqkv_scr
+    width, heads, groups, size, places,
+    core_ref, h_ref, w_ref, mask_ref, qkv_ref, do_ref, gwt_ref, gw_ref, dh_ref, dqkv_scr,
 ):
-    bias = group_bias(size, places)
-
-    def one(g, carry):
-        r = pl.ds(pl.multiple_of(g * size, size), size)
-        keep = mask_ref[r, :]
-        for h in range(heads):
-            a, b, c = (slice(j * width + h * HEAD, j * width + (h + 1) * HEAD) for j in range(3))
-            do = jnp.where(keep > 0, do_ref[0, r, a].astype(F32), 0.0).astype(BF)
-            dq, dk, dv = attend_head_back(do, qkv_ref[0, r, a], qkv_ref[0, r, b], qkv_ref[0, r, c], bias)
-            dqkv_scr[r, a] = dq
-            dqkv_scr[r, b] = dk
-            dqkv_scr[r, c] = dv
+    t = pl.program_id(0)
+    part = gw_ref.shape[1] // 8
+
+    def carry_over(i, carry):
+        r = pl.ds(pl.multiple_of(i * part, part), part)
+        gw_ref[0, r, 3 * width :] = gwt_ref[0, r]
         return carry
 
-    lax.fori_loop(0, groups, one, 0)
-    dqkv = dqkv_scr[...]
-    gw_ref[0] = dot(h_ref[...], dqkv, TN).astype(BF)
-    dh = dot(dqkv, w_ref[0, 0, :, : 3 * width], NT)
-
-    @pl.when(pl.program_id(0) == 0)
+    lax.fori_loop(0, 8, carry_over, 0)
+
+    @pl.when(t % 2 != core_ref[0])
     def _():
-        dh_ref[...] = dh
-
-    @pl.when(pl.program_id(0) > 0)
+        def clear(i, carry):
+            r = pl.ds(pl.multiple_of(i * part, part), part)
+            gw_ref[0, r, : 3 * width] = jnp.zeros((part, 3 * width), BF)
+            return carry
+
+        lax.fori_loop(0, 8, clear, 0)
+
+    @pl.when(t % 2 == core_ref[0])
     def _():
-        dh_ref[...] += dh
+        bias = group_bias(size, places)
+
+        def one(g, carry):
+            r = pl.ds(pl.multiple_of(g * size, size), size)
+            keep = mask_ref[r, :]
+            for h in range(heads):
+                a, b, c = (slice(j * width + h * HEAD, j * width + (h + 1) * HEAD) for j in range(3))
+                do = jnp.where(keep > 0, do_ref[0, r, a].astype(F32), 0.0).astype(BF)
+                dq, dk, dv = attend_head_back(do, qkv_ref[0, r, a], qkv_ref[0, r, b], qkv_ref[0, r, c], bias)
+                dqkv_scr[r, a] = dq
+                dqkv_scr[r, b] = dk
+                dqkv_scr[r, c] = dv
+            return carry
+
+        lax.fori_loop(0, groups, one, 0)
+        dqkv = dqkv_scr[...]
+        gw_ref[0, :, : 3 * width] = dot(h_ref[...], dqkv, TN).astype(BF)
+        dh = dot(dqkv, w_ref[0, 0, :, : 3 * width], NT)
+
+        dh_ref[...] = dh + jnp.where(t < 2, 0.0, dh_ref[...])
 
 
 def mlp_both(
-    width, tensors,
-    xs_ref, cot_ref, ot_ref, vec_ref, bin_ref, wt_ref, win_ref, wout_ref,
+    width, halves,
+    core_ref, xs_ref, cot_ref, ot_ref, vec_ref, bin_ref, wt_ref, win_ref, wout_ref,
     res_ref, gt_ref, do_ref, gg_ref, gwt_ref, sv_ref, gb_ref,
     xt_scr, hm_scr, xm_scr, dhm_scr,
 ):
     t = pl.program_id(0)
 
+    def each_core(fn):
+        lax.fori_loop(0, 2, lambda c, carry: fn(c, jnp.where(c == core_ref[0], 0, 1)) or carry, 0)
+
     @pl.when(t == 0)
     def _():
-        xt = xs_ref[...]
-        for j in range(tensors):
-            xt = xt + dot(ot_ref[j], wt_ref[0, j, :, 3 * width :], NT)
-        xt_scr[...] = xt
+        xt_scr[...] = xs_ref[...]
+
+        def add(c, rel):
+            for i in range(halves):
+                cols = slice(i * width, (i + 1) * width)
+                xt_scr[...] += dot(ot_ref[rel, :, cols], wt_ref[0, 2 * i + c, :, 3 * width :], NT)
+
+        each_core(add)
+        xt = xt_scr[...]
         hm_scr[...] = norm(xt, vec_ref[4:5, :], vec_ref[5:6, :]).astype(BF)
         xm_scr[...] = xt + vec_ref[6:7, :]
         dhm_scr[...] = jnp.zeros_like(dhm_scr)
@@ -241,9 +269,14 @@
         gt = gm + dx
         gt_ref[...] = gt
         dat = gt.astype(BF)
-        for j in range(tensors):
-            do_ref[j] = dot(dat, wt_ref[0, j, :, 3 * width :]).astype(BF)
-            gwt_ref[j] = dot(dat, ot_ref[j], TN).astype(BF)
+
+        def back(c, rel):
+            for i in range(halves):
+                cols = slice(i * width, (i + 1) * width)
+                do_ref[rel, :, cols] = dot(dat, wt_ref[0, 2 * i + c, :, 3 * width :]).astype(BF)
+                gwt_ref[2 * i + c] = dot(dat, ot_ref[rel, :, cols], TN).astype(BF)
+
+        each_core(back)
         sv_ref[...] = jnp.zeros_like(sv_ref)
         sv_ref[0:1, :] = dg
         sv_ref[1:2, :] = db
@@ -300,7 +333,7 @@
         pltpu.make_async_copy(src, dst, rl.at[n]).wait()
 
 
-def gather_kernel(F, T, K, KS, w_ref, s_ref, a_ref, b_ref, W_ref, S_ref, ao_ref, bo_ref, loc_sem, zs, zr, ys, yr, xs, xr, cs, cr, ss, sr, rs, rr, rl):
+def gather_kernel(F, T, K, KS, w_ref, s_ref, a_ref, W_ref, S_ref, ao_ref, loc_sem, zs, zr, ys, yr, xs, xr, cs, cr, ss, sr, rs, rr, rl):
     r, f, t = lax.axis_index("rep"), lax.axis_index("frame"), lax.axis_index("tensor")
     rows = w_ref.shape[1]
     half = rows // 2
@@ -434,7 +467,7 @@
             if d > 0:
                 x_step(k, d - 1)
         if d == 1:
-            rows_start(T, t, rc, (a_ref, b_ref), (ao_ref, bo_ref), True, rs, rr, rl)
+            rows_start(T, t, rc, (a_ref,), (ao_ref,), True, rs, rr, rl)
             for dd in range(1, F):
                 def fn(src, sign):
                     rc(s_ref, S_ref.at[t, src], ss.at[src], sr.at[src], frame=f).wait_recv()
@@ -446,7 +479,7 @@
             rc(S_ref.at[ypart], S_ref.at[ypart], ss.at[F + 2], sr.at[F + 2], tensor=core).start()
     for k in range(K):
         x_step(k, F - 1)
-    rows_wait(T, t, rc, (a_ref, b_ref), (ao_ref, bo_ref), True, rs, rr, rl)
+    rows_wait(T, t, rc, (a_ref,), (ao_ref,), True, rs, rr, rl)
     ct, cy = core, core ^ 2
     for k in range(K):
         pltpu.make_async_copy(w_ref.at[k], W_ref.at[k, t, f], loc_sem.at[k]).wait()
@@ -488,35 +521,35 @@
     rc(S_ref.at[cy], S_ref.at[cy], ss.at[F + 2], sr.at[F + 2], tensor=core).wait_recv()
 
 
-def gather_all(wl, small, a, b):
+def gather_all(wl, small, a):
     F, T = lax.axis_size("frame"), lax.axis_size("tensor")
     K, rows, D = wl.shape
     dma = pltpu.SemaphoreType.DMA
-    any_spec = pl.BlockSpec(memory_space=pl.ANY)
+    hbm = pl.BlockSpec(memory_space=pltpu.HBM)
     owned = (a.shape[1], a.shape[0]) + a.shape[2:]
     sds = jax.ShapeDtypeStruct
     return pl.pallas_call(
         partial(gather_kernel, F, T, K, KS),
         out_shape=(
             sds((K, T, F, rows, D), wl.dtype), sds((T, F) + small.shape, small.dtype),
-            sds(owned, a.dtype), sds(owned, b.dtype),
+            sds(owned, a.dtype),
         ),
-        in_specs=[pl.BlockSpec(memory_space=pltpu.VMEM)] * 4,
-        out_specs=(any_spec,) * 4,
+        in_specs=[pl.BlockSpec(memory_space=pltpu.VMEM)] * 3,
+        out_specs=(hbm,) * 3,
         scratch_shapes=[
             dma((K + 1,)), dma((K, F, 2)), dma((K, F)), dma((K, F)), dma((K, F)), dma((2 * K, F)), dma((2 * K, F)),
-            dma((5, K, F)), dma((5, K, F)), dma((F + 3,)), dma((F + 3,)), dma((2, T)), dma((2, T)), dma((2,)),
+            dma((5, K, F)), dma((5, K, F)), dma((F + 3,)), dma((F + 3,)), dma((1, T)), dma((1, T)), dma((1,)),
         ],
-        compiler_params=pltpu.CompilerParams(collective_id=0, has_side_effects=True, vmem_limit_bytes=16 * 1024 * 1024),
+        compiler_params=pltpu.CompilerParams(collective_id=0, has_side_effects=True, vmem_limit_bytes=62 * 1024 * 1024),
         name="gather_all",
-    )(wl, small, a, b)
+    )(wl, small, a)
 
 
 def reduce_kernel(F, T, G, split, *refs):
-    g_refs, h_ref, s_ref, a_ref, b_ref = refs[:G], *refs[G : G + 4]
-    out_ref, sout_ref, ao_ref, bo_ref = refs[G + 4 : G + 8]
+    g_refs, h_ref, s_ref, a_ref = refs[:G], *refs[G : G + 3]
+    out_ref, sout_ref, ao_ref = refs[G + 3 : G + 6]
     (acc, cin, xin, yin, zdn, zup, fin, sacc, scin, sxin, syin, szin,
-     lsem, cs, cr, xs, xr, ys, yr, zs, zr, fs, fr_, ss, sr, rs, rr, rl, hin, hs, hr) = refs[G + 8 :]
+     lsem, cs, cr, xs, xr, ys, yr, zs, zr, fs, fr_, ss, sr, rs, rr, rl, hin, hs, hr) = refs[G + 6 :]
     K = G * split
     r, f, t = lax.axis_index("rep"), lax.axis_index("frame"), lax.axis_index("tensor")
     rows = acc.shape[3]
@@ -605,7 +638,6 @@
         for j in (1, 0):
             c_copy(k, j).start()
             load(k, j).start()
-    rows_start(T, t, rc, (a_ref, b_ref), (ao_ref, bo_ref), False, rs, rr, rl)
 
     def add(k, j):
         c_copy(k, j).wait_recv()
@@ -652,17 +684,10 @@
         for hop in range(1, F):
             @pl.when(f == F - 1 - hop)
             def _():
-                for dst in range(F):
-                    @pl.when(dst <= f)
-                    def _():
-                        take(k, dst, True)
+                lax.fori_loop(0, F - hop, lambda dst, c: take(k, dst, True) or c, 0)
             @pl.when(f == hop)
             def _():
-                for up in range(F):
-                    dst = F - 1 - up
-                    @pl.when(dst >= f)
-                    def _():
-                        take(k, dst, False)
+                lax.fori_loop(0, F - hop, lambda i, c: take(k, F - 1 - i, False) or c, 0)
         fin_copy(k).start()
 
     def step_e(k):
@@ -677,12 +702,14 @@
                 fn(s - i)
         if s < 5:
             small_step(s)
+        if s == 1:
+            rows_start(T, t, rc, (a_ref,), (ao_ref,), False, rs, rr, rl)
         if s == K - 1:
             pair_copy().start()
     pair_copy().wait()
     for i in range(h_ref.shape[0]):
         out_ref[G + i] = h_ref[i].astype(F32) + hin[i].astype(F32)
-    rows_wait(T, t, rc, (a_ref, b_ref), (ao_ref, bo_ref), False, rs, rr, rl)
+    rows_wait(T, t, rc, (a_ref,), (ao_ref,), False, rs, rr, rl)
     for k in range(K):
         for j in (1, 0):
             c_copy(k, j).wait_send()
@@ -695,7 +722,7 @@
                 z_copy(k, dst, False).wait_send()
 
 
-def reduce_all(grads, half, small, a, b):
+def reduce_all(grads, half, small, a):
     F, T = lax.axis_size("frame"), lax.axis_size("tensor")
     G = len(grads)
     K = G * SPLIT
@@ -709,25 +736,165 @@
     split_rows = (a.shape[1], a.shape[0]) + a.shape[2:]
     return pl.pallas_call(
         partial(reduce_kernel, F, T, G, SPLIT),
-        out_shape=(sds((G + half.shape[0], full, D), F32), sds(sm, F32), sds(split_rows, a.dtype), sds(split_rows, b.dtype)),
-        in_specs=[any_spec] * G + [vmem] * 4,
-        out_specs=(vmem, vmem, any_spec, any_spec),
+        out_shape=(sds((G + half.shape[0], full, D), F32), sds(sm, F32), sds(split_rows, a.dtype)),
+        in_specs=[any_spec] * G + [vmem] * 3,
+        out_specs=(vmem, vmem, any_spec),
         scratch_shapes=[
             V((K, 2, F, rows, D), BF), V((K, 2, F, rows, D), BF), V((K, F, rows // 2, D), BF), V((K, F, rows // 2, D), BF),
             V((K, F, rows, D), BF), V((K, F, rows, D), BF), V((K, rows, D), BF),
             V((2, F) + sm, F32), V((2, F) + sm, F32), V((2, F) + sm, F32), V((F,) + sm, F32), V((F,) + sm, F32),
             dma((K, 2)), dma((K, 2)), dma((K, 2)), dma((K,)), dma((K,)), dma((K,)), dma((K,)),
             dma((K, F)), dma((K, F, 2)), dma((K,)), dma((K,)), dma((3 + F,)), dma((3 + F,)),
-            dma((2, T)), dma((2, T)), dma((2,)), V(half.shape, BF), dma(()), dma(()),
+            dma((1, T)), dma((1, T)), dma((1,)), V(half.shape, BF), dma(()), dma(()),
         ],
         compiler_params=pltpu.CompilerParams(collective_id=1, has_side_effects=True, vmem_limit_bytes=62 * 1024 * 1024),
         name="reduce_all",
-    )(*grads, half, small.reshape((2, T // 2, F) + sm).astype(F32), a, b)
-
-
-def swap_core(v):
-    size = lax.axis_size("tensor")
-    return lax.ppermute(v, "tensor", [(i, i ^ 1) for i in range(size)])
+    )(*grads, half, small.reshape((2, T // 2, F) + sm).astype(F32), a)
+
+
+def remote(src, dst, ssem, rsem, **dev):
+    return pltpu.make_async_remote_copy(src, dst, ssem, rsem, device_id=dev, device_id_type=MESH)
+
+
+def others(F, f, fn):
+    for d in range(F - 1, 0, -1):
+        for to in (f - d, f + d):
+            pl.when((to >= 0) & (to < F))(partial(fn, to))
+
+
+def greet(F, T, f, t, cores):
+    bar = pltpu.get_barrier_semaphore()
+
+    def signal(to, tt):
+        pl.semaphore_signal(bar, inc=1, device_id={"frame": to, "tensor": tt}, device_id_type=MESH)
+
+    for j in range(cores):
+        others(F, f, lambda to: signal(to, t ^ j))
+    for p in range(1, T):
+        signal(f, t ^ p)
+    pl.semaphore_wait(bar, cores * (F - 1) + T - 1)
+
+
+def rows_to_both(F, T, s_ref, a_ref, o_ref, ao_ref, zs, zr, cs, cr, ls, rs, rr, rl):
+    f, t = lax.axis_index("frame"), lax.axis_index("tensor")
+    greet(F, T, f, t, 1)
+
+    def z_copy(to, frm):
+        return remote(s_ref.at[:, to], o_ref.at[0, frm], zs.at[to], zr.at[frm], frame=to)
+
+    def c_copy(frm):
+        return remote(o_ref.at[0, frm], o_ref.at[1, frm], cs.at[frm], cr.at[frm], tensor=t ^ 1)
+
+    others(F, f, lambda to: z_copy(to, f).start())
+    rows_start(T, t, remote, (a_ref,), (ao_ref,), True, rs, rr, rl)
+    own = remote(s_ref.at[:, f], o_ref.at[1, f], cs.at[f], cr.at[f], tensor=t ^ 1)
+    own.start()
+    local = pltpu.make_async_copy(s_ref.at[:, f], o_ref.at[0, f], ls)
+    local.start()
+
+    def arrive(frm):
+        z_copy(frm, frm).wait_recv()
+        c_copy(frm).start()
+
+    others(F, f, arrive)
+
+    def finish(frm):
+        z_copy(frm, f).wait_send()
+        c_copy(frm).wait_send()
+        c_copy(frm).wait_recv()
+
+    others(F, f, finish)
+    rows_wait(T, t, remote, (a_ref,), (ao_ref,), True, rs, rr, rl)
+    own.wait()
+    local.wait()
+
+
+def cross(F, T, to_frames, *refs):
+    if to_frames:
+        s_ref, o_ref, ss, sr, ls = refs
+    else:
+        s_ref, a_ref, o_ref, ao_ref, ss, sr, ls, *row_sems = refs
+    f, t = lax.axis_index("frame"), lax.axis_index("tensor")
+    greet(F, T, f, t, 2)
+
+    def src(j, to):
+        return s_ref.at[j, to] if to_frames else s_ref.at[j, :, to]
+
+    def dst(j, frm):
+        return o_ref.at[j, :, frm] if to_frames else o_ref.at[j, frm]
+
+    def copy(j, to, frm):
+        return remote(src(j, to), dst(j, frm), ss.at[j, to], sr.at[j, frm], frame=to, tensor=t ^ j)
+
+    for j in (1, 0):
+        others(F, f, lambda to: copy(j, to, f).start())
+    copy(1, f, f).start()
+    if not to_frames:
+        rows_start(T, t, remote, (a_ref,), (ao_ref,), False, *row_sems)
+    local = pltpu.make_async_copy(src(0, f), dst(0, f), ls)
+    local.start()
+
+    def finish(j, frm):
+        copy(j, frm, f).wait_send()
+        copy(j, frm, frm).wait_recv()
+
+    for j in (1, 0):
+        others(F, f, partial(finish, j))
+    if not to_frames:
+        rows_wait(T, t, remote, (a_ref,), (ao_ref,), False, *row_sems)
+    copy(1, f, f).wait()
+    local.wait()
+
+
+def sum_to_frames(F, T, a_ref, b_ref, o_ref, cin, buf, cs, cr, zs, zr, ls):
+    f, t = lax.axis_index("frame"), lax.axis_index("tensor")
+    greet(F, T, f, t, 1)
+
+    def c_copy(to):
+        return remote(b_ref.at[to], cin.at[to], cs.at[to], cr.at[to], tensor=t ^ 1)
+
+    def z_copy(to, frm):
+        return remote(buf.at[to], o_ref.at[:, frm], zs.at[to], zr.at[frm], frame=to)
+
+    def add(to):
+        c_copy(to).wait_recv()
+        @pl.loop(0, buf.shape[1])
+        def _(i):
+            buf[to, i] = (a_ref[to, i] + cin[to, i].astype(F32)).astype(BF)
+
+    def send(to):
+        add(to)
+        z_copy(to, f).start()
+
+    others(F, f, lambda to: c_copy(to).start())
+    c_copy(f).start()
+    others(F, f, send)
+    add(f)
+    local = pltpu.make_async_copy(buf.at[f], o_ref.at[:, f], ls)
+    local.start()
+
+    def finish(frm):
+        c_copy(frm).wait_send()
+        z_copy(frm, f).wait_send()
+        z_copy(frm, frm).wait_recv()
+
+    others(F, f, finish)
+    c_copy(f).wait_send()
+    local.wait()
+
+
+def exchange(body, ins, out_shapes, scratch, collective_id, name):
+    return pl.pallas_call(
+        body,
+        out_shape=tuple(jax.ShapeDtypeStruct(s, BF) for s in out_shapes),
+        in_specs=[pl.BlockSpec(memory_space=pltpu.VMEM)] * len(ins),
+        out_specs=(pl.BlockSpec(memory_space=pltpu.HBM),) * len(out_shapes),
+        scratch_shapes=scratch,
+        compiler_params=pltpu.CompilerParams(
+            collective_id=collective_id, has_side_effects=True, vmem_limit_bytes=62 * 1024 * 1024
+        ),
+        name=name,
+    )(*ins)
 
 
 def shards(
@@ -775,12 +942,12 @@
         v = jnp.pad(v, ((0, 0), (0, 0), (0, PAD - places_dev), (0, 0)))
         return v.reshape(T, fr, PAD, D)
 
-    W, small_all, x, cot = gather_all(wl, lanes(small), split_places(tokens), split_places(cotangent))
+    W, small_all, x = gather_all(wl, lanes(small), split_places(tokens))
     FT = ("frame", "tensor")
     W, wl_mlp = lax.optimization_barrier((W, jnp.stack((mlp_in, mlp_out.T))))
     W_mlp = lax.all_gather(wl_mlp, FT, axis=0, tiled=False).reshape(F, T, 2, rows_w, D)
     W = W.reshape(2, T, F * rows_w, D)
-    x, cot = x.reshape(R, D), cot.reshape(R, D)
+    x = x.reshape(R, D)
     small_all = small_all.reshape(T, F, -1)
     nv = 7 * gain_first.shape[0]
     vec = small_all[:, :, :nv].reshape(T, F, 7, -1).transpose(2, 1, 0, 3).reshape(7, D)
@@ -813,10 +980,6 @@
     size = nf * 8
     RT = groups * size
 
-    def to_time(own):
-        v = own.transpose(1, 0, 2, 3)
-        return lax.all_to_all(v, "frame", split_axis=0, concat_axis=0, tiled=True)
-
     def group_rows(a, b):
         v = jnp.stack((a, b)).reshape(nf, groups, 8, a.shape[-1])
         return v.transpose(1, 0, 2, 3).reshape(RT, a.shape[-1])
@@ -825,12 +988,18 @@
         n = v.shape[-1]
         return v.reshape(groups, nf, 8, n).transpose(1, 0, 2, 3).reshape(2, F, fr, PAD, n)
 
-    def to_frames(v):
-        v = lax.all_to_all(v, "frame", split_axis=0, concat_axis=0, tiled=True)
-        return v.transpose(1, 0, 2, 3).reshape(R, v.shape[-1])
-
-    h_own = to_time(ht.reshape(fr, T, PAD, D))
-    h_t = group_rows(h_own, swap_core(h_own))
+    dma = pltpu.SemaphoreType.DMA
+    row_sems = [dma((1, T)), dma((1, T)), dma((1,))]
+    h_both, cot = exchange(
+        partial(rows_to_both, F, T),
+        (ht.reshape(fr, F, PAD, D), split_places(cotangent)),
+        ((2, F, fr, PAD, D), (fr, T, PAD, D)),
+        [dma((F,)), dma((F,)), dma((F,)), dma((F,)), dma(())] + row_sems,
+        2,
+        "rows_to_both",
+    )
+    cot = cot.reshape(R, D)
+    h_t = group_rows(h_both[0], h_both[1])
     keep_q = lax.dynamic_slice(
         jnp.pad(keep.astype(F32).reshape(T, places_dev), ((0, 0), (0, PAD - places_dev))), (f_id, 0), (1, PAD)
     )
@@ -852,61 +1021,70 @@
     )
     ot_u = jnp.stack([ungroup_rows(ot[i]) for i in range(halves)], axis=-2)
     ot_u = ot_u.reshape(2, F, fr, PAD, halves * width)
-    ot_mine, ot_other = to_frames(ot_u[0]), to_frames(swap_core(ot_u[1]))
-
-    def by_tensor(mine, other):
-        m = mine.reshape(R, halves, width)
-        o = other.reshape(R, halves, width)
-        first = jnp.where(core == 0, m, o)
-        second = jnp.where(core == 0, o, m)
-        return jnp.stack((first, second), axis=2).reshape(R, T, width).transpose(1, 0, 2)
-
-    ot_all = by_tensor(ot_mine, ot_other)
-    win_spec = lambda kind: pl.BlockSpec((F, 1, 1, rows_w, D), lambda t: (0, t, kind, 0, 0))
-    res, gt, dot_all, g_mlp, g_wt, sv_m, gb = call(
-        partial(mlp_both, width, T),
+    cross_sems = [dma((2, F)), dma((2, F)), dma(())]
+    (ot_both,) = exchange(
+        partial(cross, F, T, True), (ot_u,), ((2, fr, F, PAD, halves * width),), cross_sems, 3, "ot_to_frames"
+    )
+    win_spec = lambda kind: pl.BlockSpec((F, 1, 1, rows_w, D), lambda t, c: (0, t, kind, 0, 0))
+    res, gt, dot_both, g_mlp, g_wt, sv_m, gb = call(
+        partial(mlp_both, width, halves),
         T,
-        (xs, cot, ot_all, vec, bin_all, W, W_mlp, W_mlp),
+        (core_arr, xs, cot, ot_both.reshape(2, R, halves * width), vec, bin_all, W, W_mlp, W_mlp),
         [
-            whole((R, D)), whole((R, D)), whole((T, R, width)), whole((8, D)), whole((T, hid)),
-            pl.BlockSpec((1, T, D, D), lambda t: (1, 0, 0, 0)), win_spec(0), win_spec(1),
+            whole((R, D)), whole((R, D)), whole((2, R, halves * width)), whole((8, D)), whole((T, hid)),
+            pl.BlockSpec((1, T, D, D), lambda t, c: (1, 0, 0, 0)), win_spec(0), win_spec(1),
         ],
         [
-            ((R, D), BF), ((R, D), F32), ((T, R, width), BF), ((F, T, 2, rows_w, D), BF),
+            ((R, D), BF), ((R, D), F32), ((2, R, halves * width), BF), ((F, T, 2, rows_w, D), BF),
             ((T, D, width), BF), ((8, D), F32), ((T, hid), F32),
         ],
         [
-            whole((R, D)), whole((R, D)), whole((T, R, width)),
-            pl.BlockSpec((F, 1, 2, rows_w, D), lambda t: (0, t, 0, 0, 0)),
+            whole((R, D)), whole((R, D)), whole((2, R, halves * width)),
+            pl.BlockSpec((F, 1, 2, rows_w, D), lambda t, c: (0, t, 0, 0, 0)),
             whole((T, D, width)), whole((8, D)), whole((T, hid)),
         ],
         [pltpu.VMEM((R, D), F32), pltpu.VMEM((R, D), BF), pltpu.VMEM((R, D), F32), pltpu.VMEM((R, D), F32)],
+        prefetch=1,
         name="mlp_both",
     )
     share_mlp = lax.psum_scatter(
         g_mlp.reshape(F * T, 2, rows_w, D), FT, scatter_dimension=0, tiled=False
     )
-    d = dot_all.reshape(halves, 2, R, width)
-    d_mine = jnp.where(core == 0, d[:, 0], d[:, 1])
-    d_other = jnp.where(core == 0, d[:, 1], d[:, 0])
-    as_frames = lambda v: v.transpose(1, 0, 2).reshape(fr, T, PAD, halves * width)
-    d_own = to_time(as_frames(d_mine))
-    d_par = to_time(swap_core(as_frames(d_other)))
-    d_t = group_rows(d_own, d_par).reshape(RT, halves, width).transpose(1, 0, 2)
+    d_both, res_rows = exchange(
+        partial(cross, F, T, False),
+        (dot_both.reshape(2, fr, F, PAD, halves * width), res.reshape(fr, T, PAD, D)),
+        ((2, F, fr, PAD, halves * width), (T, fr, PAD, D)),
+        cross_sems + row_sems,
+        4,
+        "dot_to_time",
+    )
+    d_t = group_rows(d_both[0], d_both[1]).reshape(RT, halves, width).transpose(1, 0, 2)
     g_time, dh_part = call(
         partial(time_backward, width, heads, groups, size, 8),
-        halves,
-        (core_arr, h_t, W, mask, qkv_t, d_t),
-        [whole((RT, D)), time_w, whole((RT, 1)), per_half(3 * width), per_half(width)],
-        [((halves, D, 3 * width), BF), ((RT, D), F32)],
-        [pl.BlockSpec((1, D, 3 * width), lambda i, c: (i, 0, 0)), whole((RT, D))],
+        T,
+        (core_arr, h_t, W, mask, qkv_t, d_t, g_wt),
+        [
+            whole((RT, D)), pl.BlockSpec((1, 1, D, D), lambda t, c: (1, c[0] + 2 * (t // 2), 0, 0)), whole((RT, 1)),
+            pl.BlockSpec((1, RT, 3 * width), lambda t, c: (t // 2, 0, 0)),
+            pl.BlockSpec((1, RT, width), lambda t, c: (t // 2, 0, 0)),
+            pl.BlockSpec((1, D, width), lambda t, c: (t, 0, 0)),
+        ],
+        [((T, D, D), BF), ((RT, D), F32)],
+        [pl.BlockSpec((1, D, D), lambda t, c: (t, 0, 0)), whole((RT, D))],
         [pltpu.VMEM((RT, 3 * width), BF)],
         prefetch=1,
         name="time_backward",
     )
     dh_u = ungroup_rows(dh_part)
-    dh_sum = (dh_u[0] + swap_core(dh_u[1].astype(BF)).astype(F32)).astype(BF)
-    dht = to_frames(dh_sum)
+    (dht,) = exchange(
+        partial(sum_to_frames, F, T),
+        (dh_u[0], dh_u[1].astype(BF)),
+        ((fr, F, PAD, D),),
+        [pltpu.VMEM((F, fr, PAD, D), BF)] * 2 + [dma((F,)), dma((F,)), dma((F,)), dma((F,)), dma(())],
+        5,
+        "sum_to_frames",
+    )
+    dht = dht.reshape(R, D)
 
     gx, g_space, sv_s = call(
         partial(space_backward, width, heads, fr, rows),
@@ -922,16 +1100,11 @@
         [whole((R, D)), pl.BlockSpec((1, D, D), lambda t: (t, 0, 0)), whole((8, D))],
         [
             pltpu.VMEM((R, D), BF), pltpu.VMEM((R, D), F32), pltpu.VMEM((R, D), BF), pltpu.VMEM((R, D), F32),
-            pltpu.VMEM((R, 3 * width), BF),
+            pltpu.VMEM((R, 3 * width), BF), pltpu.VMEM((R, width), BF),
         ],
         name="space_backward",
     )
-    zero = jnp.zeros_like(g_time)
-    g_first = jnp.where(core == 0, g_time, zero)
-    g_second = jnp.where(core == 0, zero, g_time)
-    g_qkv = jnp.stack((g_first, g_second), axis=1).reshape(T, D, 3 * width)
-    kinds = (g_space, jnp.concatenate((g_qkv, g_wt), axis=2))
-    kinds = tuple(g.reshape(T, F, rows_w, D) for g in kinds)
+    kinds = tuple(g.reshape(T, F, rows_w, D) for g in (g_space, g_time))
     n = gain_first.shape[0]
     nb = bias_out.shape[0]
     norms = jnp.concatenate((sv_s[0:4], sv_m[0:2]), axis=0).reshape(6, F, T, n).transpose(2, 1, 0, 3)
@@ -943,9 +1116,7 @@
         ),
         axis=2,
     )
-    share, smalls, res_rows, gx_rows = reduce_all(
-        kinds, share_mlp, lanes(small_g), res.reshape(fr, T, PAD, D), gx.reshape(fr, T, PAD, D)
-    )
+    share, smalls, gx_rows = reduce_all(kinds, share_mlp, lanes(small_g), gx.reshape(fr, T, PAD, D))
     reps = lax.axis_size("rep")
     if reps > 2:
         share, smalls = (lax.psum(0.5 * v, "rep") for v in (share, smalls))

time: 460 us -> 423 us (0.920)
  Pallas kernels: 263 us -> 361 us
  waiting for transfers between devices: 60.9 us -> 1.18 us
  blocking collectives: 39.8 us -> 0 us
  starting transfers between devices: 23.6 us -> 0.08 us
  other arithmetic: 13.3 us -> 7.21 us
  local copies, waits for them, and re-layouts: 44.4 us -> 38.5 us
    pallas_call x0 -> x4, Pallas kernels: none -> 90.7 us  [exchange(): pl.pallas_call(body, out_shape=tuple((jax.ShapeDtypeStruct(s, BF) for s i...]
    all_to_all x4 -> x0, waiting for transfers between devices: 54 us -> none  [the longest x3 45.9 us: to_frames(): v = lax.all_to_all(v, 'frame', split_axis=0, concat_axis=0, tiled=True)]
    all_to_all x2 -> x0, blocking collectives: 39.8 us -> none  [to_time(): return lax.all_to_all(v, 'frame', split_axis=0, concat_axis=0, tiled=True)]
    all_to_all x4 -> x0, starting transfers between devices: 22.6 us -> none  [the longest x3 19.2 us: to_frames(): v = lax.all_to_all(v, 'frame', split_axis=0, concat_axis=0, tiled=True)]
    unnamed x43 -> x19, local copies, waits for them, and re-layouts: 15.4 us -> 5.86 us
    pallas_call x5, Pallas kernels: 123 us -> 130 us  [call(): pl.pallas_call(body, out_shape=tuple((jax.ShapeDtypeStruct(s, d) for s, d...]
    ppermute x4 -> x0, waiting for transfers between devices: 6.84 us -> none  [swap_core(): return lax.ppermute(v, 'tensor', [(i, i ^ 1) for i in range(size)])]
    pallas_call x1, Pallas kernels: 76.7 us -> 81.6 us  [reduce_all(): pl.pallas_call(partial(reduce_kernel, F, T, G, SPLIT), out_shape=(sds((G...]
  transfers between devices with their start and end apart: 10 -> 2, of which waited for: 8 -> 1; matrix products, arithmetic and copies ran while one was open for 6% -> 5% of each run, Pallas kernels for 21% -> 46%
where the time goes in v4:
time: 423 us; the launch traced here: 422 us
  Pallas kernels  361 us (85%)
  local copies, waits for them, and re-layouts  38.5 us (9%)
  between operations  14.4 us (3%)
  other arithmetic  7.21 us (2%)
    pallas_call x5, Pallas kernels, call(): pl.pallas_call(body, out_shape=tuple((jax.ShapeDtypeStruct(s, d) for s, d...  130 us
    pallas_call x4, Pallas kernels, exchange(): pl.pallas_call(body, out_shape=tuple((jax.ShapeDtypeStruct(s, BF) for s i...  90.7 us
    pallas_call x1, Pallas kernels, reduce_all(): pl.pallas_call(partial(reduce_kernel, F, T, G, SPLIT), out_shape=(sds((G...  81.6 us
    pallas_call x1, Pallas kernels, gather_all(): pl.pallas_call(partial(gather_kernel, F, T, K, KS), out_shape=(sds((K, T,...  58.7 us
  transfers between devices with their start and end apart: 2, of which 1 were waited for; matrix products, arithmetic and copies ran while one was open for 5% of the time, Pallas kernels for 46%

profile of v4, /device:TPU:0, one launch (start us, length us, event | category | flops | bytes accessed | tf_op | source)
XLA Modules:
  0.0 422.4 jit_solution(7965295528068699609)
XLA Ops:
  10.2 1.0 copy.73
  11.2 1.0 copy.74
  12.2 1.1 copy.94
  13.4 1.4 maximum_bitcast_fusion
  17.4 58.7 %gather_all.1 = (bf16[2,4,4,192,768]{4,3,2,1,0:T(8,128)(2,1)}, f32[4,4,8,128]{3,2,1,0:T(8,128)}, bf16[2,4,56,768]{3,2,1,0:T(8,128)(2,1)}) custom-call(bf16[2,192,768]{2,1,0:T(8,128)(2,1)} %pad_maximum_fusion.1.w_ref, f32[8,128]{1,0:T(8,128)} %pad_bitcast_fusion.s_ref, bf16[4,2,56,768]{3,2,1,0:T(8,128)(2,1)} %bitcast.103), custom_call_target="tpu_custom_call" | custom-call | tf_op jit(solution)/shard_map/gather_all/pallas_call | solution.py:531
  78.1 0.9 reshape.193.mask_ref
  81.6 13.8 %space_forward.1 = (bf16[4,448,576]{2,1,0:T(8,128)(2,1)}, bf16[4,448,192]{2,1,0:T(8,128)(2,1)}, f32[448,768]{1,0:T(8,128)}, bf16[448,768]{1,0:T(8,128)(2,1)}) custom-call(bf16[448,768]{1,0:T(8,128)(2,1)} %bitcast.98, f32[8,768]{1,0:T(8,128)} %concatenate.21.vec_ref, f32[1,224]{1,0:T(1,128)} %reshape.164.bias_ref, bf16[2,4,768,768]{3,2,1,0:T(8,128)(2,1)} %bitcast.81), custom_call_target="tpu_custom_call" | custom-call | tf_op jit(solution)/shard_map/space_forward/pallas_call | solution.py:292
  95.4 23.3 %rows_to_both.1 = (bf16[2,4,2,56,768]{4,3,2,1,0:T(8,128)(2,1)}, bf16[2,4,56,768]{3,2,1,0:T(8,128)(2,1)}) custom-call(bf16[2,4,56,768]{3,2,1,0:T(8,128)(2,1)} %bitcast.114, bf16[4,2,56,768]{3,2,1,0:T(8,128)(2,1)} %bitcast.101), custom_call_target="tpu_custom_call" | custom-call | tf_op jit(solution)/shard_map/rows_to_both/pallas_call | solution.py:887
  118.7 2.5 copy.78
  121.2 22.4 %time_forward.1 = (bf16[2,896,576]{2,1,0:T(8,128)(2,1)}, bf16[2,896,192]{2,1,0:T(8,128)(2,1)}) custom-call(s32[1]{0:T(128)} %bitcast.core_ref, bf16[896,768]{1,0:T(8,128)(2,1)} %bitcast.88, bf16[2,4,768,768]{3,2,1,0:T(8,128)(2,1)} %bitcast.82, f32[896,1]{1,0:T(8,128)} %reshape.193.mask_ref), custom_call_target="tpu_custom_call" | custom-call | tf_op jit(solution)/shard_map/time_forward/pallas_call | solution.py:292
  143.6 1.2 fusion
  145.1 0.9 copy.82
  146.1 1.3 reshape.173.refs_0_
  147.4 29.7 %ot_to_frames.1 = bf16[2,2,4,56,384]{4,3,2,1,0:T(8,128)(2,1)} custom-call(bf16[2,4,2,56,384]{4,3,2,1,0:T(8,128)(2,1)} %reshape.173.refs_0_), custom_call_target="tpu_custom_call" | custom-call | tf_op jit(solution)/shard_map/ot_to_frames/pallas_call | solution.py:887
  177.1 1.1 all-gather.3.cloned.1.call-done
  178.2 27.7 %mlp_both.1 = (bf16[448,768]{1,0:T(8,128)(2,1)}, f32[448,768]{1,0:T(8,128)}, bf16[2,448,384]{2,1,0:T(8,128)(2,1)}, bf16[4,4,2,192,768]{4,3,2,1,0:T(8,128)(2,1)},...) custom-call(s32[1]{0:T(128)} %bitcast.core_ref, f32[448,768]{1,0:T(8,128)} %get-tuple-element.54.xs_ref, ...), custom_call_target="tpu_custom_call" | custom-call | tf_op jit(solution)/shard_map/mlp_both/pallas_call | solution.py:292
  206.0 19.1 %dot_to_time.1 = (bf16[2,4,2,56,384]{4,3,2,1,0:T(8,128)(2,1)}, bf16[4,2,56,768]{3,2,1,0:T(8,128)(2,1)}) custom-call(bf16[2,2,4,56,384]{4,3,2,1,0:T(8,128)(2,1)} %bitcast.113, bf16[2,4,56,768]{3,2,1,0:T(8,128)(2,1)} %bitcast.112), custom_call_target="tpu_custom_call" | custom-call | tf_op jit(solution)/shard_map/dot_to_time/pallas_call | solution.py:887
  225.1 1.2 copy.103
  226.8 1.1 copy.102
  227.8 35.8 %time_backward.1 = (bf16[4,768,768]{2,1,0:T(8,128)(2,1)}, f32[896,768]{1,0:T(8,128)}) custom-call(s32[1]{0:T(128)} %bitcast.core_ref, bf16[896,768]{1,0:T(8,128)(2,1)} %bitcast.89, bf16[2,4,768,768]{3,2,1,0:T(8,128)(2,1)} %bitcast.84, f32[896,1]{1,0:T(8,128)} %reshape.193.mask_ref, bf16[2,896,576]{2,1,0:T(8,128)(2,1)} %get-tuple-element.64.qkv_ref, ...), custom_call_target="tpu_custom_call" | custom-call | tf_op jit(solution)/shard_map/time_backward/pallas_call | solution.py:292
  263.7 2.0 copy.101
  265.6 0.9 slice.163
  266.6 1.2 slice.136
  267.7 1.1 copy.92
  270.4 18.7 %sum_to_frames.1 = bf16[2,4,56,768]{3,2,1,0:T(8,128)(2,1)} custom-call(f32[4,2,56,768]{3,2,1,0:T(8,128)} %bitcast.93, bf16[4,2,56,768]{3,2,1,0:T(8,128)(2,1)} %bitcast.102), custom_call_target="tpu_custom_call" | custom-call | tf_op jit(solution)/shard_map/sum_to_frames/pallas_call | solution.py:887
  289.1 30.3 %space_backward.1 = (bf16[448,768]{1,0:T(8,128)(2,1)}, bf16[4,768,768]{2,1,0:T(8,128)(2,1)}, f32[8,768]{1,0:T(8,128)}) custom-call(bf16[448,768]{1,0:T(8,128)(2,1)} %bitcast.99, f32[448,768]{1,0:T(8,128)} %get-tuple-element.54.xs_ref, f32[448,768]{1,0:T(8,128)} %get-tuple-element.63.gt_ref, bf16[448,768]{1,0:T(8,128)(2,1)} %bitcast.97, ...), custom_call_target="tpu_custom_call" | custom-call | tf_op jit(solution)/shard_map/space_backward/pallas_call | solution.py:292
  321.3 81.6 %reduce_all.1 = (f32[4,192,768]{2,1,0:T(8,128)}, f32[16,128]{1,0:T(8,128)}, bf16[4,2,56,768]{3,2,1,0:T(8,128)(2,1)}) custom-call(bf16[4,4,192,768]{3,2,1,0:T(8,128)(2,1)} %bitcast.95, bf16[4,4,192,768]{3,2,1,0:T(8,128)(2,1)} %bitcast.94, bf16[2,192,768]{2,1,0:T(8,128)(2,1)} %bitcast.119, f32[2,2,4,16,128]{4,3,2,1,0:T(8,128)} %reshape_reshape.7.refs_3_, ...), custom_call_target="tpu_custom_call" | custom-call | tf_op jit(solution)/shard_map/reduce_all/pallas_call | solution.py:737
  402.9 1.3 slice.148
  404.2 1.5 fusion.1
  405.7 1.4 slice.147
  407.0 2.4 copy_convert_fusion
  409.4 2.8 slice_bitcast_fusion
  (64 shorter events, 17.7 us)
Async XLA Ops:
  7.2 8.4 %copy-start.2 = (bf16[768,192]{0,1:T(8,128)(2,1)S(1)}, bf16[768,192]{0,1:T(8,128)(2,1)}, u32[]{:S(2)}) copy-start(bf16[768,192]{0,1:T(8,128)(2,1)} %param.32) | copy-start | bytes 884740
  7.2 8.4 %copy-start.3 = (bf16[192,768]{1,0:T(8,128)(2,1)S(1)}, bf16[192,768]{1,0:T(8,128)(2,1)}, u32[]{:S(2)}) copy-start(bf16[192,768]{1,0:T(8,128)(2,1)} %param.30) | copy-start | bytes 884740
  7.2 171.0 %all-gather.3.cloned.1.call-start = ((), (), s32[]{:S(2)}) async-start(), calls=%async_computation.2 | async-start | bytes 10027008 | tf_op jit(solution)/shard_map/all_gather | solution.py:948
  15.6 61.5 %copy-start.5 = (s32[196]{0:T(256)S(1)}, s32[196]{0:T(256)}, u32[]{:S(2)}) copy-start(s32[196]{0:T(256)} %param.40) | copy-start | bytes 2356
  16.5 62.6 %copy-start.1 = (bf16[2,4,49,768]{3,1,2,0:T(4,128)(2,1)S(1)}, bf16[2,4,49,768]{3,1,2,0:T(4,128)(2,1)}, u32[]{:S(2)}) copy-start(bf16[2,4,49,768]{3,1,2,0:T(4,128)(2,1)} %param.41) | copy-start | bytes 1806340
  76.1 245.2 %reduce-scatter.2.cloned.1.call-start = ((), (), s32[]{:S(2)}) async-start(), calls=%async_computation.1 | async-start | bytes 10027008 | tf_op jit(solution)/shard_map/reduce_scatter | solution.py:1050
  265.6 2.1 copy-start
  289.1 31.3 %copy-start.4 = (f32[4,768]{1,0:T(4,128)S(1)}, f32[4,768]{1,0:T(4,128)}, u32[]{:S(2)}) copy-start(f32[4,768]{1,0:T(4,128)} %get-tuple-element.75) | copy-start | bytes 36868
Sparse Core Ops, SparseCore 0:
  76.2 101.9 all-gather.2
  206.1 109.2 reduce-scatter.1
